TPU v7x, 8 devices: a whole 2x2x1 slice. The times are simulated.
8 devices in a mesh: dp: 1 (over z), cx: 2 (over y), cy: 2 (over x), cz: 2 (over core).
Axes of the slice: x: 2, y: 2, z: 1, core: 2. Of those that a mesh axis runs over, the one named last changes fastest.
Arguments:
- q: bfloat16 [2048, 64, 128], P(('dp', 'cx', 'cy', 'cz'))
- k: bfloat16 [2048, 8, 128], P(('dp', 'cx', 'cy', 'cz'))
- v: bfloat16 [2048, 8, 128], P(('dp', 'cx', 'cy', 'cz'))
Outputs:
- output: bfloat16 [2048, 64, 128], P(('dp', 'cx', 'cy', 'cz'))
All inputs are finite; a program needn't handle non-finite values.
Results may differ from a plain program's by a relative error of at most 0.00596145.
Values are sent between devices in bfloat16 or wider.
A program may use at most 1 GiB of HBM per device.

v0:
```python
import jax
import jax.numpy as jnp
from jax import lax
from jax.sharding import PartitionSpec as P

NEG = -1e30


def _blocks(t, work):
    c = 1
    while t % (2 * c) == 0 and (work > c << 25 or (c < 8 and work >= c << 22)):
        c *= 2
    return c


def _lead(x, n):
    return jnp.swapaxes(x.reshape((n, -1) + x.shape[1:]), 0, 1).reshape(x.shape)


def _partial(q, k, v, qpos, kpos, lo=0):
    na, t, hq, d = q.shape
    nk, hkvv, _ = k.shape
    g = hq // hkvv
    w = nk // (lo + t)
    n = _blocks(t, hq * na * t * nk)
    c = t // n
    scale = d ** -0.5
    q = q.reshape(na, t, hkvv, g, d)
    outs, lses = [], []
    for j in range(n):
        r0, r1 = j * c, (j + 1) * c
        e = (lo + r1) * w
        s = jnp.einsum('aqhgd,khd->haqgk', q[:, r0:r1], k[:e], preferred_element_type=jnp.float32)
        mask = kpos[:e] <= qpos[:, r0:r1, None]
        s = jnp.where(mask[None, :, :, None, :], s * scale, NEG)
        m = jnp.max(s, axis=-1)
        p = jnp.exp(s - m[..., None])
        l = jnp.transpose(jnp.sum(p, axis=-1), (1, 2, 0, 3))
        m = jnp.transpose(m, (1, 2, 0, 3))
        o = jnp.einsum('haqgk,khd->aqhgd', p.astype(jnp.bfloat16), v[:e], preferred_element_type=jnp.float32)
        ok = m > NEG
        outs.append(o / jnp.where(ok, l, jnp.inf)[..., None])
        lses.append(jnp.where(ok, m + jnp.log(l), NEG))
    o = jnp.concatenate(outs, axis=1) if n > 1 else outs[0]
    lse = jnp.concatenate(lses, axis=1) if n > 1 else lses[0]
    return o.reshape(na, t, hq, d), lse.reshape(na, t, hq)


def solution(mesh):
    a = mesh.shape['cx']
    nz = mesh.shape['cz']
    b = mesh.shape['cy'] * nz
    dev = a * b
    spec = P(('dp', 'cx', 'cy', 'cz'))

    def local(q, k, v):
        t, hq, d = q.shape
        ix = lax.axis_index('cx')
        own = lax.axis_index('cy') * nz + lax.axis_index('cz')
        i = jnp.arange(t, dtype=jnp.int32)
        qpos = i[None, :] * dev + jnp.arange(a, dtype=jnp.int32)[:, None] * b + own
        kpos = (i[:, None] * dev + ix * b + jnp.arange(b, dtype=jnp.int32)[None, :]).reshape(-1)
        qg = lax.all_gather(q, 'cx', axis=0, tiled=True)
        kg = lax.all_gather(k, ('cy', 'cz'), axis=0, tiled=True)
        vg = lax.all_gather(v, ('cy', 'cz'), axis=0, tiled=True)
        o, lse = _partial(qg.reshape(a, t, hq, d), _lead(kg, b), _lead(vg, b), qpos, kpos)
        o = o.reshape(a * t, hq, d)
        lse = lse.reshape(a * t, hq)
        top = lax.pmax(lse, 'cx')
        tot = top + jnp.log(lax.psum(jnp.exp(lse - top), 'cx'))
        o = o * jnp.exp(lse - tot)[..., None]
        return lax.psum_scatter(o, 'cx', scatter_dimension=0, tiled=True).astype(jnp.bfloat16)

    return jax.shard_map(local, mesh=mesh, in_specs=(spec, spec, spec), out_specs=spec, check_vma=False)
```

profile of v0, /device:TPU:0, one launch (start us, length us, event | category | flops | bytes accessed | tf_op | source)
XLA Modules:
  0.0 500.3 jit_solution(17358917068264091882)
XLA Ops:
  13.8 17.4 %all-gather.6.cloned.1.call-done = bf16[1024,8,128]{2,1,0:T(8,128)(2,1)} async-done(((bf16[256,8,128]{2,1,0:T(8,128)(2,1)}), bf16[1024,8,128]{2,1,0:T(8,128)(2,1)}) %all-gather.6.cloned.1.call-update) | async-done | bytes 2097168 | tf_op jit(solution)/shard_map/all_gather | solution.py:64
  31.3 3.2 copy.142
  35.3 1.0 slice.219
  36.3 16.1 %all-gather.8.cloned.1.call-done = bf16[1024,8,128]{2,1,0:T(8,128)(2,1)} async-done(((bf16[256,8,128]{2,1,0:T(8,128)(2,1)}), bf16[1024,8,128]{2,1,0:T(8,128)(2,1)}) %all-gather.8.cloned.1.call-update) | async-done | bytes 2097168 | tf_op jit(solution)/shard_map/all_gather | solution.py:65
  52.4 3.2 copy.143
  56.5 1.0 slice.220
  57.5 1.2 slice.225
  58.7 1.2 slice.224
  59.9 1.4 slice.230
  61.3 1.5 slice.229
  62.7 1.6 slice.235
  64.8 1.8 slice.240
  66.6 1.8 slice.239
  68.3 2.0 slice.245
  70.3 1.9 slice.244
  72.2 84.0 %all-gather.4.cloned.1.call-done = bf16[512,64,128]{2,1,0:T(8,128)(2,1)} async-done(((bf16[256,64,128]{2,1,0:T(8,128)(2,1)}), bf16[512,64,128]{2,1,0:T(8,128)(2,1)}) %all-gather.4.cloned.1.call-update) | async-done | bytes 8388624 | tf_op jit(solution)/shard_map/all_gather | solution.py:63
  156.2 4.9 fusion.140
  162.0 1.4 fusion.75
  165.3 1.8 fusion.40
  168.0 1.6 fusion.24
  169.6 2.1 fusion.31
  172.7 1.8 fusion.15
  174.5 2.8 fusion.19
  178.2 2.6 fusion.9
  180.8 7.5 %fusion.13 = f32[8,2,32,8]{3,2,1,0:T(8,128)S(1)} fusion(f32[8,2,32,8,640]{4,3,2,1,0:T(8,128)S(1)} %get-tuple-element.50, f32[8,2,32,8]{3,2,1,0:T(8,128)S(1)} %get-tuple-element.49, pred[2,32,640]{2,1,0:T(8,128)(4,1)S(1)} %copy-done.44), kind=kLoop, calls=%fused_computation.23 | loop fusion | flops 10481664 | bytes 10559488 | tf_op jit(solution)/shard_map/reduce_sum | solution.py:38
  189.3 2.9 fusion.6
  192.2 7.7 %fusion.7 = f32[8,2,32,8]{3,2,1,0:T(8,128)S(1)} fusion(f32[8,2,32,8,768]{4,3,2,1,0:T(8,128)S(1)} %get-tuple-element.52, f32[8,2,32,8]{3,2,1,0:T(8,128)S(1)} %get-tuple-element.51, pred[2,32,768]{2,1,0:T(8,128)(4,1)S(1)} %broadcast_compare_fusion.2), kind=kLoop, calls=%fused_computation.15 | loop fusion | flops 12578816 | bytes 12664832 | tf_op jit(solution)/shard_map/reduce_sum | solution.py:38
  200.9 3.3 fusion.1
  204.3 4.1 fusion.4
  208.3 1.1 copy-done
  210.4 3.7 fusion
  214.1 4.9 fusion.2
  219.0 1.7 copy-done.1
  221.7 2.2 copy.79
  224.7 1.7 fusion.57
  227.1 2.5 fusion.56
  229.7 2.8 fusion.55
  232.5 5.8 %copy-done.8 = f32[2,256,8,8,128]{4,3,1,0,2:T(8,128)} copy-done((f32[2,256,8,8,128]{4,3,1,0,2:T(8,128)}, f32[2,256,8,8,128]{4,3,1,0,2:T(8,128)S(1)}, u32[]{:S(2)}) %copy-start.8) | copy-done | bytes 16777240
  238.4 4.4 fusion.54
  242.8 7.2 %fusion.53 = f32[2,256,8,8,128]{4,3,1,0,2:T(8,128)} fusion(f32[2,256,8,8,128]{4,3,1,0,2:T(8,128)} %fusion.54, bf16[640,8,128,1,1]{2,0,4,3,1:T(8,128)(2,1)S(1)} %bitcast.310, f32[8,2,32,8,640]{4,3,2,1,0:T(8,128)} %copy-done.5, f32[8,2,32,8]{3,2,1,0:T(8,128)S(1)} %copy-done.25, pred[2,32,640]{2,1,0:T(8,128)(4,1)S(1)} %copy-done.45, ...), kind=kOutput, calls=%fused_computation.65 | convolution fusion | flops 682098688 | bytes 13967360 | tf_op jit(solution)/shard_map/haqgk,khd->aqhgd/dot_general | solution.py:40
  250.1 5.7 %fusion.52 = f32[2,256,8,8,128]{4,3,1,0,2:T(8,128)} fusion(f32[2,256,8,8,128]{4,3,1,0,2:T(8,128)} %fusion.53, bf16[768,8,128,1,1]{2,0,4,3,1:T(8,128)(2,1)S(1)} %bitcast.309, f32[8,2,32,8,768]{4,3,2,1,0:T(8,128)S(1)} %bitcast.283, f32[8,2,32,8]{3,2,1,0:T(8,128)S(1)} %copy-done.19, pred[2,32,768]{2,1,0:T(8,128)(4,1)S(1)} %copy-done.43, ...), kind=kOutput, calls=%fused_computation.63 | convolution fusion | flops 818413568 | bytes 16334848 | tf_op jit(solution)/shard_map/haqgk,khd->aqhgd/dot_general | solution.py:40
  255.9 7.2 %fusion.51 = f32[2,256,8,8,128]{4,3,1,0,2:T(8,128)} fusion(f32[2,256,8,8,128]{4,3,1,0,2:T(8,128)} %fusion.52, bf16[896,8,128,1,1]{2,0,4,3,1:T(8,128)(2,1)} %bitcast.308, f32[8,2,32,8,896]{4,3,2,1,0:T(8,128)S(1)} %bitcast.272, f32[8,2,32,8]{3,2,1,0:T(8,128)} %copy-done.17, pred[2,32,896]{2,1,0:T(8,128)(4,1)} %broadcast_compare_fusion.1, ...), kind=kOutput, calls=%fused_computation.61 | convolution fusion | flops 954728448 | bytes 19193856 | tf_op jit(solution)/shard_map/haqgk,khd->aqhgd/dot_general | solution.py:40
  263.0 1.6 subtract_exponential_fusion.9
  264.7 9.5 %fusion.50 = f32[2,256,8,8,128]{4,3,1,0,2:T(8,128)} fusion(f32[2,256,8,8,128]{4,3,1,0,2:T(8,128)} %fusion.51, bf16[1024,8,128,1,1]{2,0,4,3,1:T(8,128)(2,1)S(1)} %bitcast.291, f32[8,2,32,8,1024]{4,3,2,1,0:T(8,128)} %copy-done.1, f32[8,2,32,8]{3,2,1,0:T(8,128)S(1)} %copy-done.31, pred[2,32,1024]{2,1,0:T(8,128)(4,1)S(1)} %broadcast_compare_fusion, ...), kind=kOutput, calls=%fused_computation.59 | convolution fusion | flops 1091043328 | bytes 21069824 | tf_op jit(solution)/shard_map/haqgk,khd->aqhgd/dot_general | solution.py:40
  274.3 11.9 %copy.78 = f32[2,256,8,8,128]{4,3,2,1,0:T(8,128)} copy(f32[2,256,8,8,128]{4,3,1,0,2:T(8,128)} %fusion.50) | data formatting | bytes 33554432 | tf_op jit(solution)/shard_map/concatenate | solution.py:44
  287.3 12.7 %broadcast_multiply_fusion = f32[512,64,128]{2,1,0:T(8,128)} fusion(f32[512,64,128]{2,1,0:T(8,128)} %bitcast.281, f32[512,64]{1,0:T(8,128)S(1)} %copy.80), kind=kLoop, calls=%fused_computation.18 | loop fusion | flops 4194304 | bytes 33685504 | tf_op jit(solution)/shard_map/mul | solution.py:71
  300.0 186.5 %reduce-scatter.2.cloned.1.call-done = f32[256,64,128]{2,1,0:T(8,128)} async-done(((f32[512,64,128]{2,1,0:T(8,128)}), f32[256,64,128]{2,1,0:T(8,128)}) %reduce-scatter.2.cloned.1.call-update) | async-done | bytes 8388624 | tf_op jit(solution)/shard_map/reduce_scatter | solution.py:72
  486.4 6.5 %convert_element_type.35 = bf16[256,64,128]{2,1,0:T(8,128)(2,1)} convert(f32[256,64,128]{2,1,0:T(8,128)} %reduce-scatter.2.cloned.1.call-done) | non-fusion elementwise | flops 2097152 | bytes 12582912 | tf_op jit(solution)/shard_map/convert_element_type | solution.py:72
  (202 shorter events, 21.3 us)
Async XLA Ops:
  6.5 24.8 %all-gather.6.cloned.1.call-start = ((), (), s32[]{:S(2)}) async-start(), calls=%async_computation.2 | async-start | bytes 2621440 | tf_op jit(solution)/shard_map/all_gather | solution.py:64
  7.3 45.1 %all-gather.8.cloned.1.call-start = ((), (), s32[]{:S(2)}) async-start(), calls=%async_computation.3 | async-start | bytes 2621440 | tf_op jit(solution)/shard_map/all_gather | solution.py:65
  8.0 148.2 %all-gather.4.cloned.1.call-start = ((), (), s32[]{:S(2)}) async-start(), calls=%async_computation.1 | async-start | bytes 12582912 | tf_op jit(solution)/shard_map/all_gather | solution.py:63
  8.7 254.3 %all-reduce.3.cloned.1.call-start = ((), (), s32[]{:S(2)}) async-start(), calls=%async_computation.4 | async-start | bytes 262144 | tf_op jit(solution)/shard_map/pmax | solution.py:69
  13.0 179.2 %copy-start.42 = (pred[2,32,768]{2,1,0:T(8,128)(4,1)}, pred[2,32,768]{2,1,0:T(8,128)(4,1)S(1)}, u32[]{:S(2)}) copy-start(pred[2,32,768]{2,1,0:T(8,128)(4,1)S(1)} %broadcast_compare_fusion.2) | copy-start | bytes 147460
  55.6 12.8 %copy-start.3 = (bf16[4,256,8,128]{3,0,1,2:T(4,128)(2,1)}, bf16[4,256,8,128]{3,0,1,2:T(4,128)(2,1)S(1)}, u32[]{:S(2)}) copy-start(bf16[4,256,8,128]{3,0,1,2:T(4,128)(2,1)S(1)} %copy.143) | copy-start | bytes 6291460
  162.0 5.1 %copy-start.20 = (f32[8,2,32,8]{3,2,1,0:T(8,128)}, f32[8,2,32,8]{3,2,1,0:T(8,128)S(1)}, u32[]{:S(2)}) copy-start(f32[8,2,32,8]{3,2,1,0:T(8,128)S(1)} %get-tuple-element.41) | copy-start | bytes 49156
  174.5 6.3 %copy-start.28 = (f32[8,2,32,8]{3,2,1,0:T(8,128)}, f32[8,2,32,8]{3,2,1,0:T(8,128)S(1)}, u32[]{:S(2)}) copy-start(f32[8,2,32,8]{3,2,1,0:T(8,128)S(1)} %get-tuple-element.47) | copy-start | bytes 49156
  180.8 8.5 %copy-start.5 = (f32[8,2,32,8,640]{4,3,2,1,0:T(8,128)}, f32[8,2,32,8,640]{4,3,2,1,0:T(8,128)S(1)}, u32[]{:S(2)}) copy-start(f32[8,2,32,8,640]{4,3,2,1,0:T(8,128)S(1)} %get-tuple-element.50) | copy-start | bytes 31457284
  180.8 8.4 %copy-start.24 = (f32[8,2,32,8]{3,2,1,0:T(8,128)}, f32[8,2,32,8]{3,2,1,0:T(8,128)S(1)}, u32[]{:S(2)}) copy-start(f32[8,2,32,8]{3,2,1,0:T(8,128)S(1)} %get-tuple-element.49) | copy-start | bytes 49156
  180.8 8.4 %copy-start.14 = (bf16[192,4,8,128]{3,1,0,2:T(4,128)(2,1)S(1)}, bf16[192,4,8,128]{3,1,0,2:T(4,128)(2,1)}, u32[]{:S(2)}) copy-start(bf16[192,4,8,128]{3,1,0,2:T(4,128)(2,1)} %slice.239) | copy-start | bytes 4718596
  192.2 7.8 %copy-start.2 = (f32[8,2,32,8,768]{4,3,2,1,0:T(8,128)}, f32[8,2,32,8,768]{4,3,2,1,0:T(8,128)S(1)}, u32[]{:S(2)}) copy-start(f32[8,2,32,8,768]{4,3,2,1,0:T(8,128)S(1)} %get-tuple-element.52) | copy-start | bytes 37748740
  192.2 7.8 %copy-start.18 = (f32[8,2,32,8]{3,2,1,0:T(8,128)}, f32[8,2,32,8]{3,2,1,0:T(8,128)S(1)}, u32[]{:S(2)}) copy-start(f32[8,2,32,8]{3,2,1,0:T(8,128)S(1)} %get-tuple-element.51) | copy-start | bytes 49156
  192.2 8.7 %copy-start.11 = (bf16[224,4,8,128]{3,1,0,2:T(4,128)(2,1)S(1)}, bf16[224,4,8,128]{3,1,0,2:T(4,128)(2,1)}, u32[]{:S(2)}) copy-start(bf16[224,4,8,128]{3,1,0,2:T(4,128)(2,1)} %slice.244) | copy-start | bytes 5505028
  192.2 8.7 %copy-start.38 = (pred[2,32,896]{2,1,0:T(8,128)(4,1)S(1)}, pred[2,32,896]{2,1,0:T(8,128)(4,1)}, u32[]{:S(2)}) copy-start(pred[2,32,896]{2,1,0:T(8,128)(4,1)} %broadcast_compare_fusion.1) | copy-start | bytes 172036
  204.2 5.2 %copy-start = (f32[8,2,32,8,896]{4,3,2,1,0:T(8,128)}, f32[8,2,32,8,896]{4,3,2,1,0:T(8,128)S(1)}, u32[]{:S(2)}) copy-start(f32[8,2,32,8,896]{4,3,2,1,0:T(8,128)S(1)} %get-tuple-element.54) | copy-start | bytes 44040196
  204.2 5.2 %copy-start.17 = (f32[8,2,32,8]{3,2,1,0:T(8,128)}, f32[8,2,32,8]{3,2,1,0:T(8,128)S(1)}, u32[]{:S(2)}) copy-start(f32[8,2,32,8]{3,2,1,0:T(8,128)S(1)} %get-tuple-element.53) | copy-start | bytes 49156
  214.1 6.6 %copy-start.1 = (f32[8,2,32,8,1024]{4,3,2,1,0:T(8,128)}, f32[8,2,32,8,1024]{4,3,2,1,0:T(8,128)S(1)}, u32[]{:S(2)}) copy-start(f32[8,2,32,8,1024]{4,3,2,1,0:T(8,128)S(1)} %get-tuple-element.56) | copy-start | bytes 50331652
  214.1 6.7 %copy-start.30 = (f32[8,2,32,8]{3,2,1,0:T(8,128)}, f32[8,2,32,8]{3,2,1,0:T(8,128)S(1)}, u32[]{:S(2)}) copy-start(f32[8,2,32,8]{3,2,1,0:T(8,128)S(1)} %get-tuple-element.55) | copy-start | bytes 49156
  214.1 10.5 %copy-start.13 = (f32[8,2,32,8,128]{4,3,2,1,0:T(8,128)S(1)}, f32[8,2,32,8,128]{4,3,2,1,0:T(8,128)}, u32[]{:S(2)}) copy-start(f32[8,2,32,8,128]{4,3,2,1,0:T(8,128)} %copy-done.12) | copy-start | bytes 6291460
  214.1 10.5 %copy-start.21 = (f32[8,2,32,8]{3,2,1,0:T(8,128)S(1)}, f32[8,2,32,8]{3,2,1,0:T(8,128)}, u32[]{:S(2)}) copy-start(f32[8,2,32,8]{3,2,1,0:T(8,128)} %copy-done.20) | copy-start | bytes 49156
  214.1 10.5 %copy-start.46 = (bf16[32,4,8,128]{3,1,0,2:T(4,128)(2,1)S(1)}, bf16[32,4,8,128]{3,1,0,2:T(4,128)(2,1)}, u32[]{:S(2)}) copy-start(bf16[32,4,8,128]{3,1,0,2:T(4,128)(2,1)} %slice.215) | copy-start | bytes 786436
  214.1 10.5 %copy-start.47 = (f32[2,32,8,8]{3,1,0,2:T(8,128)S(1)}, f32[2,32,8,8]{3,1,0,2:T(8,128)}, u32[]{:S(2)}) copy-start(f32[2,32,8,8]{3,1,0,2:T(8,128)} %get-tuple-element.32) | copy-start | bytes 49156
  214.1 10.5 %copy-start.59 = (pred[2,32,128]{2,1,0:T(8,128)(4,1)S(1)}, pred[2,32,128]{2,1,0:T(8,128)(4,1)}, u32[]{:S(2)}) copy-start(pred[2,32,128]{2,1,0:T(8,128)(4,1)} %broadcast_compare_fusion.7) | copy-start | bytes 24580
  224.5 61.7 %all-reduce.5.cloned.1.call-start = ((), (), s32[]{:S(2)}) async-start(), calls=%async_computation.5 | async-start | bytes 262144 | tf_op jit(solution)/shard_map/psum | solution.py:70
  227.1 11.2 %slice-start.7 = ((s8[8388608]{0:T(1024)(128)(4,1)}), s8[4194304]{0:T(1024)(128)(4,1)S(1)}, s32[]{:S(2)}) async-start(s8[8388608]{0:T(1024)(128)(4,1)} %bitcast.292), calls=%async_computation.14 | async-start | bytes 8388608
  229.7 8.6 %slice-start.8 = ((s8[8388608]{0:T(1024)(128)(4,1)}), s8[4194304]{0:T(1024)(128)(4,1)S(1)}, s32[]{:S(2)}) async-start(s8[8388608]{0:T(1024)(128)(4,1)} %bitcast.292), calls=%async_computation.15 | async-start | bytes 8388608
  229.7 8.6 %copy-start.29 = (f32[8,2,32,8]{3,2,1,0:T(8,128)S(1)}, f32[8,2,32,8]{3,2,1,0:T(8,128)}, u32[]{:S(2)}) copy-start(f32[8,2,32,8]{3,2,1,0:T(8,128)} %copy-done.28) | copy-start | bytes 49156
  229.7 8.6 %copy-start.37 = (bf16[128,4,8,128]{3,1,0,2:T(4,128)(2,1)S(1)}, bf16[128,4,8,128]{3,1,0,2:T(4,128)(2,1)}, u32[]{:S(2)}) copy-start(bf16[128,4,8,128]{3,1,0,2:T(4,128)(2,1)} %slice.230) | copy-start | bytes 3145732
  229.7 8.6 %copy-start.50 = (f32[2,32,8,8]{3,1,0,2:T(8,128)S(1)}, f32[2,32,8,8]{3,1,0,2:T(8,128)}, u32[]{:S(2)}) copy-start(f32[2,32,8,8]{3,1,0,2:T(8,128)} %get-tuple-element.26) | copy-start | bytes 49156
  232.5 5.8 %copy-start.8 = (f32[2,256,8,8,128]{4,3,1,0,2:T(8,128)}, f32[2,256,8,8,128]{4,3,1,0,2:T(8,128)S(1)}, u32[]{:S(2)}) copy-start(f32[2,256,8,8,128]{4,3,1,0,2:T(8,128)S(1)} %fusion.55) | copy-start | bytes 50331652
  238.3 11.7 %slice-start.4 = ((s8[12582912]{0:T(1024)(128)(4,1)}), s8[4194304]{0:T(1024)(128)(4,1)S(1)}, s32[]{:S(2)}) async-start(s8[12582912]{0:T(1024)(128)(4,1)} %bitcast.282), calls=%async_computation.11 | async-start | bytes 8388608
  238.4 11.7 %slice-start.5 = ((s8[12582912]{0:T(1024)(128)(4,1)}), s8[4194304]{0:T(1024)(128)(4,1)S(1)}, s32[]{:S(2)}) async-start(s8[12582912]{0:T(1024)(128)(4,1)} %bitcast.282), calls=%async_computation.12 | async-start | bytes 8388608
  242.7 7.3 %slice-start.6 = ((s8[12582912]{0:T(1024)(128)(4,1)}), s8[4194304]{0:T(1024)(128)(4,1)S(1)}, s32[]{:S(2)}) async-start(s8[12582912]{0:T(1024)(128)(4,1)} %bitcast.282), calls=%async_computation.13 | async-start | bytes 8388608
  242.7 7.3 %copy-start.19 = (f32[8,2,32,8]{3,2,1,0:T(8,128)S(1)}, f32[8,2,32,8]{3,2,1,0:T(8,128)}, u32[]{:S(2)}) copy-start(f32[8,2,32,8]{3,2,1,0:T(8,128)} %copy-done.18) | copy-start | bytes 49156
  242.8 7.3 %copy-start.34 = (bf16[192,4,8,128]{3,1,0,2:T(4,128)(2,1)S(1)}, bf16[192,4,8,128]{3,1,0,2:T(4,128)(2,1)}, u32[]{:S(2)}) copy-start(bf16[192,4,8,128]{3,1,0,2:T(4,128)(2,1)} %slice.240) | copy-start | bytes 4718596
  242.8 7.3 %copy-start.43 = (pred[2,32,768]{2,1,0:T(8,128)(4,1)S(1)}, pred[2,32,768]{2,1,0:T(8,128)(4,1)}, u32[]{:S(2)}) copy-start(pred[2,32,768]{2,1,0:T(8,128)(4,1)} %copy-done.42) | copy-start | bytes 147460
  242.8 7.3 %copy-start.53 = (f32[2,32,8,8]{3,1,0,2:T(8,128)S(1)}, f32[2,32,8,8]{3,1,0,2:T(8,128)}, u32[]{:S(2)}) copy-start(f32[2,32,8,8]{3,1,0,2:T(8,128)} %get-tuple-element.22) | copy-start | bytes 49156
  242.8 13.0 %slice-start = ((s8[14680064]{0:T(1024)(128)(4,1)}), s8[4194304]{0:T(1024)(128)(4,1)S(1)}, s32[]{:S(2)}) async-start(s8[14680064]{0:T(1024)(128)(4,1)} %bitcast.271), calls=%async_computation.7 | async-start | bytes 8388608
  242.8 13.0 %slice-start.1 = ((s8[14680064]{0:T(1024)(128)(4,1)}), s8[4194304]{0:T(1024)(128)(4,1)S(1)}, s32[]{:S(2)}) async-start(s8[14680064]{0:T(1024)(128)(4,1)} %bitcast.271), calls=%async_computation.8 | async-start | bytes 8388608
  250.1 5.7 %slice-start.2 = ((s8[14680064]{0:T(1024)(128)(4,1)}), s8[4194304]{0:T(1024)(128)(4,1)S(1)}, s32[]{:S(2)}) async-start(s8[14680064]{0:T(1024)(128)(4,1)} %bitcast.271), calls=%async_computation.9 | async-start | bytes 8388608
  250.1 5.7 %slice-start.3 = ((s8[14680064]{0:T(1024)(128)(4,1)}), s8[2097152]{0:T(1024)(128)(4,1)S(1)}, s32[]{:S(2)}) async-start(s8[14680064]{0:T(1024)(128)(4,1)} %bitcast.271), calls=%async_computation.10 | async-start | bytes 4194304
  255.8 7.2 %copy-start.33 = (f32[8,8,2,256]{3,1,2,0:T(8,128)S(1)}, f32[8,8,2,256]{3,1,2,0:T(8,128)}, u32[]{:S(2)}) copy-start(f32[8,8,2,256]{3,1,2,0:T(8,128)} %copy.105) | copy-start | bytes 393220
  255.8 8.9 %copy-start.4 = (bf16[4,256,8,128]{3,0,1,2:T(4,128)(2,1)S(1)}, bf16[4,256,8,128]{3,0,1,2:T(4,128)(2,1)}, u32[]{:S(2)}) copy-start(bf16[4,256,8,128]{3,0,1,2:T(4,128)(2,1)} %copy-done.3) | copy-start | bytes 6291460
  255.9 8.9 %copy-start.31 = (f32[8,2,32,8]{3,2,1,0:T(8,128)S(1)}, f32[8,2,32,8]{3,2,1,0:T(8,128)}, u32[]{:S(2)}) copy-start(f32[8,2,32,8]{3,2,1,0:T(8,128)} %copy-done.30) | copy-start | bytes 49156
  255.9 8.9 %copy-start.51 = (f32[2,32,8,8]{3,1,0,2:T(8,128)S(1)}, f32[2,32,8,8]{3,1,0,2:T(8,128)}, u32[]{:S(2)}) copy-start(f32[2,32,8,8]{3,1,0,2:T(8,128)} %get-tuple-element.18) | copy-start | bytes 49156
  264.6 221.8 %reduce-scatter.2.cloned.1.call-start = ((), (), s32[]{:S(2)}) async-start(), calls=%async_computation.6 | async-start | bytes 25165824 | tf_op jit(solution)/shard_map/reduce_scatter | solution.py:72
  274.3 11.9 %copy-start.41 = (f32[512,64]{0,1:T(8,128)S(1)}, f32[512,64]{0,1:T(8,128)}, u32[]{:S(2)}) copy-start(f32[512,64]{0,1:T(8,128)} %all-reduce.3.cloned.1.call-done) | copy-start | bytes 393220
  (29 other events, 101.6 us)
Sparse Core Ops, SparseCore 0:
  8.9 22.3 all-gather.5
  32.8 19.5 all-gather.7
  53.9 102.2 all-gather.3
  224.7 15.8 all-reduce.2
  264.8 15.7 all-reduce.4
  300.1 186.2 reduce-scatter.1
where the time goes:
time: 508 us; the launch traced here: 500 us
  waiting for transfers between devices  306 us (60%)
  other arithmetic  65.1 us (13%)
  matrix products  58.6 us (12%)
  local copies, waits for them, and re-layouts  55.2 us (11%)
  between operations  15.1 us (3%)
    reduce_scatter x1, waiting for transfers between devices, local(): lax.psum_scatter(o, 'cx', scatter_dimension=0, tiled=True)  186 us
    all_gather x1, waiting for transfers between devices, local(): qg = lax.all_gather(q, 'cx', axis=0, tiled=True)  84 us
    dot_general x8, matrix products, _partial(): jnp.einsum('haqgk,khd->aqhgd', p.astype(jnp.bfloat16), v[:e], preferred_e...  40.9 us
    reduce_sum x8, other arithmetic, _partial(): l = jnp.transpose(jnp.sum(p, axis=-1), (1, 2, 0, 3))  32.2 us
    dot_general x8, matrix products, _partial(): jnp.einsum('aqhgd,khd->haqgk', q[:, r0:r1], k[:e], preferred_element_type...  17.7 us
    all_gather x1, waiting for transfers between devices, local(): kg = lax.all_gather(k, ('cy', 'cz'), axis=0, tiled=True)  17.4 us
    all_gather x1, waiting for transfers between devices, local(): vg = lax.all_gather(v, ('cy', 'cz'), axis=0, tiled=True)  16.1 us
    mul x1, other arithmetic, local(): o = o * jnp.exp(lse - tot)[..., None]  12.7 us
  transfers between devices with their start and end apart: 6, of which 4 were waited for; matrix products, arithmetic and copies ran while one was open for 17% of the time, Pallas kernels for 0%

commit v1 on v0

v1 whole, which is shorter than its diff:
```python
import functools
import jax
import jax.numpy as jnp
from jax import lax
from jax.experimental import pallas as pl
from jax.experimental.pallas import tpu as pltpu
from jax.sharding import PartitionSpec as P

T = 256
HQ = 64
HKV = 8
G = 8
D = 128
DEV = 8
NB = 8
SUB = T // NB
KB = DEV * SUB
C = (D ** -0.5) * 1.4426950408889634
NT = (((1,), (1,)), ((), ()))
AXES = ("cx", "cy", "cz")


def attn(q_ref, k_ref, v_ref, o_ref, bias, vt):
    me = (lax.axis_index("cx") * 2 + lax.axis_index("cy")) * 2 + lax.axis_index("cz")

    @pl.when(pl.program_id(0) == 0)
    def _():
        kk = lax.broadcasted_iota(jnp.int32, (KB, KB), 0)
        qq = lax.broadcasted_iota(jnp.int32, (KB, KB), 1)
        kpos = (kk % SUB) * DEV + kk // SUB
        qpos = (qq // G) * DEV + me
        bias[...] = jnp.where(kpos <= qpos, 0.0, -1e30)

    vt[...] = v_ref[0].T
    for j in range(NB):
        n = (j + 1) * KB
        q = q_ref[j * SUB:(j + 1) * SUB].reshape(KB, D)
        s = lax.dot_general(k_ref[0, :n], q, NT, preferred_element_type=jnp.float32)
        d = s[n - KB:] + bias[...]
        s = jnp.concatenate([s[:n - KB], d], axis=0) if j else d
        m = jnp.max(s, axis=0, keepdims=True)
        p = jnp.exp2((s - m) * C)
        l = jnp.sum(p, axis=0, keepdims=True)
        o = jnp.dot(vt[:, :n], p.astype(jnp.bfloat16), preferred_element_type=jnp.float32)
        o = (o * (1.0 / l)).T
        o_ref[j * SUB:(j + 1) * SUB] = o.astype(jnp.bfloat16).reshape(SUB, G, D)


def solution(mesh):
    spec = P(("dp", "cx", "cy", "cz"))

    def order(x):
        x = lax.all_gather(x, AXES, axis=0, tiled=True)
        x = x.reshape(DEV, NB, SUB, HKV, D)
        return jnp.transpose(x, (3, 1, 0, 2, 4)).reshape(HKV, DEV * T, D)

    def local(q, k, v):
        qo = pl.BlockSpec((T, G, D), lambda h: (0, h, 0))
        kv = pl.BlockSpec((1, DEV * T, D), lambda h: (h, 0, 0))
        return pl.pallas_call(
            attn,
            grid=(HKV,),
            out_shape=jax.ShapeDtypeStruct(q.shape, q.dtype),
            in_specs=[qo, kv, kv],
            out_specs=qo,
            scratch_shapes=[pltpu.VMEM((KB, KB), jnp.float32), pltpu.VMEM((D, DEV * T), jnp.bfloat16)],
            compiler_params=pltpu.CompilerParams(vmem_limit_bytes=60 << 20),
        )(q, order(k), order(v))

    return jax.shard_map(local, mesh=mesh, in_specs=(spec, spec, spec), out_specs=spec, check_vma=False)
```

time: 508 us -> 137 us (0.27); the launches traced: 500 us -> 137 us
  waiting for transfers between devices: 306 us -> 63.5 us
  other arithmetic: 65.1 us -> 0 us
  matrix products: 58.6 us -> 0 us
  Pallas kernels: 0 us -> 49.8 us
  local copies, waits for them, and re-layouts: 55.2 us -> 10.4 us
    reduce_scatter x1 -> x0, waiting for transfers between devices: 186 us -> none  [local(): lax.psum_scatter(o, 'cx', scatter_dimension=0, tiled=True)]
    dot_general x16 -> x0, matrix products: 58.6 us -> none  [the longest x8 40.9 us: _partial(): jnp.einsum('haqgk,khd->aqhgd', p.astype(jnp.bfloat16), v[:e], preferred_e...]
    all_gather x3 -> x2, waiting for transfers between devices: 117 us -> 62.1 us  [order(): x = lax.all_gather(x, AXES, axis=0, tiled=True)]
    pallas_call x0 -> x1, Pallas kernels: none -> 49.8 us  [local(): pl.pallas_call(attn, grid=(HKV,), out_shape=jax.ShapeDtypeStruct(q.shape,...]
    reduce_sum x8 -> x0, other arithmetic: 32.2 us -> none  [_partial(): l = jnp.transpose(jnp.sum(p, axis=-1), (1, 2, 0, 3))]
    slice x23 -> x0, local copies, waits for them, and re-layouts: 23.4 us -> none  [the longest x7 9.8 us: _partial(): v[:e]]
    concatenate x2 -> x0, local copies, waits for them, and re-layouts: 14.1 us -> none  [the longest x1 11.9 us: _partial(): o = jnp.concatenate(outs, axis=1) if n > 1 else outs[0]]
    mul x3 -> x0, other arithmetic: 12.7 us -> none  [the longest x1 12.7 us: local(): o = o * jnp.exp(lse - tot)[..., None]]
  transfers between devices with their start and end apart: 6 -> 2, of which waited for: 4 -> 2; matrix products, arithmetic and copies ran while one was open for 17% -> 4% of each run, Pallas kernels for 0% -> 0%
where the time goes in v1:
time: 137 us
  waiting for transfers between devices  63.5 us (46%)
  Pallas kernels  49.8 us (36%)
  between operations  13.4 us (10%)
  local copies, waits for them, and re-layouts  10.4 us (8%)
    all_gather x2, waiting for transfers between devices, order(): x = lax.all_gather(x, AXES, axis=0, tiled=True)  62.1 us
    pallas_call x1, Pallas kernels, local(): pl.pallas_call(attn, grid=(HKV,), out_shape=jax.ShapeDtypeStruct(q.shape,...  49.8 us
    reshape x2, local copies, waits for them, and re-layouts, order(): x = x.reshape(DEV, NB, SUB, HKV, D)  10.4 us
  transfers between devices with their start and end apart: 2, of which 2 were waited for; matrix products, arithmetic and copies ran while one was open for 4% of the time, Pallas kernels for 0%

profile of v1, /device:TPU:0, one launch (start us, length us, event | category | flops | bytes accessed | tf_op | source)
XLA Modules:
  0.0 137.2 jit_solution(2579470297094465056)
XLA Ops:
  6.5 0.0 all-gather.3.cloned.1.call-start
  6.5 0.7 all-gather.3.cloned.1.call-update
  7.3 0.0 all-gather.5.cloned.1.call-start
  7.3 0.7 all-gather.5.cloned.1.call-update
  8.0 34.7 %all-gather.3.cloned.1.call-done = bf16[2048,8,128]{2,1,0:T(8,128)(2,1)} async-done(((bf16[256,8,128]{2,1,0:T(8,128)(2,1)}), bf16[2048,8,128]{2,1,0:T(8,128)(2,1)}) %all-gather.3.cloned.1.call-update) | async-done | bytes 4194320 | tf_op jit(solution)/shard_map/all_gather | solution.py:53
  42.8 5.2 %copy.6 = bf16[8,8,32,8,128]{4,2,0,1,3:T(8,128)(2,1)} copy(bf16[8,8,32,8,128]{4,3,2,1,0:T(8,128)(2,1)} %bitcast.10) | data formatting | bytes 8388608 | tf_op jit(solution)/shard_map/reshape | solution.py:54
  48.0 27.4 %all-gather.5.cloned.1.call-done = bf16[2048,8,128]{2,1,0:T(8,128)(2,1)} async-done(((bf16[256,8,128]{2,1,0:T(8,128)(2,1)}), bf16[2048,8,128]{2,1,0:T(8,128)(2,1)}) %all-gather.5.cloned.1.call-update) | async-done | bytes 4194320 | tf_op jit(solution)/shard_map/all_gather | solution.py:53
  75.3 5.2 %copy.7 = bf16[8,8,32,8,128]{4,2,0,1,3:T(8,128)(2,1)} copy(bf16[8,8,32,8,128]{4,3,2,1,0:T(8,128)(2,1)} %bitcast.11) | data formatting | bytes 8388608 | tf_op jit(solution)/shard_map/reshape | solution.py:54
  80.5 49.8 %shard_map.37 = bf16[256,64,128]{2,1,0:T(8,128)(2,1)} custom-call(bf16[256,64,128]{2,1,0:T(8,128)(2,1)} %q_ref.1, bf16[8,2048,128]{2,1,0:T(8,128)(2,1)} %bitcast.8, bf16[8,2048,128]{2,1,0:T(8,128)(2,1)} %bitcast.9), custom_call_target="tpu_custom_call" | custom-call | tf_op jit(solution)/shard_map/pallas_call | solution.py:60
Async XLA Ops:
  6.5 36.2 %all-gather.3.cloned.1.call-start = ((), (), s32[]{:S(2)}) async-start(), calls=%async_computation | async-start | bytes 4718592 | tf_op jit(solution)/shard_map/all_gather | solution.py:53
  7.3 68.1 %all-gather.5.cloned.1.call-start = ((), (), s32[]{:S(2)}) async-start(), calls=%async_computation.1 | async-start | bytes 4718592 | tf_op jit(solution)/shard_map/all_gather | solution.py:53
Sparse Core Ops, SparseCore 0:
  9.1 33.5 all-gather.2
  44.6 30.7 all-gather.4

commit v2 on v1

v2 whole, which is shorter than its diff:
```python
import jax
import jax.numpy as jnp
from jax import lax
from jax.experimental import pallas as pl
from jax.experimental.pallas import tpu as pltpu
from jax.sharding import PartitionSpec as P

T = 256
HKV = 8
G = 8
D = 128
NB = 8
SUB = T // NB
QB = SUB * G
S1 = 6
S2 = 2
C = (D ** -0.5) * 1.4426950408889634
NT = (((1,), (1,)), ((), ()))
ORDER = (0, 2, 4, 6, 7, 5, 3, 1)
BF = jnp.bfloat16
F32 = jnp.float32


def chunks(n):
    return [(r, min(r + 256, n)) for r in range(0, n, 256)]


def fold(f, x):
    return f(x.reshape(-1, 8, x.shape[-1]), axis=0)


def blocks(nslot, q_of, k_of, vt, bias, sref, begin, finish):
    rows = nslot * SUB
    st = {}

    def scores(j, c):
        r0, r1 = c
        parts = [k_of(*divmod(u, nslot)) for u in range(r0 // SUB, r1 // SUB)]
        s = lax.dot_general(jnp.concatenate(parts, axis=0), q_of(j), NT, preferred_element_type=F32)
        lo = max(r0, j * rows)
        if lo < r1:
            d = s[lo - r0:] + bias[lo - j * rows:r1 - j * rows]
            s = d if lo == r0 else jnp.concatenate([s[:lo - r0], d], axis=0)
        sref[ORDER.index(j) % 2, r0:r1] = s
        m = fold(jnp.max, s)
        st[j] = jnp.maximum(st[j], m) if j in st else m

    def values(j, c, m, acc):
        r0, r1 = c
        p = jnp.exp2((sref[ORDER.index(j) % 2, r0:r1] - m) * C)
        l = fold(jnp.sum, p)
        o = jnp.dot(vt[:, r0:r1], p.astype(BF), preferred_element_type=F32)
        return (acc[0] + l, acc[1] + o) if acc else (l, o)

    for c in chunks((ORDER[0] + 1) * rows):
        scores(ORDER[0], c)
    for i, j in enumerate(ORDER):
        m, a = begin(j, jnp.max(st[j], axis=0, keepdims=True))
        acc = None
        mine = chunks((j + 1) * rows)
        later = chunks((ORDER[i + 1] + 1) * rows) if i + 1 < NB else []
        done = 0
        for t, c in enumerate(mine):
            upto = len(later) * (t + 1) // len(mine)
            for u in range(done, upto):
                scores(ORDER[i + 1], later[u])
            done = upto
            acc = values(j, c, m, acc)
        finish(j, m, a, jnp.sum(acc[0], axis=0, keepdims=True), acc[1])


def kernel(q_hbm, k_hbm, v_hbm, o_hbm, qb, ob, raw, wide, kv1, kv2, vt, sref, bias1, bias2, oacc, ml,
           lsem, qsem, osem, ssem, rsem):
    cx, cy, cz = lax.axis_index("cx"), lax.axis_index("cy"), lax.axis_index("cz")
    me = (cx * 2 + cy) * 2 + cz
    nx = {"cy": 1 - cy}
    ny = {"cx": 1 - cx}
    sib = {"cz": 1 - cz}

    barrier = pltpu.get_barrier_semaphore()
    for dev in (nx, ny, sib):
        pl.semaphore_signal(barrier, inc=1, device_id=dev, device_id_type=pl.DeviceIdType.MESH)

    loads = [pltpu.make_async_copy(x, raw.at[i], lsem.at[i]) for i, x in enumerate((k_hbm, v_hbm))]
    for x in loads:
        x.start()

    def qload(h):
        return pltpu.make_async_copy(q_hbm.at[:, pl.ds(pl.multiple_of(h * G, G), G), :], qb.at[h], qsem.at[h])

    def ostore(h):
        return pltpu.make_async_copy(ob.at[h], o_hbm.at[:, pl.ds(pl.multiple_of(h * G, G), G), :], osem.at[h])

    @pl.loop(0, HKV)
    def _(h):
        qload(h).start()

    def rdma(kind, h):
        src, dst, dev = (
            (kv1.at[h, :, :, 0], kv1.at[h, :, :, 2], nx),
            (kv1.at[h, :, :, 0], kv1.at[h, :, :, 4], ny),
            (kv1.at[h, :, :, 0], kv1.at[h, :, :, 1], sib),
            (kv1.at[h, :, :, 2], kv1.at[h, :, :, 3], sib),
            (kv1.at[h, :, :, 4], kv1.at[h, :, :, 5], sib),
            (kv1.at[h, 0, :, 2], kv2.at[h, 0, :, 0], ny),
            (kv1.at[h, 1, :, 4], kv2.at[h, 1, :, 0], nx),
            (kv2.at[h, :, :, 0], kv2.at[h, :, :, 1], sib),
        )[kind]
        return pltpu.make_async_remote_copy(src, dst, ssem.at[kind, h], rsem.at[kind, h], dev,
                                            pl.DeviceIdType.MESH)

    def mask(nslot, base, ref):
        r = lax.broadcasted_iota(jnp.int32, (nslot * SUB, QB), 0)
        c = lax.broadcasted_iota(jnp.int32, (nslot * SUB, QB), 1)
        kpos = (r % SUB) * 8 + (me ^ (r // SUB + base))
        qpos = (c // G) * 8 + me
        ref[...] = jnp.where(kpos <= qpos, 0.0, -1e30)

    for i in range(2):
        loads[i].wait()
        wide[...] = raw[i].astype(F32).reshape(T * HKV, D)
        for h in range(HKV):
            kv1[h, i, :, 0] = wide[pl.ds(h, T, stride=HKV), :].astype(BF).reshape(NB, SUB, D)
    pl.semaphore_wait(barrier, 3)

    @pl.loop(0, HKV)
    def _(h):
        for kind in range(3):
            rdma(kind, h).start()

    mask(S1, 0, bias1)
    mask(S2, S1, bias2)

    def pass_on(h):
        rdma(0, h).wait_recv()
        rdma(1, h).wait_recv()
        for kind in (3, 4, 5, 6):
            rdma(kind, h).start()

    def pass_on2(h):
        rdma(5, h).wait_recv()
        rdma(6, h).wait_recv()
        rdma(7, h).start()

    pass_on(0)

    @pl.loop(0, HKV)
    def _(h):
        @pl.when(h < HKV - 1)
        def _():
            pass_on(h + 1)

        qload(h).wait()
        for kind in (2, 3, 4):
            rdma(kind, h).wait_recv()
        vt[...] = kv1[h, 1].reshape(S1 * T, D).T

        def finish(j, m, a, l, o):
            oacc[h, j] = o
            ml[h, j, 0:1] = m
            ml[h, j, 1:2] = l

        blocks(S1, lambda j: qb[h, j * SUB:(j + 1) * SUB].reshape(QB, D), lambda t, s: kv1[h, 0, t, s],
               vt, bias1, sref, lambda j, m: (m, None), finish)

    pass_on2(0)

    @pl.loop(0, HKV)
    def _(h):
        @pl.when(h < HKV - 1)
        def _():
            pass_on2(h + 1)

        rdma(7, h).wait_recv()
        vt[:, :S2 * T] = kv2[h, 1].reshape(S2 * T, D).T

        def begin(j, m):
            m1 = ml[h, j, 0:1]
            m = jnp.maximum(m, m1)
            return m, jnp.exp2((m1 - m) * C)

        def finish(j, m, a, l, o):
            l = ml[h, j, 1:2] * a + l
            r = 1.0 / l
            o = oacc[h, j] * (a * r) + o * r
            ob[h, j * SUB:(j + 1) * SUB] = o.T.astype(BF).reshape(SUB, G, D)

        blocks(S2, lambda j: qb[h, j * SUB:(j + 1) * SUB].reshape(QB, D), lambda t, s: kv2[h, 0, t, s],
               vt, bias2, sref, begin, finish)
        ostore(h).start()

    @pl.loop(0, HKV)
    def _(h):
        for kind in range(8):
            rdma(kind, h).wait_send()
        ostore(h).wait()


def solution(mesh):
    spec = P(("dp", "cx", "cy", "cz"))

    def local(q, k, v):
        hbm = pl.BlockSpec(memory_space=pl.ANY)
        return pl.pallas_call(
            kernel,
            out_shape=jax.ShapeDtypeStruct(q.shape, q.dtype),
            in_specs=[hbm] * 3,
            out_specs=hbm,
            scratch_shapes=[
                pltpu.VMEM((HKV, T, G, D), BF),
                pltpu.VMEM((HKV, T, G, D), BF),
                pltpu.VMEM((2, T, HKV, D), BF),
                pltpu.VMEM((T * HKV, D), F32),
                pltpu.VMEM((HKV, 2, NB, S1, SUB, D), BF),
                pltpu.VMEM((HKV, 2, NB, S2, SUB, D), BF),
                pltpu.VMEM((D, S1 * T), BF),
                pltpu.VMEM((2, S1 * T, QB), F32),
                pltpu.VMEM((S1 * SUB, QB), F32),
                pltpu.VMEM((S2 * SUB, QB), F32),
                pltpu.VMEM((HKV, NB, D, QB), F32),
                pltpu.VMEM((HKV, NB, 8, QB), F32),
                pltpu.SemaphoreType.DMA((2,)),
                pltpu.SemaphoreType.DMA((HKV,)),
                pltpu.SemaphoreType.DMA((HKV,)),
                pltpu.SemaphoreType.DMA((8, HKV)),
                pltpu.SemaphoreType.DMA((8, HKV)),
            ],
            compiler_params=pltpu.CompilerParams(
                vmem_limit_bytes=60 << 20, collective_id=0, has_side_effects=True),
        )(q, k, v)

    return jax.shard_map(local, mesh=mesh, in_specs=(spec, spec, spec), out_specs=spec, check_vma=False)
```

time: 137 us -> 52.1 us (0.38)
  waiting for transfers between devices: 63.5 us -> 0 us
  between operations: 13.4 us -> 0.01 us
  local copies, waits for them, and re-layouts: 10.4 us -> 5.16 us
  Pallas kernels: 49.8 us -> 46.8 us
    all_gather x2 -> x0, waiting for transfers between devices: 62.1 us -> none  [order(): x = lax.all_gather(x, AXES, axis=0, tiled=True)]
    reshape x2 -> x0, local copies, waits for them, and re-layouts: 10.4 us -> none  [order(): x = x.reshape(DEV, NB, SUB, HKV, D)]
    unnamed x0 -> x1, local copies, waits for them, and re-layouts: none -> 5.16 us
    pallas_call x1, Pallas kernels: 49.8 us -> 46.8 us  [local(): pl.pallas_call(kernel, out_shape=jax.ShapeDtypeStruct(q.shape, q.dtype),...]
    unnamed x2 -> x0, waiting for transfers between devices: 1.41 us -> none
  transfers between devices with their start and end apart: 2 -> 0, of which waited for: 2 -> 0; matrix products, arithmetic and copies ran while one was open for 4% -> 0% of each run, Pallas kernels for 0% -> 0%
where the time goes in v2:
time: 52.1 us; the launch traced here: 52 us
  Pallas kernels  46.8 us (90%)
  local copies, waits for them, and re-layouts  5.16 us (10%)
    pallas_call x1, Pallas kernels, local(): pl.pallas_call(kernel, out_shape=jax.ShapeDtypeStruct(q.shape, q.dtype),...  46.8 us
    unnamed x1, local copies, waits for them, and re-layouts  5.16 us

profile of v2, /device:TPU:0, one launch (start us, length us, event | category | flops | bytes accessed | tf_op | source)
XLA Modules:
  0.0 52.0 jit_solution(10676040331821741831)
XLA Ops:
  0.0 46.8 %shard_map.37 = bf16[256,64,128]{2,1,0:T(8,128)(2,1)} custom-call(bf16[256,64,128]{2,1,0:T(8,128)(2,1)} %q_hbm.1, bf16[256,8,128]{2,1,0:T(8,128)(2,1)} %k_hbm.1, bf16[256,8,128]{2,1,0:T(8,128)(2,1)} %v_hbm.1), custom_call_target="tpu_custom_call" | custom-call | tf_op jit(solution)/shard_map/pallas_call | solution.py:204
  46.8 5.2 %copy.5 = bf16[256,64,128]{2,1,0:T(8,128)(2,1)} copy(bf16[256,64,128]{2,1,0:T(8,128)(2,1)} %shard_map.37) | data formatting | bytes 8388608

commit v3 on v2

--- a/solution.py
+++ b/solution.py
@@ -23,6 +23,10 @@
 
 def chunks(n):
     return [(r, min(r + 256, n)) for r in range(0, n, 256)]
+
+
+def by_tile(kv, h, nslot):
+    return jnp.concatenate([kv[h, s, 1, t * SUB:(t + 1) * SUB] for t in range(NB) for s in range(nslot)], axis=0)
 
 
 def fold(f, x):
@@ -69,8 +73,8 @@
         finish(j, m, a, jnp.sum(acc[0], axis=0, keepdims=True), acc[1])
 
 
-def kernel(q_hbm, k_hbm, v_hbm, o_hbm, qb, ob, raw, wide, kv1, kv2, vt, sref, bias1, bias2, oacc, ml,
-           lsem, qsem, osem, ssem, rsem):
+def kernel(q_hbm, k_hbm, v_hbm, ob, qb, raw, wide, kv1, kv2, vt, sref, bias1, bias2, oacc, ml,
+           lsem, qsem, ssem, rsem):
     cx, cy, cz = lax.axis_index("cx"), lax.axis_index("cy"), lax.axis_index("cz")
     me = (cx * 2 + cy) * 2 + cz
     nx = {"cy": 1 - cy}
@@ -88,23 +92,20 @@
     def qload(h):
         return pltpu.make_async_copy(q_hbm.at[:, pl.ds(pl.multiple_of(h * G, G), G), :], qb.at[h], qsem.at[h])
 
-    def ostore(h):
-        return pltpu.make_async_copy(ob.at[h], o_hbm.at[:, pl.ds(pl.multiple_of(h * G, G), G), :], osem.at[h])
-
     @pl.loop(0, HKV)
     def _(h):
         qload(h).start()
 
     def rdma(kind, h):
         src, dst, dev = (
-            (kv1.at[h, :, :, 0], kv1.at[h, :, :, 2], nx),
-            (kv1.at[h, :, :, 0], kv1.at[h, :, :, 4], ny),
-            (kv1.at[h, :, :, 0], kv1.at[h, :, :, 1], sib),
-            (kv1.at[h, :, :, 2], kv1.at[h, :, :, 3], sib),
-            (kv1.at[h, :, :, 4], kv1.at[h, :, :, 5], sib),
-            (kv1.at[h, 0, :, 2], kv2.at[h, 0, :, 0], ny),
-            (kv1.at[h, 1, :, 4], kv2.at[h, 1, :, 0], nx),
-            (kv2.at[h, :, :, 0], kv2.at[h, :, :, 1], sib),
+            (kv1.at[h, 0], kv1.at[h, 2], nx),
+            (kv1.at[h, 0], kv1.at[h, 4], ny),
+            (kv1.at[h, 0], kv1.at[h, 1], sib),
+            (kv1.at[h, 2], kv1.at[h, 3], sib),
+            (kv1.at[h, 4], kv1.at[h, 5], sib),
+            (kv1.at[h, 2, 0], kv2.at[h, 0, 0], ny),
+            (kv1.at[h, 4, 1], kv2.at[h, 0, 1], nx),
+            (kv2.at[h, 0], kv2.at[h, 1], sib),
         )[kind]
         return pltpu.make_async_remote_copy(src, dst, ssem.at[kind, h], rsem.at[kind, h], dev,
                                             pl.DeviceIdType.MESH)
@@ -120,7 +121,7 @@
         loads[i].wait()
         wide[...] = raw[i].astype(F32).reshape(T * HKV, D)
         for h in range(HKV):
-            kv1[h, i, :, 0] = wide[pl.ds(h, T, stride=HKV), :].astype(BF).reshape(NB, SUB, D)
+            kv1[h, 0, i] = wide[pl.ds(h, T, stride=HKV), :].astype(BF)
     pl.semaphore_wait(barrier, 3)
 
     @pl.loop(0, HKV)
@@ -153,14 +154,14 @@
         qload(h).wait()
         for kind in (2, 3, 4):
             rdma(kind, h).wait_recv()
-        vt[...] = kv1[h, 1].reshape(S1 * T, D).T
+        vt[...] = by_tile(kv1, h, S1).T
 
         def finish(j, m, a, l, o):
             oacc[h, j] = o
             ml[h, j, 0:1] = m
             ml[h, j, 1:2] = l
 
-        blocks(S1, lambda j: qb[h, j * SUB:(j + 1) * SUB].reshape(QB, D), lambda t, s: kv1[h, 0, t, s],
+        blocks(S1, lambda j: qb[h, j * SUB:(j + 1) * SUB].reshape(QB, D), lambda t, s: kv1[h, s, 0, t * SUB:(t + 1) * SUB],
                vt, bias1, sref, lambda j, m: (m, None), finish)
 
     pass_on2(0)
@@ -172,7 +173,7 @@
             pass_on2(h + 1)
 
         rdma(7, h).wait_recv()
-        vt[:, :S2 * T] = kv2[h, 1].reshape(S2 * T, D).T
+        vt[:, :S2 * T] = by_tile(kv2, h, S2).T
 
         def begin(j, m):
             m1 = ml[h, j, 0:1]
@@ -185,34 +186,40 @@
             o = oacc[h, j] * (a * r) + o * r
             ob[h, j * SUB:(j + 1) * SUB] = o.T.astype(BF).reshape(SUB, G, D)
 
-        blocks(S2, lambda j: qb[h, j * SUB:(j + 1) * SUB].reshape(QB, D), lambda t, s: kv2[h, 0, t, s],
+        blocks(S2, lambda j: qb[h, j * SUB:(j + 1) * SUB].reshape(QB, D), lambda t, s: kv2[h, s, 0, t * SUB:(t + 1) * SUB],
                vt, bias2, sref, begin, finish)
-        ostore(h).start()
 
     @pl.loop(0, HKV)
     def _(h):
         for kind in range(8):
             rdma(kind, h).wait_send()
-        ostore(h).wait()
+
+
+def spread(ob, o_hbm, sem):
+    copies = [pltpu.make_async_copy(ob.at[h], o_hbm.at[:, h * G:(h + 1) * G, :], sem.at[h]) for h in range(HKV)]
+    for x in copies:
+        x.start()
+    for x in copies:
+        x.wait()
 
 
 def solution(mesh):
     spec = P(("dp", "cx", "cy", "cz"))
 
     def local(q, k, v):
-        hbm = pl.BlockSpec(memory_space=pl.ANY)
-        return pl.pallas_call(
+        hbm = pl.BlockSpec(memory_space=pltpu.HBM)
+        vmem = pl.BlockSpec(memory_space=pltpu.VMEM)
+        heads = pl.pallas_call(
             kernel,
-            out_shape=jax.ShapeDtypeStruct(q.shape, q.dtype),
+            out_shape=pltpu.VMEM((HKV, T, G, D), BF),
             in_specs=[hbm] * 3,
-            out_specs=hbm,
+            out_specs=vmem,
             scratch_shapes=[
-                pltpu.VMEM((HKV, T, G, D), BF),
                 pltpu.VMEM((HKV, T, G, D), BF),
                 pltpu.VMEM((2, T, HKV, D), BF),
                 pltpu.VMEM((T * HKV, D), F32),
-                pltpu.VMEM((HKV, 2, NB, S1, SUB, D), BF),
-                pltpu.VMEM((HKV, 2, NB, S2, SUB, D), BF),
+                pltpu.VMEM((HKV, S1, 2, T, D), BF),
+                pltpu.VMEM((HKV, S2, 2, T, D), BF),
                 pltpu.VMEM((D, S1 * T), BF),
                 pltpu.VMEM((2, S1 * T, QB), F32),
                 pltpu.VMEM((S1 * SUB, QB), F32),
@@ -221,12 +228,19 @@
                 pltpu.VMEM((HKV, NB, 8, QB), F32),
                 pltpu.SemaphoreType.DMA((2,)),
                 pltpu.SemaphoreType.DMA((HKV,)),
-                pltpu.SemaphoreType.DMA((HKV,)),
                 pltpu.SemaphoreType.DMA((8, HKV)),
                 pltpu.SemaphoreType.DMA((8, HKV)),
             ],
             compiler_params=pltpu.CompilerParams(
-                vmem_limit_bytes=60 << 20, collective_id=0, has_side_effects=True),
+                vmem_limit_bytes=48 << 20, collective_id=0, has_side_effects=True),
         )(q, k, v)
+        return pl.pallas_call(
+            spread,
+            out_shape=jax.ShapeDtypeStruct(q.shape, q.dtype),
+            in_specs=[vmem],
+            out_specs=hbm,
+            scratch_shapes=[pltpu.SemaphoreType.DMA((HKV,))],
+            compiler_params=pltpu.CompilerParams(vmem_limit_bytes=1 << 20),
+        )(heads)
 
     return jax.shard_map(local, mesh=mesh, in_specs=(spec, spec, spec), out_specs=spec, check_vma=False)

time: 52.1 us -> 50.3 us (0.965)
  local copies, waits for them, and re-layouts: 5.16 us -> 2.08 us
  Pallas kernels: 46.8 us -> 48 us
    unnamed x1 -> x4, local copies, waits for them, and re-layouts: 5.16 us -> 2.08 us
    pallas_call x1 -> x2, Pallas kernels: 46.8 us -> 48 us  [the longest x1 46 us: local(): pl.pallas_call(kernel, out_shape=pltpu.VMEM((HKV, T, G, D), BF), in_specs...]
where the time goes in v3:
time: 50.3 us; the launch traced here: 50.1 us
  Pallas kernels  48 us (95%)
  local copies, waits for them, and re-layouts  2.08 us (4%)
    pallas_call x1, Pallas kernels, local(): pl.pallas_call(kernel, out_shape=pltpu.VMEM((HKV, T, G, D), BF), in_specs...  46 us
    unnamed x4, local copies, waits for them, and re-layouts  2.08 us
    pallas_call x1, Pallas kernels, local(): pl.pallas_call(spread, out_shape=jax.ShapeDtypeStruct(q.shape, q.dtype),...  2.07 us

profile of v3, /device:TPU:0, one launch (start us, length us, event | category | flops | bytes accessed | tf_op | source)
XLA Modules:
  0.0 50.1 jit_solution(2119691919075565247)
XLA Ops:
  0.0 0.0 copy-start
  0.0 1.0 %copy-done = bf16[256,8,128]{2,1,0:T(8,128)(2,1)S(1)} copy-done((bf16[256,8,128]{2,1,0:T(8,128)(2,1)S(1)}, bf16[256,8,128]{2,1,0:T(8,128)(2,1)}, u32[]{:S(2)}) %copy-start) | copy-done | bytes 524312
  1.0 0.0 copy-start.1
  1.0 1.0 %copy-done.1 = bf16[256,8,128]{2,1,0:T(8,128)(2,1)S(1)} copy-done((bf16[256,8,128]{2,1,0:T(8,128)(2,1)S(1)}, bf16[256,8,128]{2,1,0:T(8,128)(2,1)}, u32[]{:S(2)}) %copy-start.1) | copy-done | bytes 524312
  2.1 46.0 %shard_map.37.ob = bf16[8,256,8,128]{3,2,1,0:T(8,128)(2,1)S(1)} custom-call(bf16[256,64,128]{2,1,0:T(8,128)(2,1)} %q_hbm.1, bf16[256,8,128]{2,1,0:T(8,128)(2,1)S(1)} %copy-done, bf16[256,8,128]{2,1,0:T(8,128)(2,1)S(1)} %copy-done.1), custom_call_target="tpu_custom_call" | custom-call | tf_op jit(solution)/shard_map/pallas_call | solution.py:212
  48.1 2.1 %shard_map.38 = bf16[256,64,128]{2,1,0:T(8,128)(2,1)} custom-call(bf16[8,256,8,128]{3,2,1,0:T(8,128)(2,1)S(1)} %shard_map.37.ob), custom_call_target="tpu_custom_call" | custom-call | tf_op jit(solution)/shard_map/pallas_call | solution.py:237
Async XLA Ops:
  0.0 1.0 %copy-start = (bf16[256,8,128]{2,1,0:T(8,128)(2,1)S(1)}, bf16[256,8,128]{2,1,0:T(8,128)(2,1)}, u32[]{:S(2)}) copy-start(bf16[256,8,128]{2,1,0:T(8,128)(2,1)} %k_hbm.1) | copy-start | bytes 1572868
  1.0 1.0 %copy-start.1 = (bf16[256,8,128]{2,1,0:T(8,128)(2,1)S(1)}, bf16[256,8,128]{2,1,0:T(8,128)(2,1)}, u32[]{:S(2)}) copy-start(bf16[256,8,128]{2,1,0:T(8,128)(2,1)} %v_hbm.1) | copy-start | bytes 1572868

commit v4 on v3

--- a/solution.py
+++ b/solution.py
@@ -73,7 +73,25 @@
         finish(j, m, a, jnp.sum(acc[0], axis=0, keepdims=True), acc[1])
 
 
-def kernel(q_hbm, k_hbm, v_hbm, ob, qb, raw, wide, kv1, kv2, vt, sref, bias1, bias2, oacc, ml,
+def diagonal(h, out, qb, kv2, bias2, oacc, ml, vt, sref):
+    vt[:, :S2 * T] = by_tile(kv2, h, S2).T
+
+    def begin(j, m):
+        m1 = ml[h, j, 0:1]
+        m = jnp.maximum(m, m1)
+        return m, jnp.exp2((m1 - m) * C)
+
+    def finish(j, m, a, l, o):
+        l = ml[h, j, 1:2] * a + l
+        r = 1.0 / l
+        o = oacc[h, j] * (a * r) + o * r
+        out[j * SUB:(j + 1) * SUB] = o.T.astype(BF).reshape(SUB, G, D)
+
+    blocks(S2, lambda j: qb[h, j * SUB:(j + 1) * SUB].reshape(QB, D),
+           lambda t, s: kv2[h, s, 0, t * SUB:(t + 1) * SUB], vt, bias2, sref, begin, finish)
+
+
+def kernel(q_hbm, k_hbm, v_hbm, ob, qb, kv2, bias2, oacc, ml, raw, wide, kv1, vt, sref, bias1,
            lsem, qsem, ssem, rsem):
     cx, cy, cz = lax.axis_index("cx"), lax.axis_index("cy"), lax.axis_index("cz")
     me = (cx * 2 + cy) * 2 + cz
@@ -119,18 +137,23 @@
 
     for i in range(2):
         loads[i].wait()
-        wide[...] = raw[i].astype(F32).reshape(T * HKV, D)
-        for h in range(HKV):
-            kv1[h, 0, i] = wide[pl.ds(h, T, stride=HKV), :].astype(BF)
-    pl.semaphore_wait(barrier, 3)
-
-    @pl.loop(0, HKV)
-    def _(h):
+        wide[i] = raw[i].astype(F32).reshape(T * HKV, D)
+
+    def send(h):
         for kind in range(3):
             rdma(kind, h).start()
 
+    for h in range(HKV):
+        for i in range(2):
+            kv1[h, 0, i] = wide[i, pl.ds(h, T, stride=HKV), :].astype(BF)
+        if h == 1:
+            pl.semaphore_wait(barrier, 3)
+        if h:
+            send(h - 1)
+
     mask(S1, 0, bias1)
     mask(S2, S1, bias2)
+    send(HKV - 1)
 
     def pass_on(h):
         rdma(0, h).wait_recv()
@@ -166,28 +189,13 @@
 
     pass_on2(0)
 
-    @pl.loop(0, HKV)
-    def _(h):
-        @pl.when(h < HKV - 1)
-        def _():
-            pass_on2(h + 1)
-
+    @pl.loop(0, HKV - 1)
+    def _(h):
+        pass_on2(h + 1)
         rdma(7, h).wait_recv()
-        vt[:, :S2 * T] = by_tile(kv2, h, S2).T
-
-        def begin(j, m):
-            m1 = ml[h, j, 0:1]
-            m = jnp.maximum(m, m1)
-            return m, jnp.exp2((m1 - m) * C)
-
-        def finish(j, m, a, l, o):
-            l = ml[h, j, 1:2] * a + l
-            r = 1.0 / l
-            o = oacc[h, j] * (a * r) + o * r
-            ob[h, j * SUB:(j + 1) * SUB] = o.T.astype(BF).reshape(SUB, G, D)
-
-        blocks(S2, lambda j: qb[h, j * SUB:(j + 1) * SUB].reshape(QB, D), lambda t, s: kv2[h, s, 0, t * SUB:(t + 1) * SUB],
-               vt, bias2, sref, begin, finish)
+        diagonal(h, ob.at[h], qb, kv2, bias2, oacc, ml, vt, sref)
+
+    rdma(7, HKV - 1).wait_recv()
 
     @pl.loop(0, HKV)
     def _(h):
@@ -195,10 +203,13 @@
             rdma(kind, h).wait_send()
 
 
-def spread(ob, o_hbm, sem):
-    copies = [pltpu.make_async_copy(ob.at[h], o_hbm.at[:, h * G:(h + 1) * G, :], sem.at[h]) for h in range(HKV)]
-    for x in copies:
+def spread(ob, qb, kv2, bias2, oacc, ml, o_hbm, last, vt, sref, sem):
+    copies = [pltpu.make_async_copy(ob.at[h] if h < HKV - 1 else last, o_hbm.at[:, h * G:(h + 1) * G, :], sem.at[h])
+              for h in range(HKV)]
+    for x in copies[:-1]:
         x.start()
+    diagonal(HKV - 1, last, qb, kv2, bias2, oacc, ml, vt, sref)
+    copies[-1].start()
     for x in copies:
         x.wait()
 
@@ -209,38 +220,45 @@
     def local(q, k, v):
         hbm = pl.BlockSpec(memory_space=pltpu.HBM)
         vmem = pl.BlockSpec(memory_space=pltpu.VMEM)
-        heads = pl.pallas_call(
+        parts = pl.pallas_call(
             kernel,
-            out_shape=pltpu.VMEM((HKV, T, G, D), BF),
+            out_shape=[
+                pltpu.VMEM((HKV - 1, T, G, D), BF),
+                pltpu.VMEM((HKV, T, G, D), BF),
+                pltpu.VMEM((HKV, S2, 2, T, D), BF),
+                pltpu.VMEM((S2 * SUB, QB), F32),
+                pltpu.VMEM((HKV, NB, D, QB), F32),
+                pltpu.VMEM((HKV, NB, 8, QB), F32),
+            ],
             in_specs=[hbm] * 3,
-            out_specs=vmem,
+            out_specs=[vmem] * 6,
             scratch_shapes=[
-                pltpu.VMEM((HKV, T, G, D), BF),
                 pltpu.VMEM((2, T, HKV, D), BF),
-                pltpu.VMEM((T * HKV, D), F32),
+                pltpu.VMEM((2, T * HKV, D), F32),
                 pltpu.VMEM((HKV, S1, 2, T, D), BF),
-                pltpu.VMEM((HKV, S2, 2, T, D), BF),
                 pltpu.VMEM((D, S1 * T), BF),
                 pltpu.VMEM((2, S1 * T, QB), F32),
                 pltpu.VMEM((S1 * SUB, QB), F32),
-                pltpu.VMEM((S2 * SUB, QB), F32),
-                pltpu.VMEM((HKV, NB, D, QB), F32),
-                pltpu.VMEM((HKV, NB, 8, QB), F32),
                 pltpu.SemaphoreType.DMA((2,)),
                 pltpu.SemaphoreType.DMA((HKV,)),
                 pltpu.SemaphoreType.DMA((8, HKV)),
                 pltpu.SemaphoreType.DMA((8, HKV)),
             ],
             compiler_params=pltpu.CompilerParams(
-                vmem_limit_bytes=48 << 20, collective_id=0, has_side_effects=True),
-        )(q, k, v)
+                vmem_limit_bytes=36 << 20, collective_id=0, has_side_effects=True),
+        )(*(pltpu.with_memory_space_constraint(x, pltpu.HBM) for x in (q, k, v)))
         return pl.pallas_call(
             spread,
             out_shape=jax.ShapeDtypeStruct(q.shape, q.dtype),
-            in_specs=[vmem],
+            in_specs=[vmem] * 6,
             out_specs=hbm,
-            scratch_shapes=[pltpu.SemaphoreType.DMA((HKV,))],
-            compiler_params=pltpu.CompilerParams(vmem_limit_bytes=1 << 20),
-        )(heads)
+            scratch_shapes=[
+                pltpu.VMEM((T, G, D), BF),
+                pltpu.VMEM((D, S2 * T), BF),
+                pltpu.VMEM((2, S2 * T, QB), F32),
+                pltpu.SemaphoreType.DMA((HKV,)),
+            ],
+            compiler_params=pltpu.CompilerParams(vmem_limit_bytes=8 << 20),
+        )(*parts)
 
     return jax.shard_map(local, mesh=mesh, in_specs=(spec, spec, spec), out_specs=spec, check_vma=False)

time: 50.3 us -> 47.4 us (0.942)
  local copies, waits for them, and re-layouts: 2.08 us -> 0 us
  Pallas kernels: 48 us -> 47.3 us
    unnamed x4 -> x0, local copies, waits for them, and re-layouts: 2.08 us -> none
    pallas_call x1, Pallas kernels: 46 us -> 44.7 us  [local(): pl.pallas_call(kernel, out_shape=[pltpu.VMEM((HKV - 1, T, G, D), BF), plt...]
where the time goes in v4:
time: 47.4 us; the launch traced here: 47.3 us
  Pallas kernels  47.3 us (100%)
    pallas_call x1, Pallas kernels, local(): pl.pallas_call(kernel, out_shape=[pltpu.VMEM((HKV - 1, T, G, D), BF), plt...  44.7 us
    pallas_call x1, Pallas kernels, local(): pl.pallas_call(spread, out_shape=jax.ShapeDtypeStruct(q.shape, q.dtype),...  2.57 us

profile of v4, /device:TPU:0, one launch (start us, length us, event | category | flops | bytes accessed | tf_op | source)
XLA Modules:
  0.0 47.3 jit_solution(8470145700696705969)
XLA Ops:
  0.0 44.7 %shard_map.37 = (bf16[7,256,8,128]{3,2,1,0:T(8,128)(2,1)S(1)}, bf16[8,256,8,128]{3,2,1,0:T(8,128)(2,1)S(1)}, bf16[8,2,2,256,128]{4,3,2,1,0:T(8,128)(2,1)S(1)}, f...) custom-call(bf16[256,64,128]{2,1,0:T(8,128)(2,1)} %q_hbm.1, ...), custom_call_target="tpu_custom_call" | custom-call | tf_op jit(solution)/shard_map/pallas_call | solution.py:223
  44.7 2.6 %shard_map.38 = bf16[256,64,128]{2,1,0:T(8,128)(2,1)} custom-call(bf16[7,256,8,128]{3,2,1,0:T(8,128)(2,1)S(1)} %get-tuple-element.11.ob, bf16[8,256,8,128]{3,2,1,0:T(8,128)(2,1)S(1)} %get-tuple-element.12.qb, bf16[8,2,2,256,128]{4,3,2,1,0:T(8,128)(2,1)S(1)} %get-tuple-element.13.kv2, f32[64,256]{1,0:T(8,128)S(1)} %get-tuple-element.14.bias2, ...), custom_call_target="tpu_custom_call" | custom-call | tf_op jit(solution)/shard_map/pallas_call | solution.py:250

commit v5 on v4

--- a/solution.py
+++ b/solution.py
@@ -73,7 +73,7 @@
         finish(j, m, a, jnp.sum(acc[0], axis=0, keepdims=True), acc[1])
 
 
-def diagonal(h, out, qb, kv2, bias2, oacc, ml, vt, sref):
+def diagonal(h, out, qb, kv2, bias2, oacc, ml, vt, sref, done=None):
     vt[:, :S2 * T] = by_tile(kv2, h, S2).T
 
     def begin(j, m):
@@ -82,6 +82,8 @@
         return m, jnp.exp2((m1 - m) * C)
 
     def finish(j, m, a, l, o):
+        if done:
+            done(j)
         l = ml[h, j, 1:2] * a + l
         r = 1.0 / l
         o = oacc[h, j] * (a * r) + o * r
@@ -109,10 +111,6 @@
 
     def qload(h):
         return pltpu.make_async_copy(q_hbm.at[:, pl.ds(pl.multiple_of(h * G, G), G), :], qb.at[h], qsem.at[h])
-
-    @pl.loop(0, HKV)
-    def _(h):
-        qload(h).start()
 
     def rdma(kind, h):
         src, dst, dev = (
@@ -151,9 +149,14 @@
         if h:
             send(h - 1)
 
-    mask(S1, 0, bias1)
     mask(S2, S1, bias2)
     send(HKV - 1)
+
+    @pl.loop(0, HKV)
+    def _(h):
+        qload(h).start()
+
+    mask(S1, 0, bias1)
 
     def pass_on(h):
         rdma(0, h).wait_recv()
@@ -204,12 +207,20 @@
 
 
 def spread(ob, qb, kv2, bias2, oacc, ml, o_hbm, last, vt, sref, sem):
-    copies = [pltpu.make_async_copy(ob.at[h] if h < HKV - 1 else last, o_hbm.at[:, h * G:(h + 1) * G, :], sem.at[h])
-              for h in range(HKV)]
-    for x in copies[:-1]:
+    copies = [pltpu.make_async_copy(ob.at[h], o_hbm.at[:, h * G:(h + 1) * G, :], sem.at[h]) for h in range(HKV - 1)]
+    copies += [pltpu.make_async_copy(last.at[j * SUB:(j + 1) * SUB],
+                                     o_hbm.at[j * SUB:(j + 1) * SUB, (HKV - 1) * G:, :], sem.at[HKV - 1 + j])
+               for j in range(NB)]
+    for x in copies[:HKV - 1]:
         x.start()
-    diagonal(HKV - 1, last, qb, kv2, bias2, oacc, ml, vt, sref)
-    copies[-1].start()
+
+    def done(j):
+        i = ORDER.index(j)
+        if i:
+            copies[HKV - 1 + ORDER[i - 1]].start()
+
+    diagonal(HKV - 1, last, qb, kv2, bias2, oacc, ml, vt, sref, done)
+    copies[HKV - 1 + ORDER[-1]].start()
     for x in copies:
         x.wait()
 
@@ -256,7 +267,7 @@
                 pltpu.VMEM((T, G, D), BF),
                 pltpu.VMEM((D, S2 * T), BF),
                 pltpu.VMEM((2, S2 * T, QB), F32),
-                pltpu.SemaphoreType.DMA((HKV,)),
+                pltpu.SemaphoreType.DMA((HKV - 1 + NB,)),
             ],
             compiler_params=pltpu.CompilerParams(vmem_limit_bytes=8 << 20),
         )(*parts)

time: 47.4 us -> 47.7 us (level)
  no operation moved by 1% of the time
where the time goes in v5:
time: 47.7 us; the launch traced here: 47.6 us
  Pallas kernels  47.6 us (100%)
    pallas_call x1, Pallas kernels, local(): pl.pallas_call(kernel, out_shape=[pltpu.VMEM((HKV - 1, T, G, D), BF), plt...  44.7 us
    pallas_call x1, Pallas kernels, local(): pl.pallas_call(spread, out_shape=jax.ShapeDtypeStruct(q.shape, q.dtype),...  2.86 us

profile of v5, /device:TPU:0, one launch (start us, length us, event | category | flops | bytes accessed | tf_op | source)
XLA Modules:
  0.0 47.6 jit_solution(6248298342942269322)
XLA Ops:
  0.0 44.7 %shard_map.37 = (bf16[7,256,8,128]{3,2,1,0:T(8,128)(2,1)S(1)}, bf16[8,256,8,128]{3,2,1,0:T(8,128)(2,1)S(1)}, bf16[8,2,2,256,128]{4,3,2,1,0:T(8,128)(2,1)S(1)}, f...) custom-call(bf16[256,64,128]{2,1,0:T(8,128)(2,1)} %q_hbm.1, ...), custom_call_target="tpu_custom_call" | custom-call | tf_op jit(solution)/shard_map/pallas_call | solution.py:234
  44.7 2.9 %shard_map.38 = bf16[256,64,128]{2,1,0:T(8,128)(2,1)} custom-call(bf16[7,256,8,128]{3,2,1,0:T(8,128)(2,1)S(1)} %get-tuple-element.11.ob, bf16[8,256,8,128]{3,2,1,0:T(8,128)(2,1)S(1)} %get-tuple-element.12.qb, bf16[8,2,2,256,128]{4,3,2,1,0:T(8,128)(2,1)S(1)} %get-tuple-element.13.kv2, f32[64,256]{1,0:T(8,128)S(1)} %get-tuple-element.14.bias2, ...), custom_call_target="tpu_custom_call" | custom-call | tf_op jit(solution)/shard_map/pallas_call | solution.py:261

commit v6 on v4

--- a/solution.py
+++ b/solution.py
@@ -25,8 +25,8 @@
     return [(r, min(r + 256, n)) for r in range(0, n, 256)]
 
 
-def by_tile(kv, h, nslot):
-    return jnp.concatenate([kv[h, s, 1, t * SUB:(t + 1) * SUB] for t in range(NB) for s in range(nslot)], axis=0)
+def by_tile(kv, h, s0, ns):
+    return jnp.concatenate([kv[h, s, 1, t * SUB:(t + 1) * SUB] for t in range(NB) for s in range(s0, s0 + ns)], axis=0)
 
 
 def fold(f, x):
@@ -73,25 +73,33 @@
         finish(j, m, a, jnp.sum(acc[0], axis=0, keepdims=True), acc[1])
 
 
-def diagonal(h, out, qb, kv2, bias2, oacc, ml, vt, sref):
-    vt[:, :S2 * T] = by_tile(kv2, h, S2).T
+def attend(h, kv, s0, ns, bias, qb, oacc, ml, vt, sref, first=False, out=None):
+    vt[:, :ns * T] = by_tile(kv, h, s0, ns).T
 
     def begin(j, m):
+        if first:
+            return m, None
         m1 = ml[h, j, 0:1]
         m = jnp.maximum(m, m1)
         return m, jnp.exp2((m1 - m) * C)
 
     def finish(j, m, a, l, o):
-        l = ml[h, j, 1:2] * a + l
+        if not first:
+            l = ml[h, j, 1:2] * a + l
+        if out is None:
+            oacc[h, j] = o if first else oacc[h, j] * a + o
+            ml[h, j, 0:1] = m
+            ml[h, j, 1:2] = l
+            return
         r = 1.0 / l
         o = oacc[h, j] * (a * r) + o * r
         out[j * SUB:(j + 1) * SUB] = o.T.astype(BF).reshape(SUB, G, D)
 
-    blocks(S2, lambda j: qb[h, j * SUB:(j + 1) * SUB].reshape(QB, D),
-           lambda t, s: kv2[h, s, 0, t * SUB:(t + 1) * SUB], vt, bias2, sref, begin, finish)
-
-
-def kernel(q_hbm, k_hbm, v_hbm, ob, qb, kv2, bias2, oacc, ml, raw, wide, kv1, vt, sref, bias1,
+    blocks(ns, lambda j: qb[h, j * SUB:(j + 1) * SUB].reshape(QB, D),
+           lambda t, s: kv[h, s0 + s, 0, t * SUB:(t + 1) * SUB], vt, bias, sref, begin, finish)
+
+
+def kernel(q_hbm, k_hbm, v_hbm, ob, qb, kv2, bias2, oacc, ml, raw, wide, kv1, vt, sref, bias0, bias1,
            lsem, qsem, ssem, rsem):
     cx, cy, cz = lax.axis_index("cx"), lax.axis_index("cy"), lax.axis_index("cz")
     me = (cx * 2 + cy) * 2 + cz
@@ -109,10 +117,6 @@
 
     def qload(h):
         return pltpu.make_async_copy(q_hbm.at[:, pl.ds(pl.multiple_of(h * G, G), G), :], qb.at[h], qsem.at[h])
-
-    @pl.loop(0, HKV)
-    def _(h):
-        qload(h).start()
 
     def rdma(kind, h):
         src, dst, dev = (
@@ -151,9 +155,15 @@
         if h:
             send(h - 1)
 
-    mask(S1, 0, bias1)
-    mask(S2, S1, bias2)
+    mask(2, 0, bias0)
     send(HKV - 1)
+
+    @pl.loop(0, HKV)
+    def _(h):
+        qload(h).start()
+
+    mask(4, 2, bias1)
+    mask(2, 6, bias2)
 
     def pass_on(h):
         rdma(0, h).wait_recv()
@@ -166,6 +176,12 @@
         rdma(6, h).wait_recv()
         rdma(7, h).start()
 
+    @pl.loop(0, HKV)
+    def _(h):
+        qload(h).wait()
+        rdma(2, h).wait_recv()
+        attend(h, kv1, 0, 2, bias0, qb, oacc, ml, vt, sref, first=True)
+
     pass_on(0)
 
     @pl.loop(0, HKV)
@@ -174,18 +190,9 @@
         def _():
             pass_on(h + 1)
 
-        qload(h).wait()
-        for kind in (2, 3, 4):
+        for kind in (3, 4):
             rdma(kind, h).wait_recv()
-        vt[...] = by_tile(kv1, h, S1).T
-
-        def finish(j, m, a, l, o):
-            oacc[h, j] = o
-            ml[h, j, 0:1] = m
-            ml[h, j, 1:2] = l
-
-        blocks(S1, lambda j: qb[h, j * SUB:(j + 1) * SUB].reshape(QB, D), lambda t, s: kv1[h, s, 0, t * SUB:(t + 1) * SUB],
-               vt, bias1, sref, lambda j, m: (m, None), finish)
+        attend(h, kv1, 2, 4, bias1, qb, oacc, ml, vt, sref)
 
     pass_on2(0)
 
@@ -193,7 +200,7 @@
     def _(h):
         pass_on2(h + 1)
         rdma(7, h).wait_recv()
-        diagonal(h, ob.at[h], qb, kv2, bias2, oacc, ml, vt, sref)
+        attend(h, kv2, 0, 2, bias2, qb, oacc, ml, vt, sref, out=ob.at[h])
 
     rdma(7, HKV - 1).wait_recv()
 
@@ -208,7 +215,7 @@
               for h in range(HKV)]
     for x in copies[:-1]:
         x.start()
-    diagonal(HKV - 1, last, qb, kv2, bias2, oacc, ml, vt, sref)
+    attend(HKV - 1, kv2, 0, 2, bias2, qb, oacc, ml, vt, sref, out=last)
     copies[-1].start()
     for x in copies:
         x.wait()
@@ -236,9 +243,10 @@
                 pltpu.VMEM((2, T, HKV, D), BF),
                 pltpu.VMEM((2, T * HKV, D), F32),
                 pltpu.VMEM((HKV, S1, 2, T, D), BF),
-                pltpu.VMEM((D, S1 * T), BF),
-                pltpu.VMEM((2, S1 * T, QB), F32),
-                pltpu.VMEM((S1 * SUB, QB), F32),
+                pltpu.VMEM((D, 4 * T), BF),
+                pltpu.VMEM((2, 4 * T, QB), F32),
+                pltpu.VMEM((2 * SUB, QB), F32),
+                pltpu.VMEM((4 * SUB, QB), F32),
                 pltpu.SemaphoreType.DMA((2,)),
                 pltpu.SemaphoreType.DMA((HKV,)),
                 pltpu.SemaphoreType.DMA((8, HKV)),

time: 47.4 us -> 46.3 us (0.977)
  Pallas kernels: 47.3 us -> 46.2 us
    pallas_call x1, Pallas kernels: 44.7 us -> 43.6 us  [local(): pl.pallas_call(kernel, out_shape=[pltpu.VMEM((HKV - 1, T, G, D), BF), plt...]
where the time goes in v6:
time: 46.3 us; the launch traced here: 46.2 us
  Pallas kernels  46.2 us (100%)
    pallas_call x1, Pallas kernels, local(): pl.pallas_call(kernel, out_shape=[pltpu.VMEM((HKV - 1, T, G, D), BF), plt...  43.6 us
    pallas_call x1, Pallas kernels, local(): pl.pallas_call(spread, out_shape=jax.ShapeDtypeStruct(q.shape, q.dtype),...  2.57 us

profile of v6, /device:TPU:0, one launch (start us, length us, event | category | flops | bytes accessed | tf_op | source)
XLA Modules:
  0.0 46.2 jit_solution(17486905776875975205)
XLA Ops:
  0.0 43.6 %shard_map.37 = (bf16[7,256,8,128]{3,2,1,0:T(8,128)(2,1)S(1)}, bf16[8,256,8,128]{3,2,1,0:T(8,128)(2,1)S(1)}, bf16[8,2,2,256,128]{4,3,2,1,0:T(8,128)(2,1)S(1)}, f...) custom-call(bf16[256,64,128]{2,1,0:T(8,128)(2,1)} %q_hbm.1, ...), custom_call_target="tpu_custom_call" | custom-call | tf_op jit(solution)/shard_map/pallas_call | solution.py:230
  43.6 2.6 %shard_map.38 = bf16[256,64,128]{2,1,0:T(8,128)(2,1)} custom-call(bf16[7,256,8,128]{3,2,1,0:T(8,128)(2,1)S(1)} %get-tuple-element.11.ob, bf16[8,256,8,128]{3,2,1,0:T(8,128)(2,1)S(1)} %get-tuple-element.12.qb, bf16[8,2,2,256,128]{4,3,2,1,0:T(8,128)(2,1)S(1)} %get-tuple-element.13.kv2, f32[64,256]{1,0:T(8,128)S(1)} %get-tuple-element.14.bias2, ...), custom_call_target="tpu_custom_call" | custom-call | tf_op jit(solution)/shard_map/pallas_call | solution.py:258

commit v7 on v6

--- a/solution.py
+++ b/solution.py
@@ -15,10 +15,12 @@
 S1 = 6
 S2 = 2
 C = (D ** -0.5) * 1.4426950408889634
-NT = (((1,), (1,)), ((), ()))
 ORDER = (0, 2, 4, 6, 7, 5, 3, 1)
+AHEAD = 3
+U0, U1, U2 = 2,2,1
 BF = jnp.bfloat16
 F32 = jnp.float32
+NT = (((1,), (1,)), ((), ()))
 
 
 def chunks(n):
@@ -33,57 +35,41 @@
     return f(x.reshape(-1, 8, x.shape[-1]), axis=0)
 
 
-def blocks(nslot, q_of, k_of, vt, bias, sref, begin, finish):
-    rows = nslot * SUB
-    st = {}
-
-    def scores(j, c):
+def attend(heads, kv, s0, ns, bias, qt, oacc, ml, vt, sref, arrive=None, first=False, out=None):
+    rows = ns * SUB
+    items = [(u, j) for u in range(len(heads)) for j in ORDER]
+    tops = {}
+
+    def scores(i, c):
+        u, j = items[i]
+        h = heads[u]
         r0, r1 = c
-        parts = [k_of(*divmod(u, nslot)) for u in range(r0 // SUB, r1 // SUB)]
-        s = lax.dot_general(jnp.concatenate(parts, axis=0), q_of(j), NT, preferred_element_type=F32)
+        if j == ORDER[0] and r0 == 0:
+            if arrive:
+                arrive(u)
+            vt[u, :, :ns * T] = by_tile(kv, h, s0, ns).T
+        parts = [kv[h, s0 + x % ns, 0, x // ns * SUB:(x // ns + 1) * SUB] for x in range(r0 // SUB, r1 // SUB)]
+        s = lax.dot_general(jnp.concatenate(parts, axis=0), qt[h, j * SUB:(j + 1) * SUB].reshape(QB, D), NT,
+                            preferred_element_type=F32)
         lo = max(r0, j * rows)
         if lo < r1:
             d = s[lo - r0:] + bias[lo - j * rows:r1 - j * rows]
             s = d if lo == r0 else jnp.concatenate([s[:lo - r0], d], axis=0)
-        sref[ORDER.index(j) % 2, r0:r1] = s
+        sref[i % (AHEAD + 1), r0:r1] = s
         m = fold(jnp.max, s)
-        st[j] = jnp.maximum(st[j], m) if j in st else m
-
-    def values(j, c, m, acc):
+        tops[i] = jnp.maximum(tops[i], m) if i in tops else m
+
+    def values(i, c, m, acc):
+        u, j = items[i]
         r0, r1 = c
-        p = jnp.exp2((sref[ORDER.index(j) % 2, r0:r1] - m) * C)
+        p = jnp.exp2((sref[i % (AHEAD + 1), r0:r1] - m) * C)
         l = fold(jnp.sum, p)
-        o = jnp.dot(vt[:, r0:r1], p.astype(BF), preferred_element_type=F32)
+        o = jnp.dot(vt[u, :, r0:r1], p.astype(BF), preferred_element_type=F32)
         return (acc[0] + l, acc[1] + o) if acc else (l, o)
 
-    for c in chunks((ORDER[0] + 1) * rows):
-        scores(ORDER[0], c)
-    for i, j in enumerate(ORDER):
-        m, a = begin(j, jnp.max(st[j], axis=0, keepdims=True))
-        acc = None
-        mine = chunks((j + 1) * rows)
-        later = chunks((ORDER[i + 1] + 1) * rows) if i + 1 < NB else []
-        done = 0
-        for t, c in enumerate(mine):
-            upto = len(later) * (t + 1) // len(mine)
-            for u in range(done, upto):
-                scores(ORDER[i + 1], later[u])
-            done = upto
-            acc = values(j, c, m, acc)
-        finish(j, m, a, jnp.sum(acc[0], axis=0, keepdims=True), acc[1])
-
-
-def attend(h, kv, s0, ns, bias, qb, oacc, ml, vt, sref, first=False, out=None):
-    vt[:, :ns * T] = by_tile(kv, h, s0, ns).T
-
-    def begin(j, m):
-        if first:
-            return m, None
-        m1 = ml[h, j, 0:1]
-        m = jnp.maximum(m, m1)
-        return m, jnp.exp2((m1 - m) * C)
-
-    def finish(j, m, a, l, o):
+    def finish(i, m, a, l, o):
+        u, j = items[i]
+        h = heads[u]
         if not first:
             l = ml[h, j, 1:2] * a + l
         if out is None:
@@ -93,13 +79,36 @@
             return
         r = 1.0 / l
         o = oacc[h, j] * (a * r) + o * r
-        out[j * SUB:(j + 1) * SUB] = o.T.astype(BF).reshape(SUB, G, D)
-
-    blocks(ns, lambda j: qb[h, j * SUB:(j + 1) * SUB].reshape(QB, D),
-           lambda t, s: kv[h, s0 + s, 0, t * SUB:(t + 1) * SUB], vt, bias, sref, begin, finish)
-
-
-def kernel(q_hbm, k_hbm, v_hbm, ob, qb, kv2, bias2, oacc, ml, raw, wide, kv1, vt, sref, bias0, bias1,
+        out(u)[j * SUB:(j + 1) * SUB] = o.T.astype(BF).reshape(SUB, G, D)
+
+    todo = [(i, c) for i, (u, j) in enumerate(items) for c in chunks((j + 1) * rows)]
+    total = len(todo)
+    sizes = [len(chunks((j + 1) * rows)) for u, j in items]
+    at = 0
+    while at < total and todo[at][0] < AHEAD:
+        scores(*todo[at])
+        at += 1
+    for i, (u, j) in enumerate(items):
+        top = jnp.max(tops[i], axis=0, keepdims=True)
+        m, a = top, None
+        if not first:
+            m1 = ml[heads[u], j, 0:1]
+            m = jnp.maximum(top, m1)
+            a = jnp.exp2((m1 - m) * C)
+        acc = None
+        goal = sum(sizes[:i + AHEAD + 1])
+        start = at
+        mine = chunks((j + 1) * rows)
+        for t, c in enumerate(mine):
+            upto = start + (goal - start) * (t + 1) // len(mine)
+            while at < upto:
+                scores(*todo[at])
+                at += 1
+            acc = values(i, c, m, acc)
+        finish(i, m, a, jnp.sum(acc[0], axis=0, keepdims=True), acc[1])
+
+
+def kernel(q_hbm, k_hbm, v_hbm, ob, qt, kv2, bias2, oacc, ml, raw, wide, kv1, vt, sref, bias0, bias1,
            lsem, qsem, ssem, rsem):
     cx, cy, cz = lax.axis_index("cx"), lax.axis_index("cy"), lax.axis_index("cz")
     me = (cx * 2 + cy) * 2 + cz
@@ -116,7 +125,7 @@
         x.start()
 
     def qload(h):
-        return pltpu.make_async_copy(q_hbm.at[:, pl.ds(pl.multiple_of(h * G, G), G), :], qb.at[h], qsem.at[h])
+        return pltpu.make_async_copy(q_hbm.at[:, pl.ds(pl.multiple_of(h * G, G), G), :], qt.at[h], qsem.at[h])
 
     def rdma(kind, h):
         src, dst, dev = (
@@ -176,31 +185,48 @@
         rdma(6, h).wait_recv()
         rdma(7, h).start()
 
-    @pl.loop(0, HKV)
-    def _(h):
-        qload(h).wait()
-        rdma(2, h).wait_recv()
-        attend(h, kv1, 0, 2, bias0, qb, oacc, ml, vt, sref, first=True)
+    @pl.loop(0, HKV // U0)
+    def _(g):
+        heads = [g * U0 + u for u in range(U0)]
+
+        def arrive(u):
+            h = heads[u]
+            qload(h).wait()
+            rdma(2, h).wait_recv()
+
+        attend(heads, kv1, 0, 2, bias0, qt, oacc, ml, vt, sref, arrive, first=True)
 
     pass_on(0)
 
-    @pl.loop(0, HKV)
-    def _(h):
-        @pl.when(h < HKV - 1)
-        def _():
-            pass_on(h + 1)
-
-        for kind in (3, 4):
-            rdma(kind, h).wait_recv()
-        attend(h, kv1, 2, 4, bias1, qb, oacc, ml, vt, sref)
+    @pl.loop(0, HKV // U1)
+    def _(g):
+        heads = [g * U1 + u for u in range(U1)]
+
+        def arrive(u):
+            h = heads[u]
+            if u < U1 - 1:
+                pass_on(h + 1)
+            else:
+                @pl.when(h < HKV - 1)
+                def _():
+                    pass_on(h + 1)
+
+            rdma(3, h).wait_recv()
+            rdma(4, h).wait_recv()
+
+        attend(heads, kv1, 2, 4, bias1, qt, oacc, ml, vt, sref, arrive)
 
     pass_on2(0)
 
-    @pl.loop(0, HKV - 1)
-    def _(h):
-        pass_on2(h + 1)
-        rdma(7, h).wait_recv()
-        attend(h, kv2, 0, 2, bias2, qb, oacc, ml, vt, sref, out=ob.at[h])
+    @pl.loop(0, (HKV - 1) // U2)
+    def _(g):
+        heads = [g * U2 + u for u in range(U2)]
+
+        def arrive(u):
+            pass_on2(heads[u] + 1)
+            rdma(7, heads[u]).wait_recv()
+
+        attend(heads, kv2, 0, 2, bias2, qt, oacc, ml, vt, sref, arrive, out=lambda u: ob.at[heads[u]])
 
     rdma(7, HKV - 1).wait_recv()
 
@@ -210,12 +236,12 @@
             rdma(kind, h).wait_send()
 
 
-def spread(ob, qb, kv2, bias2, oacc, ml, o_hbm, last, vt, sref, sem):
+def spread(ob, qt, kv2, bias2, oacc, ml, o_hbm, last, vt, sref, sem):
     copies = [pltpu.make_async_copy(ob.at[h] if h < HKV - 1 else last, o_hbm.at[:, h * G:(h + 1) * G, :], sem.at[h])
               for h in range(HKV)]
     for x in copies[:-1]:
         x.start()
-    attend(HKV - 1, kv2, 0, 2, bias2, qb, oacc, ml, vt, sref, out=last)
+    attend([HKV - 1], kv2, 0, 2, bias2, qt, oacc, ml, vt, sref, out=lambda u: last)
     copies[-1].start()
     for x in copies:
         x.wait()
@@ -243,8 +269,8 @@
                 pltpu.VMEM((2, T, HKV, D), BF),
                 pltpu.VMEM((2, T * HKV, D), F32),
                 pltpu.VMEM((HKV, S1, 2, T, D), BF),
-                pltpu.VMEM((D, 4 * T), BF),
-                pltpu.VMEM((2, 4 * T, QB), F32),
+                pltpu.VMEM((max(U0, U1, U2), D, 4 * T), BF),
+                pltpu.VMEM((AHEAD + 1, 4 * T, QB), F32),
                 pltpu.VMEM((2 * SUB, QB), F32),
                 pltpu.VMEM((4 * SUB, QB), F32),
                 pltpu.SemaphoreType.DMA((2,)),
@@ -262,8 +288,8 @@
             out_specs=hbm,
             scratch_shapes=[
                 pltpu.VMEM((T, G, D), BF),
-                pltpu.VMEM((D, S2 * T), BF),
-                pltpu.VMEM((2, S2 * T, QB), F32),
+                pltpu.VMEM((1, D, S2 * T), BF),
+                pltpu.VMEM((AHEAD + 1, S2 * T, QB), F32),
                 pltpu.SemaphoreType.DMA((HKV,)),
             ],
             compiler_params=pltpu.CompilerParams(vmem_limit_bytes=8 << 20),

time: 46.3 us -> 44.9 us (0.970)
  Pallas kernels: 46.2 us -> 44.8 us
    pallas_call x1, Pallas kernels: 43.6 us -> 41.8 us  [local(): pl.pallas_call(kernel, out_shape=[pltpu.VMEM((HKV - 1, T, G, D), BF), plt...]
where the time goes in v7:
time: 44.9 us; the launch traced here: 44.8 us
  Pallas kernels  44.8 us (100%)
    pallas_call x1, Pallas kernels, local(): pl.pallas_call(kernel, out_shape=[pltpu.VMEM((HKV - 1, T, G, D), BF), plt...  41.8 us
    pallas_call x1, Pallas kernels, local(): pl.pallas_call(spread, out_shape=jax.ShapeDtypeStruct(q.shape, q.dtype),...  2.96 us

profile of v7, /device:TPU:0, one launch (start us, length us, event | category | flops | bytes accessed | tf_op | source)
XLA Modules:
  0.0 44.8 jit_solution(11359134554569344007)
XLA Ops:
  0.0 41.8 %shard_map.37 = (bf16[7,256,8,128]{3,2,1,0:T(8,128)(2,1)S(1)}, bf16[8,256,8,128]{3,2,1,0:T(8,128)(2,1)S(1)}, bf16[8,2,2,256,128]{4,3,2,1,0:T(8,128)(2,1)S(1)}, f...) custom-call(bf16[256,64,128]{2,1,0:T(8,128)(2,1)} %q_hbm.1, ...), custom_call_target="tpu_custom_call" | custom-call | tf_op jit(solution)/shard_map/pallas_call | solution.py:256
  41.8 3.0 %shard_map.38 = bf16[256,64,128]{2,1,0:T(8,128)(2,1)} custom-call(bf16[7,256,8,128]{3,2,1,0:T(8,128)(2,1)S(1)} %get-tuple-element.11.ob, bf16[8,256,8,128]{3,2,1,0:T(8,128)(2,1)S(1)} %get-tuple-element.12.qt, bf16[8,2,2,256,128]{4,3,2,1,0:T(8,128)(2,1)S(1)} %get-tuple-element.13.kv2, f32[64,256]{1,0:T(8,128)S(1)} %get-tuple-element.14.bias2, ...), custom_call_target="tpu_custom_call" | custom-call | tf_op jit(solution)/shard_map/pallas_call | solution.py:284

commit v8 on v7

--- a/solution.py
+++ b/solution.py
@@ -16,8 +16,8 @@
 S2 = 2
 C = (D ** -0.5) * 1.4426950408889634
 ORDER = (0, 2, 4, 6, 7, 5, 3, 1)
-AHEAD = 3
-U0, U1, U2 = 2,2,1
+AHEAD = 4
+U0, U1, U2 = 1, 1, 1
 BF = jnp.bfloat16
 F32 = jnp.float32
 NT = (((1,), (1,)), ((), ()))
@@ -237,14 +237,21 @@
 
 
 def spread(ob, qt, kv2, bias2, oacc, ml, o_hbm, last, vt, sref, sem):
-    copies = [pltpu.make_async_copy(ob.at[h] if h < HKV - 1 else last, o_hbm.at[:, h * G:(h + 1) * G, :], sem.at[h])
-              for h in range(HKV)]
-    for x in copies[:-1]:
-        x.start()
+    def put(src, h):
+        return pltpu.make_async_copy(src, o_hbm.at[:, pl.ds(pl.multiple_of(h * G, G), G), :], sem.at[h])
+
+    @pl.loop(0, HKV - 1)
+    def _(h):
+        put(ob.at[h], h).start()
+
     attend([HKV - 1], kv2, 0, 2, bias2, qt, oacc, ml, vt, sref, out=lambda u: last)
-    copies[-1].start()
-    for x in copies:
-        x.wait()
+    put(last, HKV - 1).start()
+
+    @pl.loop(0, HKV - 1)
+    def _(h):
+        put(ob.at[h], h).wait()
+
+    put(last, HKV - 1).wait()
 
 
 def solution(mesh):

time: 44.9 us -> 44 us (0.980)
  Pallas kernels: 44.8 us -> 43.9 us
    pallas_call x1, Pallas kernels: 2.96 us -> 2.07 us  [local(): pl.pallas_call(spread, out_shape=jax.ShapeDtypeStruct(q.shape, q.dtype),...]
where the time goes in v8:
time: 44 us; the launch traced here: 43.9 us
  Pallas kernels  43.9 us (100%)
    pallas_call x1, Pallas kernels, local(): pl.pallas_call(kernel, out_shape=[pltpu.VMEM((HKV - 1, T, G, D), BF), plt...  41.8 us
    pallas_call x1, Pallas kernels, local(): pl.pallas_call(spread, out_shape=jax.ShapeDtypeStruct(q.shape, q.dtype),...  2.07 us

profile of v8, /device:TPU:0, one launch (start us, length us, event | category | flops | bytes accessed | tf_op | source)
XLA Modules:
  0.0 43.9 jit_solution(2896686752203281935)
XLA Ops:
  0.0 41.8 %shard_map.37 = (bf16[7,256,8,128]{3,2,1,0:T(8,128)(2,1)S(1)}, bf16[8,256,8,128]{3,2,1,0:T(8,128)(2,1)S(1)}, bf16[8,2,2,256,128]{4,3,2,1,0:T(8,128)(2,1)S(1)}, f...) custom-call(bf16[256,64,128]{2,1,0:T(8,128)(2,1)} %q_hbm.1, ...), custom_call_target="tpu_custom_call" | custom-call | tf_op jit(solution)/shard_map/pallas_call | solution.py:263
  41.8 2.1 %shard_map.38 = bf16[256,64,128]{2,1,0:T(8,128)(2,1)} custom-call(bf16[7,256,8,128]{3,2,1,0:T(8,128)(2,1)S(1)} %get-tuple-element.11.ob, bf16[8,256,8,128]{3,2,1,0:T(8,128)(2,1)S(1)} %get-tuple-element.12.qt, bf16[8,2,2,256,128]{4,3,2,1,0:T(8,128)(2,1)S(1)} %get-tuple-element.13.kv2, f32[64,256]{1,0:T(8,128)S(1)} %get-tuple-element.14.bias2, ...), custom_call_target="tpu_custom_call" | custom-call | tf_op jit(solution)/shard_map/pallas_call | solution.py:291

commit v9 on v8

--- a/solution.py
+++ b/solution.py
@@ -27,15 +27,15 @@
     return [(r, min(r + 256, n)) for r in range(0, n, 256)]
 
 
-def by_tile(kv, h, s0, ns):
-    return jnp.concatenate([kv[h, s, 1, t * SUB:(t + 1) * SUB] for t in range(NB) for s in range(s0, s0 + ns)], axis=0)
+def by_tile(piece, kind, ns):
+    return jnp.concatenate([piece(kind, x, t) for t in range(NB) for x in range(ns)], axis=0)
 
 
 def fold(f, x):
     return f(x.reshape(-1, 8, x.shape[-1]), axis=0)
 
 
-def attend(heads, kv, s0, ns, bias, qt, oacc, ml, vt, sref, arrive=None, first=False, out=None):
+def attend(heads, piece_of, ns, bias, qt, oacc, ml, vt, sref, arrive=None, first=False, out=None):
     rows = ns * SUB
     items = [(u, j) for u in range(len(heads)) for j in ORDER]
     tops = {}
@@ -47,8 +47,8 @@
         if j == ORDER[0] and r0 == 0:
             if arrive:
                 arrive(u)
-            vt[u, :, :ns * T] = by_tile(kv, h, s0, ns).T
-        parts = [kv[h, s0 + x % ns, 0, x // ns * SUB:(x // ns + 1) * SUB] for x in range(r0 // SUB, r1 // SUB)]
+            vt[u, :, :ns * T] = by_tile(piece_of(h), 1, ns).T
+        parts = [piece_of(h)(0, x % ns, x // ns) for x in range(r0 // SUB, r1 // SUB)]
         s = lax.dot_general(jnp.concatenate(parts, axis=0), qt[h, j * SUB:(j + 1) * SUB].reshape(QB, D), NT,
                             preferred_element_type=F32)
         lo = max(r0, j * rows)
@@ -108,16 +108,32 @@
         finish(i, m, a, jnp.sum(acc[0], axis=0, keepdims=True), acc[1])
 
 
+def near(kv1, chip):
+    def of(h):
+        return lambda kind, x, t: kv1[h, kind, chip + x // 2, x % 2, t * SUB:(t + 1) * SUB]
+    return of
+
+
+def far(kv2):
+    def of(h):
+        return lambda kind, x, t: kv2[h, kind, x, t * SUB:(t + 1) * SUB]
+    return of
+
+
 def kernel(q_hbm, k_hbm, v_hbm, ob, qt, kv2, bias2, oacc, ml, raw, wide, kv1, vt, sref, bias0, bias1,
            lsem, qsem, ssem, rsem):
     cx, cy, cz = lax.axis_index("cx"), lax.axis_index("cy"), lax.axis_index("cz")
     me = (cx * 2 + cy) * 2 + cz
-    nx = {"cy": 1 - cy}
-    ny = {"cx": 1 - cx}
+    chip = cx * 2 + cy
+    mine = 1 - cz
+
+    def over(core):
+        return {"cx": cx + cz - 2 * cx * cz, "cy": cy + mine - 2 * cy * mine, "cz": core}
+
     sib = {"cz": 1 - cz}
 
     barrier = pltpu.get_barrier_semaphore()
-    for dev in (nx, ny, sib):
+    for dev in ({"cx": cx, "cy": 1 - cy, "cz": 0}, {"cx": 1 - cx, "cy": cy, "cz": 1}, sib):
         pl.semaphore_signal(barrier, inc=1, device_id=dev, device_id_type=pl.DeviceIdType.MESH)
 
     loads = [pltpu.make_async_copy(x, raw.at[i], lsem.at[i]) for i, x in enumerate((k_hbm, v_hbm))]
@@ -127,24 +143,42 @@
     def qload(h):
         return pltpu.make_async_copy(q_hbm.at[:, pl.ds(pl.multiple_of(h * G, G), G), :], qt.at[h], qsem.at[h])
 
-    def rdma(kind, h):
-        src, dst, dev = (
-            (kv1.at[h, 0], kv1.at[h, 2], nx),
-            (kv1.at[h, 0], kv1.at[h, 4], ny),
-            (kv1.at[h, 0], kv1.at[h, 1], sib),
-            (kv1.at[h, 2], kv1.at[h, 3], sib),
-            (kv1.at[h, 4], kv1.at[h, 5], sib),
-            (kv1.at[h, 2, 0], kv2.at[h, 0, 0], ny),
-            (kv1.at[h, 4, 1], kv2.at[h, 0, 1], nx),
-            (kv2.at[h, 0], kv2.at[h, 1], sib),
-        )[kind]
-        return pltpu.make_async_remote_copy(src, dst, ssem.at[kind, h], rsem.at[kind, h], dev,
+    def rdma(src, dst, send, recv, h, dev):
+        return pltpu.make_async_remote_copy(src, dst, ssem.at[send, h], rsem.at[recv, h], dev,
                                             pl.DeviceIdType.MESH)
 
-    def mask(nslot, base, ref):
+    def swap(h):
+        return rdma(kv1.at[h, :, 0, cz], kv1.at[h, :, 0, cz], 0, 5, h, sib)
+
+    def out_k(h):
+        return rdma(kv1.at[h, 0, 0], kv1.at[h, 0, 1 + cz], 1, cz, h, over(1))
+
+    def out_v(h):
+        return rdma(kv1.at[h, 1, 0], kv1.at[h, 1, 1 + cz], 2, cz, h, over(0))
+
+    def half_k(z):
+        return rdma(kv1.at[0, 0, 0, z], kv1.at[0, 0, 1 + cz, z], 1, cz, 0, over(1))
+
+    def half_v(z):
+        return rdma(kv1.at[0, 1, 0, z], kv1.at[0, 1, 1 + cz, z], 2, cz, 0, over(0))
+
+    def relay(h):
+        return rdma(kv1.at[h, mine, 1:3], kv1.at[h, mine, 1:3], 3, 2, h, sib)
+
+    def forward(h):
+        return rdma(kv1.at[h, mine, 2 - cz], kv2.at[h, mine], 4, 3, h, over(cz))
+
+    def relay2(h):
+        return rdma(kv2.at[h, mine], kv2.at[h, mine], 5, 4, h, sib)
+
+    def arrived(dst, recv, h):
+        rdma(dst, dst, 0, recv, h, sib).wait_recv()
+
+    def mask(nslot, far_chip, ref):
         r = lax.broadcasted_iota(jnp.int32, (nslot * SUB, QB), 0)
         c = lax.broadcasted_iota(jnp.int32, (nslot * SUB, QB), 1)
-        kpos = (r % SUB) * 8 + (me ^ (r // SUB + base))
+        x = r // SUB
+        kpos = (r % SUB) * 8 + (chip ^ (x // 2 + far_chip)) * 2 + x % 2
         qpos = (c // G) * 8 + me
         ref[...] = jnp.where(kpos <= qpos, 0.0, -1e30)
 
@@ -152,38 +186,45 @@
         loads[i].wait()
         wide[i] = raw[i].astype(F32).reshape(T * HKV, D)
 
-    def send(h):
-        for kind in range(3):
-            rdma(kind, h).start()
-
     for h in range(HKV):
         for i in range(2):
-            kv1[h, 0, i] = wide[i, pl.ds(h, T, stride=HKV), :].astype(BF)
+            kv1[h, i, 0, cz] = wide[i, pl.ds(h, T, stride=HKV), :].astype(BF)
         if h == 1:
             pl.semaphore_wait(barrier, 3)
+            half_k(cz).start()
+            half_v(cz).start()
         if h:
-            send(h - 1)
+            swap(h - 1).start()
 
     mask(2, 0, bias0)
-    send(HKV - 1)
+    swap(HKV - 1).start()
+
+    arrived(kv1.at[0, :, 0, cz], 5, 0)
+    half_k(1 - cz).start()
+    half_v(1 - cz).start()
+
+    @pl.loop(1, HKV)
+    def _(h):
+        arrived(kv1.at[h, :, 0, cz], 5, h)
+        out_k(h).start()
+        out_v(h).start()
 
     @pl.loop(0, HKV)
     def _(h):
         qload(h).start()
 
-    mask(4, 2, bias1)
-    mask(2, 6, bias2)
+    mask(4, 1, bias1)
+    mask(2, 3, bias2)
 
     def pass_on(h):
-        rdma(0, h).wait_recv()
-        rdma(1, h).wait_recv()
-        for kind in (3, 4, 5, 6):
-            rdma(kind, h).start()
+        arrived(kv1.at[h, mine, 1], 0, h)
+        arrived(kv1.at[h, mine, 2], 1, h)
+        relay(h).start()
+        forward(h).start()
 
     def pass_on2(h):
-        rdma(5, h).wait_recv()
-        rdma(6, h).wait_recv()
-        rdma(7, h).start()
+        arrived(kv2.at[h, mine], 3, h)
+        relay2(h).start()
 
     @pl.loop(0, HKV // U0)
     def _(g):
@@ -192,9 +233,8 @@
         def arrive(u):
             h = heads[u]
             qload(h).wait()
-            rdma(2, h).wait_recv()
-
-        attend(heads, kv1, 0, 2, bias0, qt, oacc, ml, vt, sref, arrive, first=True)
+
+        attend(heads, near(kv1, 0), 2, bias0, qt, oacc, ml, vt, sref, arrive, first=True)
 
     pass_on(0)
 
@@ -211,10 +251,9 @@
                 def _():
                     pass_on(h + 1)
 
-            rdma(3, h).wait_recv()
-            rdma(4, h).wait_recv()
-
-        attend(heads, kv1, 2, 4, bias1, qt, oacc, ml, vt, sref, arrive)
+            arrived(kv1.at[h, cz, 1:3], 2, h)
+
+        attend(heads, near(kv1, 1), 4, bias1, qt, oacc, ml, vt, sref, arrive)
 
     pass_on2(0)
 
@@ -224,16 +263,16 @@
 
         def arrive(u):
             pass_on2(heads[u] + 1)
-            rdma(7, heads[u]).wait_recv()
-
-        attend(heads, kv2, 0, 2, bias2, qt, oacc, ml, vt, sref, arrive, out=lambda u: ob.at[heads[u]])
-
-    rdma(7, HKV - 1).wait_recv()
+            arrived(kv2.at[heads[u], cz], 4, heads[u])
+
+        attend(heads, far(kv2), 2, bias2, qt, oacc, ml, vt, sref, arrive, out=lambda u: ob.at[heads[u]])
+
+    arrived(kv2.at[HKV - 1, cz], 4, HKV - 1)
 
     @pl.loop(0, HKV)
     def _(h):
-        for kind in range(8):
-            rdma(kind, h).wait_send()
+        for sent in (swap, out_k, out_v, relay, forward, relay2):
+            sent(h).wait_send()
 
 
 def spread(ob, qt, kv2, bias2, oacc, ml, o_hbm, last, vt, sref, sem):
@@ -244,7 +283,7 @@
     def _(h):
         put(ob.at[h], h).start()
 
-    attend([HKV - 1], kv2, 0, 2, bias2, qt, oacc, ml, vt, sref, out=lambda u: last)
+    attend([HKV - 1], far(kv2), 2, bias2, qt, oacc, ml, vt, sref, out=lambda u: last)
     put(last, HKV - 1).start()
 
     @pl.loop(0, HKV - 1)
@@ -265,7 +304,7 @@
             out_shape=[
                 pltpu.VMEM((HKV - 1, T, G, D), BF),
                 pltpu.VMEM((HKV, T, G, D), BF),
-                pltpu.VMEM((HKV, S2, 2, T, D), BF),
+                pltpu.VMEM((HKV, 2, 2, T, D), BF),
                 pltpu.VMEM((S2 * SUB, QB), F32),
                 pltpu.VMEM((HKV, NB, D, QB), F32),
                 pltpu.VMEM((HKV, NB, 8, QB), F32),
@@ -275,15 +314,15 @@
             scratch_shapes=[
                 pltpu.VMEM((2, T, HKV, D), BF),
                 pltpu.VMEM((2, T * HKV, D), F32),
-                pltpu.VMEM((HKV, S1, 2, T, D), BF),
+                pltpu.VMEM((HKV, 2, 3, 2, T, D), BF),
                 pltpu.VMEM((max(U0, U1, U2), D, 4 * T), BF),
                 pltpu.VMEM((AHEAD + 1, 4 * T, QB), F32),
                 pltpu.VMEM((2 * SUB, QB), F32),
                 pltpu.VMEM((4 * SUB, QB), F32),
                 pltpu.SemaphoreType.DMA((2,)),
                 pltpu.SemaphoreType.DMA((HKV,)),
-                pltpu.SemaphoreType.DMA((8, HKV)),
-                pltpu.SemaphoreType.DMA((8, HKV)),
+                pltpu.SemaphoreType.DMA((6, HKV)),
+                pltpu.SemaphoreType.DMA((6, HKV)),
             ],
             compiler_params=pltpu.CompilerParams(
                 vmem_limit_bytes=36 << 20, collective_id=0, has_side_effects=True),

time: 44 us -> 44.2 us (level)
  no operation moved by 1% of the time
where the time goes in v9:
time: 44.2 us; the launch traced here: 44.1 us
  Pallas kernels  44.1 us (100%)
    pallas_call x1, Pallas kernels, local(): pl.pallas_call(kernel, out_shape=[pltpu.VMEM((HKV - 1, T, G, D), BF), plt...  42 us
    pallas_call x1, Pallas kernels, local(): pl.pallas_call(spread, out_shape=jax.ShapeDtypeStruct(q.shape, q.dtype),...  2.07 us

profile of v9, /device:TPU:0, one launch (start us, length us, event | category | flops | bytes accessed | tf_op | source)
XLA Modules:
  0.0 44.1 jit_solution(14294960482873013569)
XLA Ops:
  0.0 42.0 %shard_map.37 = (bf16[7,256,8,128]{3,2,1,0:T(8,128)(2,1)S(1)}, bf16[8,256,8,128]{3,2,1,0:T(8,128)(2,1)S(1)}, bf16[8,2,2,256,128]{4,3,2,1,0:T(8,128)(2,1)S(1)}, f...) custom-call(bf16[256,64,128]{2,1,0:T(8,128)(2,1)} %q_hbm.1, ...), custom_call_target="tpu_custom_call" | custom-call | tf_op jit(solution)/shard_map/pallas_call | solution.py:302
  42.0 2.1 %shard_map.38 = bf16[256,64,128]{2,1,0:T(8,128)(2,1)} custom-call(bf16[7,256,8,128]{3,2,1,0:T(8,128)(2,1)S(1)} %get-tuple-element.11.ob, bf16[8,256,8,128]{3,2,1,0:T(8,128)(2,1)S(1)} %get-tuple-element.12.qt, bf16[8,2,2,256,128]{4,3,2,1,0:T(8,128)(2,1)S(1)} %get-tuple-element.13.kv2, f32[64,256]{1,0:T(8,128)S(1)} %get-tuple-element.14.bias2, ...), custom_call_target="tpu_custom_call" | custom-call | tf_op jit(solution)/shard_map/pallas_call | solution.py:330

commit v10 on v8

--- a/solution.py
+++ b/solution.py
@@ -6,6 +6,7 @@
 from jax.sharding import PartitionSpec as P
 
 T = 256
+CUT = 160
 HKV = 8
 G = 8
 D = 128
@@ -109,7 +110,7 @@
 
 
 def kernel(q_hbm, k_hbm, v_hbm, ob, qt, kv2, bias2, oacc, ml, raw, wide, kv1, vt, sref, bias0, bias1,
-           lsem, qsem, ssem, rsem):
+           lsem, qsem, ssem, rsem, lssem, lrsem):
     cx, cy, cz = lax.axis_index("cx"), lax.axis_index("cy"), lax.axis_index("cz")
     me = (cx * 2 + cy) * 2 + cz
     nx = {"cy": 1 - cy}
@@ -127,7 +128,7 @@
     def qload(h):
         return pltpu.make_async_copy(q_hbm.at[:, pl.ds(pl.multiple_of(h * G, G), G), :], qt.at[h], qsem.at[h])
 
-    def rdma(kind, h):
+    def rdma(kind, h, i=None):
         src, dst, dev = (
             (kv1.at[h, 0], kv1.at[h, 2], nx),
             (kv1.at[h, 0], kv1.at[h, 4], ny),
@@ -138,8 +139,23 @@
             (kv1.at[h, 4, 1], kv2.at[h, 0, 1], nx),
             (kv2.at[h, 0], kv2.at[h, 1], sib),
         )[kind]
+        if i is not None:
+            src, dst = src.at[i], dst.at[i]
         return pltpu.make_async_remote_copy(src, dst, ssem.at[kind, h], rsem.at[kind, h], dev,
                                             pl.DeviceIdType.MESH)
+
+    def last(i, part):
+        rows = pl.ds(0, CUT) if part == 0 else pl.ds(CUT, T - CUT)
+        src = kv1.at[HKV - 1, (2, 4)[i], i, rows]
+        dst = kv2.at[HKV - 1, 1 if part == 2 else 0, i, rows]
+        dev = (ny, nx)[i] if part < 2 else ((ny, nx)[i] | sib)
+        return pltpu.make_async_remote_copy(src, dst, lssem.at[i, part], lrsem.at[i, part], dev,
+                                            pl.DeviceIdType.MESH)
+
+    def last_relay():
+        rows = pl.ds(0, CUT)
+        return pltpu.make_async_remote_copy(kv2.at[HKV - 1, 0, :, rows], kv2.at[HKV - 1, 1, :, rows],
+                                            ssem.at[7, HKV - 1], rsem.at[7, HKV - 1], sib, pl.DeviceIdType.MESH)
 
     def mask(nslot, base, ref):
         r = lax.broadcasted_iota(jnp.int32, (nslot * SUB, QB), 0)
@@ -148,21 +164,27 @@
         qpos = (c // G) * 8 + me
         ref[...] = jnp.where(kpos <= qpos, 0.0, -1e30)
 
+    def relaid(h, i):
+        kv1[h, 0, i] = wide[i, pl.ds(h, T, stride=HKV), :].astype(BF)
+
+    def send(h):
+        for kind in range(3):
+            rdma(kind, h).start()
+
     for i in range(2):
         loads[i].wait()
         wide[i] = raw[i].astype(F32).reshape(T * HKV, D)
-
-    def send(h):
+        relaid(0, i)
+        relaid(1, i)
+        if i == 0:
+            pl.semaphore_wait(barrier, 3)
         for kind in range(3):
-            rdma(kind, h).start()
-
-    for h in range(HKV):
+            rdma(kind, 0, i).start()
+
+    for h in range(2, HKV):
         for i in range(2):
-            kv1[h, 0, i] = wide[i, pl.ds(h, T, stride=HKV), :].astype(BF)
-        if h == 1:
-            pl.semaphore_wait(barrier, 3)
-        if h:
-            send(h - 1)
+            relaid(h, i)
+        send(h - 1)
 
     mask(2, 0, bias0)
     send(HKV - 1)
@@ -177,13 +199,32 @@
     def pass_on(h):
         rdma(0, h).wait_recv()
         rdma(1, h).wait_recv()
-        for kind in (3, 4, 5, 6):
+        for kind in (3, 4):
             rdma(kind, h).start()
 
+        @pl.when(h < HKV - 1)
+        def _():
+            for kind in (5, 6):
+                rdma(kind, h).start()
+
+        @pl.when(h == HKV - 1)
+        def _():
+            for part in range(3):
+                for i in range(2):
+                    last(i, part).start()
+
     def pass_on2(h):
-        rdma(5, h).wait_recv()
-        rdma(6, h).wait_recv()
-        rdma(7, h).start()
+        @pl.when(h < HKV - 1)
+        def _():
+            rdma(5, h).wait_recv()
+            rdma(6, h).wait_recv()
+            rdma(7, h).start()
+
+        @pl.when(h == HKV - 1)
+        def _():
+            for i in range(2):
+                last(i, 0).wait_recv()
+            last_relay().start()
 
     @pl.loop(0, HKV // U0)
     def _(g):
@@ -196,7 +237,7 @@
 
         attend(heads, kv1, 0, 2, bias0, qt, oacc, ml, vt, sref, arrive, first=True)
 
-    pass_on(0)
+    pass_on(jnp.int32(0))
 
     @pl.loop(0, HKV // U1)
     def _(g):
@@ -216,7 +257,7 @@
 
         attend(heads, kv1, 2, 4, bias1, qt, oacc, ml, vt, sref, arrive)
 
-    pass_on2(0)
+    pass_on2(jnp.int32(0))
 
     @pl.loop(0, (HKV - 1) // U2)
     def _(g):
@@ -228,12 +269,25 @@
 
         attend(heads, kv2, 0, 2, bias2, qt, oacc, ml, vt, sref, arrive, out=lambda u: ob.at[heads[u]])
 
-    rdma(7, HKV - 1).wait_recv()
+    for part in (1, 2):
+        for i in range(2):
+            last(i, part).wait_recv()
+    last_relay().wait_recv()
 
     @pl.loop(0, HKV)
     def _(h):
-        for kind in range(8):
+        for kind in range(5):
             rdma(kind, h).wait_send()
+
+    @pl.loop(0, HKV - 1)
+    def _(h):
+        for kind in range(5, 8):
+            rdma(kind, h).wait_send()
+
+    for part in range(3):
+        for i in range(2):
+            last(i, part).wait_send()
+    last_relay().wait_send()
 
 
 def spread(ob, qt, kv2, bias2, oacc, ml, o_hbm, last, vt, sref, sem):
@@ -284,6 +338,8 @@
                 pltpu.SemaphoreType.DMA((HKV,)),
                 pltpu.SemaphoreType.DMA((8, HKV)),
                 pltpu.SemaphoreType.DMA((8, HKV)),
+                pltpu.SemaphoreType.DMA((2, 3)),
+                pltpu.SemaphoreType.DMA((2, 3)),
             ],
             compiler_params=pltpu.CompilerParams(
                 vmem_limit_bytes=36 << 20, collective_id=0, has_side_effects=True),

time: 44 us -> 44.2 us (level)
  no operation moved by 1% of the time
where the time goes in v10:
time: 44.2 us; the launch traced here: 44.1 us
  Pallas kernels  44.1 us (100%)
    pallas_call x1, Pallas kernels, local(): pl.pallas_call(kernel, out_shape=[pltpu.VMEM((HKV - 1, T, G, D), BF), plt...  42 us
    pallas_call x1, Pallas kernels, local(): pl.pallas_call(spread, out_shape=jax.ShapeDtypeStruct(q.shape, q.dtype),...  2.07 us

profile of v10, /device:TPU:0, one launch (start us, length us, event | category | flops | bytes accessed | tf_op | source)
XLA Modules:
  0.0 44.1 jit_solution(15771961561487961941)
XLA Ops:
  0.0 42.0 %shard_map.37 = (bf16[7,256,8,128]{3,2,1,0:T(8,128)(2,1)S(1)}, bf16[8,256,8,128]{3,2,1,0:T(8,128)(2,1)S(1)}, bf16[8,2,2,256,128]{4,3,2,1,0:T(8,128)(2,1)S(1)}, f...) custom-call(bf16[256,64,128]{2,1,0:T(8,128)(2,1)} %q_hbm.1, ...), custom_call_target="tpu_custom_call" | custom-call | tf_op jit(solution)/shard_map/pallas_call | solution.py:317
  42.1 2.1 %shard_map.38 = bf16[256,64,128]{2,1,0:T(8,128)(2,1)} custom-call(bf16[7,256,8,128]{3,2,1,0:T(8,128)(2,1)S(1)} %get-tuple-element.11.ob, bf16[8,256,8,128]{3,2,1,0:T(8,128)(2,1)S(1)} %get-tuple-element.12.qt, bf16[8,2,2,256,128]{4,3,2,1,0:T(8,128)(2,1)S(1)} %get-tuple-element.13.kv2, f32[64,256]{1,0:T(8,128)S(1)} %get-tuple-element.14.bias2, ...), custom_call_target="tpu_custom_call" | custom-call | tf_op jit(solution)/shard_map/pallas_call | solution.py:347

commit v11 on v8

--- a/solution.py
+++ b/solution.py
@@ -17,7 +17,7 @@
 C = (D ** -0.5) * 1.4426950408889634
 ORDER = (0, 2, 4, 6, 7, 5, 3, 1)
 AHEAD = 4
-U0, U1, U2 = 1, 1, 1
+U0, U1, U2 = 2, 2, 1
 BF = jnp.bfloat16
 F32 = jnp.float32
 NT = (((1,), (1,)), ((), ()))
@@ -128,10 +128,11 @@
         return pltpu.make_async_copy(q_hbm.at[:, pl.ds(pl.multiple_of(h * G, G), G), :], qt.at[h], qsem.at[h])
 
     def rdma(kind, h):
+        two = pl.ds(h if kind < 3 else 0, 2)
         src, dst, dev = (
-            (kv1.at[h, 0], kv1.at[h, 2], nx),
-            (kv1.at[h, 0], kv1.at[h, 4], ny),
-            (kv1.at[h, 0], kv1.at[h, 1], sib),
+            (kv1.at[two, 0], kv1.at[two, 2], nx),
+            (kv1.at[two, 0], kv1.at[two, 4], ny),
+            (kv1.at[two, 0], kv1.at[two, 1], sib),
             (kv1.at[h, 2], kv1.at[h, 3], sib),
             (kv1.at[h, 4], kv1.at[h, 5], sib),
             (kv1.at[h, 2, 0], kv2.at[h, 0, 0], ny),
@@ -159,13 +160,13 @@
     for h in range(HKV):
         for i in range(2):
             kv1[h, 0, i] = wide[i, pl.ds(h, T, stride=HKV), :].astype(BF)
-        if h == 1:
+        if h == 2:
             pl.semaphore_wait(barrier, 3)
-        if h:
-            send(h - 1)
+        if h and h % 2 == 0:
+            send(h - 2)
 
     mask(2, 0, bias0)
-    send(HKV - 1)
+    send(HKV - 2)
 
     @pl.loop(0, HKV)
     def _(h):
@@ -177,8 +178,9 @@
     def pass_on(h):
         rdma(0, h).wait_recv()
         rdma(1, h).wait_recv()
-        for kind in (3, 4, 5, 6):
-            rdma(kind, h).start()
+        for u in range(2):
+            for kind in (3, 4, 5, 6):
+                rdma(kind, h + u).start()
 
     def pass_on2(h):
         rdma(5, h).wait_recv()
@@ -192,7 +194,8 @@
         def arrive(u):
             h = heads[u]
             qload(h).wait()
-            rdma(2, h).wait_recv()
+            if u == 0:
+                rdma(2, h).wait_recv()
 
         attend(heads, kv1, 0, 2, bias0, qt, oacc, ml, vt, sref, arrive, first=True)
 
@@ -204,9 +207,7 @@
 
         def arrive(u):
             h = heads[u]
-            if u < U1 - 1:
-                pass_on(h + 1)
-            else:
+            if u == 1:
                 @pl.when(h < HKV - 1)
                 def _():
                     pass_on(h + 1)
@@ -230,9 +231,14 @@
 
     rdma(7, HKV - 1).wait_recv()
 
+    @pl.loop(0, HKV // 2)
+    def _(g):
+        for kind in range(3):
+            rdma(kind, 2 * g).wait_send()
+
     @pl.loop(0, HKV)
     def _(h):
-        for kind in range(8):
+        for kind in range(3, 8):
             rdma(kind, h).wait_send()
 
 

time: 44 us -> 45.3 us (1.030)
  Pallas kernels: 43.9 us -> 45.2 us
    pallas_call x1, Pallas kernels: 41.8 us -> 43.1 us  [local(): pl.pallas_call(kernel, out_shape=[pltpu.VMEM((HKV - 1, T, G, D), BF), plt...]
where the time goes in v11:
time: 45.3 us; the launch traced here: 45.2 us
  Pallas kernels  45.2 us (100%)
    pallas_call x1, Pallas kernels, local(): pl.pallas_call(kernel, out_shape=[pltpu.VMEM((HKV - 1, T, G, D), BF), plt...  43.1 us
    pallas_call x1, Pallas kernels, local(): pl.pallas_call(spread, out_shape=jax.ShapeDtypeStruct(q.shape, q.dtype),...  2.07 us

profile of v11, /device:TPU:0, one launch (start us, length us, event | category | flops | bytes accessed | tf_op | source)
XLA Modules:
  0.0 45.2 jit_solution(396603864096327078)
XLA Ops:
  0.0 43.1 %shard_map.37 = (bf16[7,256,8,128]{3,2,1,0:T(8,128)(2,1)S(1)}, bf16[8,256,8,128]{3,2,1,0:T(8,128)(2,1)S(1)}, bf16[8,2,2,256,128]{4,3,2,1,0:T(8,128)(2,1)S(1)}, f...) custom-call(bf16[256,64,128]{2,1,0:T(8,128)(2,1)} %q_hbm.1, ...), custom_call_target="tpu_custom_call" | custom-call | tf_op jit(solution)/shard_map/pallas_call | solution.py:269
  43.1 2.1 %shard_map.38 = bf16[256,64,128]{2,1,0:T(8,128)(2,1)} custom-call(bf16[7,256,8,128]{3,2,1,0:T(8,128)(2,1)S(1)} %get-tuple-element.11.ob, bf16[8,256,8,128]{3,2,1,0:T(8,128)(2,1)S(1)} %get-tuple-element.12.qt, bf16[8,2,2,256,128]{4,3,2,1,0:T(8,128)(2,1)S(1)} %get-tuple-element.13.kv2, f32[64,256]{1,0:T(8,128)S(1)} %get-tuple-element.14.bias2, ...), custom_call_target="tpu_custom_call" | custom-call | tf_op jit(solution)/shard_map/pallas_call | solution.py:297

commit v12 on v10

--- a/solution.py
+++ b/solution.py
@@ -18,6 +18,7 @@
 C = (D ** -0.5) * 1.4426950408889634
 ORDER = (0, 2, 4, 6, 7, 5, 3, 1)
 AHEAD = 4
+HOOK = 4
 U0, U1, U2 = 1, 1, 1
 BF = jnp.bfloat16
 F32 = jnp.float32
@@ -36,7 +37,7 @@
     return f(x.reshape(-1, 8, x.shape[-1]), axis=0)
 
 
-def attend(heads, kv, s0, ns, bias, qt, oacc, ml, vt, sref, arrive=None, first=False, out=None):
+def attend(heads, kv, s0, ns, bias, qt, oacc, ml, vt, sref, arrive=None, first=False, out=None, hook=None):
     rows = ns * SUB
     items = [(u, j) for u in range(len(heads)) for j in ORDER]
     tops = {}
@@ -90,6 +91,8 @@
         scores(*todo[at])
         at += 1
     for i, (u, j) in enumerate(items):
+        if hook and i == HOOK:
+            hook()
         top = jnp.max(tops[i], axis=0, keepdims=True)
         m, a = top, None
         if not first:
@@ -239,25 +242,16 @@
 
     pass_on(jnp.int32(0))
 
-    @pl.loop(0, HKV // U1)
-    def _(g):
-        heads = [g * U1 + u for u in range(U1)]
-
-        def arrive(u):
-            h = heads[u]
-            if u < U1 - 1:
-                pass_on(h + 1)
-            else:
-                @pl.when(h < HKV - 1)
-                def _():
-                    pass_on(h + 1)
-
-            rdma(3, h).wait_recv()
-            rdma(4, h).wait_recv()
-
-        attend(heads, kv1, 2, 4, bias1, qt, oacc, ml, vt, sref, arrive)
-
-    pass_on2(jnp.int32(0))
+    @pl.loop(0, HKV - 1)
+    def _(h):
+        pass_on(h + 1)
+        rdma(3, h).wait_recv()
+        rdma(4, h).wait_recv()
+        attend([h], kv1, 2, 4, bias1, qt, oacc, ml, vt, sref)
+
+    rdma(3, HKV - 1).wait_recv()
+    rdma(4, HKV - 1).wait_recv()
+    attend([HKV - 1], kv1, 2, 4, bias1, qt, oacc, ml, vt, sref, hook=lambda: pass_on2(jnp.int32(0)))
 
     @pl.loop(0, (HKV - 1) // U2)
     def _(g):

time: 44.2 us -> 44.2 us (level)
  no operation moved by 1% of the time
where the time goes in v12:
time: 44.2 us; the launch traced here: 44.1 us
  Pallas kernels  44.1 us (100%)
    pallas_call x1, Pallas kernels, local(): pl.pallas_call(kernel, out_shape=[pltpu.VMEM((HKV - 1, T, G, D), BF), plt...  42.1 us
    pallas_call x1, Pallas kernels, local(): pl.pallas_call(spread, out_shape=jax.ShapeDtypeStruct(q.shape, q.dtype),...  2.07 us

profile of v12, /device:TPU:0, one launch (start us, length us, event | category | flops | bytes accessed | tf_op | source)
XLA Modules:
  0.0 44.1 jit_solution(10020000549269590127)
XLA Ops:
  0.0 42.1 %shard_map.37 = (bf16[7,256,8,128]{3,2,1,0:T(8,128)(2,1)S(1)}, bf16[8,256,8,128]{3,2,1,0:T(8,128)(2,1)S(1)}, bf16[8,2,2,256,128]{4,3,2,1,0:T(8,128)(2,1)S(1)}, f...) custom-call(bf16[256,64,128]{2,1,0:T(8,128)(2,1)} %q_hbm.1, ...), custom_call_target="tpu_custom_call" | custom-call | tf_op jit(solution)/shard_map/pallas_call | solution.py:311
  42.1 2.1 %shard_map.38 = bf16[256,64,128]{2,1,0:T(8,128)(2,1)} custom-call(bf16[7,256,8,128]{3,2,1,0:T(8,128)(2,1)S(1)} %get-tuple-element.11.ob, bf16[8,256,8,128]{3,2,1,0:T(8,128)(2,1)S(1)} %get-tuple-element.12.qt, bf16[8,2,2,256,128]{4,3,2,1,0:T(8,128)(2,1)S(1)} %get-tuple-element.13.kv2, f32[64,256]{1,0:T(8,128)S(1)} %get-tuple-element.14.bias2, ...), custom_call_target="tpu_custom_call" | custom-call | tf_op jit(solution)/shard_map/pallas_call | solution.py:341

commit v13 on v9

--- a/solution.py
+++ b/solution.py
@@ -17,6 +17,7 @@
 C = (D ** -0.5) * 1.4426950408889634
 ORDER = (0, 2, 4, 6, 7, 5, 3, 1)
 AHEAD = 4
+HOOK = 4
 U0, U1, U2 = 1, 1, 1
 BF = jnp.bfloat16
 F32 = jnp.float32
@@ -35,7 +36,7 @@
     return f(x.reshape(-1, 8, x.shape[-1]), axis=0)
 
 
-def attend(heads, piece_of, ns, bias, qt, oacc, ml, vt, sref, arrive=None, first=False, out=None):
+def attend(heads, piece_of, ns, bias, qt, oacc, ml, vt, sref, arrive=None, first=False, out=None, hook=None):
     rows = ns * SUB
     items = [(u, j) for u in range(len(heads)) for j in ORDER]
     tops = {}
@@ -89,6 +90,8 @@
         scores(*todo[at])
         at += 1
     for i, (u, j) in enumerate(items):
+        if hook and i == HOOK:
+            hook()
         top = jnp.max(tops[i], axis=0, keepdims=True)
         m, a = top, None
         if not first:
@@ -121,7 +124,7 @@
 
 
 def kernel(q_hbm, k_hbm, v_hbm, ob, qt, kv2, bias2, oacc, ml, raw, wide, kv1, vt, sref, bias0, bias1,
-           lsem, qsem, ssem, rsem):
+           lsem, qsem, ssem, rsem, lssem, lrsem):
     cx, cy, cz = lax.axis_index("cx"), lax.axis_index("cy"), lax.axis_index("cz")
     me = (cx * 2 + cy) * 2 + cz
     chip = cx * 2 + cy
@@ -156,17 +159,23 @@
     def out_v(h):
         return rdma(kv1.at[h, 1, 0], kv1.at[h, 1, 1 + cz], 2, cz, h, over(0))
 
-    def half_k(z):
-        return rdma(kv1.at[0, 0, 0, z], kv1.at[0, 0, 1 + cz, z], 1, cz, 0, over(1))
-
-    def half_v(z):
-        return rdma(kv1.at[0, 1, 0, z], kv1.at[0, 1, 1 + cz, z], 2, cz, 0, over(0))
+    def half(h, i, z):
+        return rdma(kv1.at[h, i, 0, z], kv1.at[h, i, 1 + cz, z], 1 + i, cz, h, over(1 - i))
 
     def relay(h):
         return rdma(kv1.at[h, mine, 1:3], kv1.at[h, mine, 1:3], 3, 2, h, sib)
 
     def forward(h):
         return rdma(kv1.at[h, mine, 2 - cz], kv2.at[h, mine], 4, 3, h, over(cz))
+
+    def last(part):
+        z = 0 if part == 0 else 1
+        return pltpu.make_async_remote_copy(kv1.at[HKV - 1, mine, 2 - cz, z], kv2.at[HKV - 1, mine, z],
+                                            lssem.at[part], lrsem.at[part], over(1 - cz if part == 2 else cz),
+                                            pl.DeviceIdType.MESH)
+
+    def last_relay():
+        return rdma(kv2.at[HKV - 1, mine, 0], kv2.at[HKV - 1, mine, 0], 5, 4, HKV - 1, sib)
 
     def relay2(h):
         return rdma(kv2.at[h, mine], kv2.at[h, mine], 5, 4, h, sib)
@@ -182,28 +191,36 @@
         qpos = (c // G) * 8 + me
         ref[...] = jnp.where(kpos <= qpos, 0.0, -1e30)
 
+    def relaid(h, i):
+        kv1[h, i, 0, cz] = wide[i, pl.ds(h, T, stride=HKV), :].astype(BF)
+
     for i in range(2):
         loads[i].wait()
         wide[i] = raw[i].astype(F32).reshape(T * HKV, D)
-
-    for h in range(HKV):
+        relaid(0, i)
+        relaid(1, i)
+        if i == 0:
+            pl.semaphore_wait(barrier, 3)
+        half(0, i, cz).start()
+    swap(0).start()
+
+    for h in range(2, HKV):
         for i in range(2):
-            kv1[h, i, 0, cz] = wide[i, pl.ds(h, T, stride=HKV), :].astype(BF)
-        if h == 1:
-            pl.semaphore_wait(barrier, 3)
-            half_k(cz).start()
-            half_v(cz).start()
-        if h:
-            swap(h - 1).start()
+            relaid(h, i)
+        if h == 2:
+            for i in range(2):
+                half(1, i, cz).start()
+        swap(h - 1).start()
 
     mask(2, 0, bias0)
     swap(HKV - 1).start()
 
-    arrived(kv1.at[0, :, 0, cz], 5, 0)
-    half_k(1 - cz).start()
-    half_v(1 - cz).start()
-
-    @pl.loop(1, HKV)
+    for h in range(2):
+        arrived(kv1.at[h, :, 0, cz], 5, h)
+        for i in range(2):
+            half(h, i, 1 - cz).start()
+
+    @pl.loop(2, HKV)
     def _(h):
         arrived(kv1.at[h, :, 0, cz], 5, h)
         out_k(h).start()
@@ -220,11 +237,26 @@
         arrived(kv1.at[h, mine, 1], 0, h)
         arrived(kv1.at[h, mine, 2], 1, h)
         relay(h).start()
-        forward(h).start()
+
+        @pl.when(h < HKV - 1)
+        def _():
+            forward(h).start()
+
+        @pl.when(h == HKV - 1)
+        def _():
+            for part in range(3):
+                last(part).start()
 
     def pass_on2(h):
-        arrived(kv2.at[h, mine], 3, h)
-        relay2(h).start()
+        @pl.when(h < HKV - 1)
+        def _():
+            arrived(kv2.at[h, mine], 3, h)
+            relay2(h).start()
+
+        @pl.when(h == HKV - 1)
+        def _():
+            last(0).wait_recv()
+            last_relay().start()
 
     @pl.loop(0, HKV // U0)
     def _(g):
@@ -236,26 +268,16 @@
 
         attend(heads, near(kv1, 0), 2, bias0, qt, oacc, ml, vt, sref, arrive, first=True)
 
-    pass_on(0)
-
-    @pl.loop(0, HKV // U1)
-    def _(g):
-        heads = [g * U1 + u for u in range(U1)]
-
-        def arrive(u):
-            h = heads[u]
-            if u < U1 - 1:
-                pass_on(h + 1)
-            else:
-                @pl.when(h < HKV - 1)
-                def _():
-                    pass_on(h + 1)
-
-            arrived(kv1.at[h, cz, 1:3], 2, h)
-
-        attend(heads, near(kv1, 1), 4, bias1, qt, oacc, ml, vt, sref, arrive)
-
-    pass_on2(0)
+    pass_on(jnp.int32(0))
+
+    @pl.loop(0, HKV - 1)
+    def _(h):
+        pass_on(h + 1)
+        arrived(kv1.at[h, cz, 1:3], 2, h)
+        attend([h], near(kv1, 1), 4, bias1, qt, oacc, ml, vt, sref)
+
+    arrived(kv1.at[HKV - 1, cz, 1:3], 2, HKV - 1)
+    attend([HKV - 1], near(kv1, 1), 4, bias1, qt, oacc, ml, vt, sref, hook=lambda: pass_on2(jnp.int32(0)))
 
     @pl.loop(0, (HKV - 1) // U2)
     def _(g):
@@ -267,12 +289,23 @@
 
         attend(heads, far(kv2), 2, bias2, qt, oacc, ml, vt, sref, arrive, out=lambda u: ob.at[heads[u]])
 
-    arrived(kv2.at[HKV - 1, cz], 4, HKV - 1)
+    for part in (1, 2):
+        last(part).wait_recv()
+    last_relay().wait_recv()
 
     @pl.loop(0, HKV)
     def _(h):
-        for sent in (swap, out_k, out_v, relay, forward, relay2):
+        for sent in (swap, out_k, out_v, relay):
             sent(h).wait_send()
+
+    @pl.loop(0, HKV - 1)
+    def _(h):
+        forward(h).wait_send()
+        relay2(h).wait_send()
+
+    for part in range(3):
+        last(part).wait_send()
+    last_relay().wait_send()
 
 
 def spread(ob, qt, kv2, bias2, oacc, ml, o_hbm, last, vt, sref, sem):
@@ -323,6 +356,8 @@
                 pltpu.SemaphoreType.DMA((HKV,)),
                 pltpu.SemaphoreType.DMA((6, HKV)),
                 pltpu.SemaphoreType.DMA((6, HKV)),
+                pltpu.SemaphoreType.DMA((3,)),
+                pltpu.SemaphoreType.DMA((3,)),
             ],
             compiler_params=pltpu.CompilerParams(
                 vmem_limit_bytes=36 << 20, collective_id=0, has_side_effects=True),

time: 44.2 us -> 43.7 us (0.989)
  Pallas kernels: 44.1 us -> 43.6 us
    pallas_call x1, Pallas kernels: 42 us -> 41.5 us  [local(): pl.pallas_call(kernel, out_shape=[pltpu.VMEM((HKV - 1, T, G, D), BF), plt...]
where the time goes in v13:
time: 43.7 us; the launch traced here: 43.6 us
  Pallas kernels  43.6 us (100%)
    pallas_call x1, Pallas kernels, local(): pl.pallas_call(kernel, out_shape=[pltpu.VMEM((HKV - 1, T, G, D), BF), plt...  41.5 us
    pallas_call x1, Pallas kernels, local(): pl.pallas_call(spread, out_shape=jax.ShapeDtypeStruct(q.shape, q.dtype),...  2.07 us

profile of v13, /device:TPU:0, one launch (start us, length us, event | category | flops | bytes accessed | tf_op | source)
XLA Modules:
  0.0 43.6 jit_solution(289121296516188823)
XLA Ops:
  0.0 41.5 %shard_map.37 = (bf16[7,256,8,128]{3,2,1,0:T(8,128)(2,1)S(1)}, bf16[8,256,8,128]{3,2,1,0:T(8,128)(2,1)S(1)}, bf16[8,2,2,256,128]{4,3,2,1,0:T(8,128)(2,1)S(1)}, f...) custom-call(bf16[256,64,128]{2,1,0:T(8,128)(2,1)} %q_hbm.1, ...), custom_call_target="tpu_custom_call" | custom-call | tf_op jit(solution)/shard_map/pallas_call | solution.py:335
  41.5 2.1 %shard_map.38 = bf16[256,64,128]{2,1,0:T(8,128)(2,1)} custom-call(bf16[7,256,8,128]{3,2,1,0:T(8,128)(2,1)S(1)} %get-tuple-element.11.ob, bf16[8,256,8,128]{3,2,1,0:T(8,128)(2,1)S(1)} %get-tuple-element.12.qt, bf16[8,2,2,256,128]{4,3,2,1,0:T(8,128)(2,1)S(1)} %get-tuple-element.13.kv2, f32[64,256]{1,0:T(8,128)S(1)} %get-tuple-element.14.bias2, ...), custom_call_target="tpu_custom_call" | custom-call | tf_op jit(solution)/shard_map/pallas_call | solution.py:365

commit v14 on v13

--- a/solution.py
+++ b/solution.py
@@ -128,15 +128,18 @@
     cx, cy, cz = lax.axis_index("cx"), lax.axis_index("cy"), lax.axis_index("cz")
     me = (cx * 2 + cy) * 2 + cz
     chip = cx * 2 + cy
-    mine = 1 - cz
-
-    def over(core):
-        return {"cx": cx + cz - 2 * cx * cz, "cy": cy + mine - 2 * cy * mine, "cz": core}
+    link = 1 - (cx + cz - 2 * cx * cz)
+    mine = 1 - link
+
+    def over(role):
+        x = cx + link - 2 * cx * link
+        y = cy + mine - 2 * cy * mine
+        return {"cx": x, "cy": y, "cz": x + (1 - role) - 2 * x * (1 - role)}
 
     sib = {"cz": 1 - cz}
 
     barrier = pltpu.get_barrier_semaphore()
-    for dev in ({"cx": cx, "cy": 1 - cy, "cz": 0}, {"cx": 1 - cx, "cy": cy, "cz": 1}, sib):
+    for dev in ({"cy": 1 - cy, "cz": 1 - cx}, {"cx": 1 - cx, "cz": 1 - cx}, sib):
         pl.semaphore_signal(barrier, inc=1, device_id=dev, device_id_type=pl.DeviceIdType.MESH)
 
     loads = [pltpu.make_async_copy(x, raw.at[i], lsem.at[i]) for i, x in enumerate((k_hbm, v_hbm))]
@@ -154,24 +157,24 @@
         return rdma(kv1.at[h, :, 0, cz], kv1.at[h, :, 0, cz], 0, 5, h, sib)
 
     def out_k(h):
-        return rdma(kv1.at[h, 0, 0], kv1.at[h, 0, 1 + cz], 1, cz, h, over(1))
+        return rdma(kv1.at[h, 0, 0], kv1.at[h, 0, 1 + link], 1, link, h, over(1))
 
     def out_v(h):
-        return rdma(kv1.at[h, 1, 0], kv1.at[h, 1, 1 + cz], 2, cz, h, over(0))
+        return rdma(kv1.at[h, 1, 0], kv1.at[h, 1, 1 + link], 2, link, h, over(0))
 
     def half(h, i, z):
-        return rdma(kv1.at[h, i, 0, z], kv1.at[h, i, 1 + cz, z], 1 + i, cz, h, over(1 - i))
+        return rdma(kv1.at[h, i, 0, z], kv1.at[h, i, 1 + link, z], 1 + i, link, h, over(1 - i))
 
     def relay(h):
         return rdma(kv1.at[h, mine, 1:3], kv1.at[h, mine, 1:3], 3, 2, h, sib)
 
     def forward(h):
-        return rdma(kv1.at[h, mine, 2 - cz], kv2.at[h, mine], 4, 3, h, over(cz))
+        return rdma(kv1.at[h, mine, 2 - link], kv2.at[h, mine], 4, 3, h, over(link))
 
     def last(part):
         z = 0 if part == 0 else 1
-        return pltpu.make_async_remote_copy(kv1.at[HKV - 1, mine, 2 - cz, z], kv2.at[HKV - 1, mine, z],
-                                            lssem.at[part], lrsem.at[part], over(1 - cz if part == 2 else cz),
+        return pltpu.make_async_remote_copy(kv1.at[HKV - 1, mine, 2 - link, z], kv2.at[HKV - 1, mine, z],
+                                            lssem.at[part], lrsem.at[part], over(mine if part == 2 else link),
                                             pl.DeviceIdType.MESH)
 
     def last_relay():
@@ -273,10 +276,10 @@
     @pl.loop(0, HKV - 1)
     def _(h):
         pass_on(h + 1)
-        arrived(kv1.at[h, cz, 1:3], 2, h)
+        arrived(kv1.at[h, link, 1:3], 2, h)
         attend([h], near(kv1, 1), 4, bias1, qt, oacc, ml, vt, sref)
 
-    arrived(kv1.at[HKV - 1, cz, 1:3], 2, HKV - 1)
+    arrived(kv1.at[HKV - 1, link, 1:3], 2, HKV - 1)
     attend([HKV - 1], near(kv1, 1), 4, bias1, qt, oacc, ml, vt, sref, hook=lambda: pass_on2(jnp.int32(0)))
 
     @pl.loop(0, (HKV - 1) // U2)
@@ -285,7 +288,7 @@
 
         def arrive(u):
             pass_on2(heads[u] + 1)
-            arrived(kv2.at[heads[u], cz], 4, heads[u])
+            arrived(kv2.at[heads[u], link], 4, heads[u])
 
         attend(heads, far(kv2), 2, bias2, qt, oacc, ml, vt, sref, arrive, out=lambda u: ob.at[heads[u]])
 

time: 43.7 us -> 42.9 us (0.982)
  Pallas kernels: 43.6 us -> 42.8 us
    pallas_call x1, Pallas kernels: 41.5 us -> 40.7 us  [local(): pl.pallas_call(kernel, out_shape=[pltpu.VMEM((HKV - 1, T, G, D), BF), plt...]
where the time goes in v14:
time: 42.9 us; the launch traced here: 42.8 us
  Pallas kernels  42.8 us (100%)
    pallas_call x1, Pallas kernels, local(): pl.pallas_call(kernel, out_shape=[pltpu.VMEM((HKV - 1, T, G, D), BF), plt...  40.7 us
    pallas_call x1, Pallas kernels, local(): pl.pallas_call(spread, out_shape=jax.ShapeDtypeStruct(q.shape, q.dtype),...  2.07 us

profile of v14, /device:TPU:0, one launch (start us, length us, event | category | flops | bytes accessed | tf_op | source)
XLA Modules:
  0.0 42.8 jit_solution(15567318160827307137)
XLA Ops:
  0.0 40.7 %shard_map.37 = (bf16[7,256,8,128]{3,2,1,0:T(8,128)(2,1)S(1)}, bf16[8,256,8,128]{3,2,1,0:T(8,128)(2,1)S(1)}, bf16[8,2,2,256,128]{4,3,2,1,0:T(8,128)(2,1)S(1)}, f...) custom-call(bf16[256,64,128]{2,1,0:T(8,128)(2,1)} %q_hbm.1, ...), custom_call_target="tpu_custom_call" | custom-call | tf_op jit(solution)/shard_map/pallas_call | solution.py:338
  40.7 2.1 %shard_map.38 = bf16[256,64,128]{2,1,0:T(8,128)(2,1)} custom-call(bf16[7,256,8,128]{3,2,1,0:T(8,128)(2,1)S(1)} %get-tuple-element.11.ob, bf16[8,256,8,128]{3,2,1,0:T(8,128)(2,1)S(1)} %get-tuple-element.12.qt, bf16[8,2,2,256,128]{4,3,2,1,0:T(8,128)(2,1)S(1)} %get-tuple-element.13.kv2, f32[64,256]{1,0:T(8,128)S(1)} %get-tuple-element.14.bias2, ...), custom_call_target="tpu_custom_call" | custom-call | tf_op jit(solution)/shard_map/pallas_call | solution.py:368

commit v15 on v14

--- a/solution.py
+++ b/solution.py
@@ -290,7 +290,7 @@
             pass_on2(heads[u] + 1)
             arrived(kv2.at[heads[u], link], 4, heads[u])
 
-        attend(heads, far(kv2), 2, bias2, qt, oacc, ml, vt, sref, arrive, out=lambda u: ob.at[heads[u]])
+        attend(heads, far(kv2), 2, bias2, qt, oacc, ml, vt, sref, arrive, out=lambda u: ob.at[:, pl.ds(pl.multiple_of(heads[u] * G, G), G), :])
 
     for part in (1, 2):
         last(part).wait_recv()
@@ -312,21 +312,25 @@
 
 
 def spread(ob, qt, kv2, bias2, oacc, ml, o_hbm, last, vt, sref, sem):
-    def put(src, h):
-        return pltpu.make_async_copy(src, o_hbm.at[:, pl.ds(pl.multiple_of(h * G, G), G), :], sem.at[h])
-
-    @pl.loop(0, HKV - 1)
-    def _(h):
-        put(ob.at[h], h).start()
+    done = (HKV - 1) * G
+
+    def put(b):
+        rows = pl.ds(pl.multiple_of(b * SUB, SUB), SUB)
+        return pltpu.make_async_copy(ob.at[rows], o_hbm.at[rows, :done, :], sem.at[b])
+
+    @pl.loop(0, NB)
+    def _(b):
+        put(b).start()
 
     attend([HKV - 1], far(kv2), 2, bias2, qt, oacc, ml, vt, sref, out=lambda u: last)
-    put(last, HKV - 1).start()
-
-    @pl.loop(0, HKV - 1)
-    def _(h):
-        put(ob.at[h], h).wait()
-
-    put(last, HKV - 1).wait()
+    tail = pltpu.make_async_copy(last, o_hbm.at[:, done:, :], sem.at[NB])
+    tail.start()
+
+    @pl.loop(0, NB)
+    def _(b):
+        put(b).wait()
+
+    tail.wait()
 
 
 def solution(mesh):
@@ -338,7 +342,7 @@
         parts = pl.pallas_call(
             kernel,
             out_shape=[
-                pltpu.VMEM((HKV - 1, T, G, D), BF),
+                pltpu.VMEM((T, (HKV - 1) * G, D), BF),
                 pltpu.VMEM((HKV, T, G, D), BF),
                 pltpu.VMEM((HKV, 2, 2, T, D), BF),
                 pltpu.VMEM((S2 * SUB, QB), F32),
@@ -374,7 +378,7 @@
                 pltpu.VMEM((T, G, D), BF),
                 pltpu.VMEM((1, D, S2 * T), BF),
                 pltpu.VMEM((AHEAD + 1, S2 * T, QB), F32),
-                pltpu.SemaphoreType.DMA((HKV,)),
+                pltpu.SemaphoreType.DMA((NB + 1,)),
             ],
             compiler_params=pltpu.CompilerParams(vmem_limit_bytes=8 << 20),
         )(*parts)

time: 42.9 us -> 42.9 us (level)
  no operation moved by 1% of the time
where the time goes in v15:
time: 42.9 us; the launch traced here: 42.8 us
  Pallas kernels  42.8 us (100%)
    pallas_call x1, Pallas kernels, local(): pl.pallas_call(kernel, out_shape=[pltpu.VMEM((T, (HKV - 1) * G, D), BF),...  40.7 us
    pallas_call x1, Pallas kernels, local(): pl.pallas_call(spread, out_shape=jax.ShapeDtypeStruct(q.shape, q.dtype),...  2.08 us

profile of v15, /device:TPU:0, one launch (start us, length us, event | category | flops | bytes accessed | tf_op | source)
XLA Modules:
  0.0 42.8 jit_solution(6013864272328252488)
XLA Ops:
  0.0 40.7 %shard_map.37 = (bf16[256,56,128]{2,1,0:T(8,128)(2,1)S(1)}, bf16[8,256,8,128]{3,2,1,0:T(8,128)(2,1)S(1)}, bf16[8,2,2,256,128]{4,3,2,1,0:T(8,128)(2,1)S(1)}, f32[...) custom-call(bf16[256,64,128]{2,1,0:T(8,128)(2,1)} %q_hbm.1, ...), custom_call_target="tpu_custom_call" | custom-call | tf_op jit(solution)/shard_map/pallas_call | solution.py:342
  40.7 2.1 %shard_map.38 = bf16[256,64,128]{2,1,0:T(8,128)(2,1)} custom-call(bf16[256,56,128]{2,1,0:T(8,128)(2,1)S(1)} %get-tuple-element.11.ob, bf16[8,256,8,128]{3,2,1,0:T(8,128)(2,1)S(1)} %get-tuple-element.12.qt, bf16[8,2,2,256,128]{4,3,2,1,0:T(8,128)(2,1)S(1)} %get-tuple-element.13.kv2, f32[64,256]{1,0:T(8,128)S(1)} %get-tuple-element.14.bias2, ...), custom_call_target="tpu_custom_call" | custom-call | tf_op jit(solution)/shard_map/pallas_call | solution.py:372

commit v16 on v14

--- a/solution.py
+++ b/solution.py
@@ -6,6 +6,7 @@
 from jax.sharding import PartitionSpec as P
 
 T = 256
+CUT = 128
 HKV = 8
 G = 8
 D = 128
@@ -172,13 +173,15 @@
         return rdma(kv1.at[h, mine, 2 - link], kv2.at[h, mine], 4, 3, h, over(link))
 
     def last(part):
-        z = 0 if part == 0 else 1
-        return pltpu.make_async_remote_copy(kv1.at[HKV - 1, mine, 2 - link, z], kv2.at[HKV - 1, mine, z],
-                                            lssem.at[part], lrsem.at[part], over(mine if part == 2 else link),
+        z, rows = ((0, pl.ds(0, T)), (1, pl.ds(0, CUT)), (1, pl.ds(CUT, T - CUT)), (1, pl.ds(CUT, T - CUT)))[part]
+        return pltpu.make_async_remote_copy(kv1.at[HKV - 1, mine, 2 - link, z, rows], kv2.at[HKV - 1, mine, z, rows],
+                                            lssem.at[part], lrsem.at[part], over(mine if part == 3 else link),
                                             pl.DeviceIdType.MESH)
 
-    def last_relay():
-        return rdma(kv2.at[HKV - 1, mine, 0], kv2.at[HKV - 1, mine, 0], 5, 4, HKV - 1, sib)
+    def last_relay(z):
+        rows = pl.ds(0, CUT if z else T)
+        return pltpu.make_async_remote_copy(kv2.at[HKV - 1, mine, z, rows], kv2.at[HKV - 1, mine, z, rows],
+                                            lssem.at[4 + z], lrsem.at[4 + z], sib, pl.DeviceIdType.MESH)
 
     def relay2(h):
         return rdma(kv2.at[h, mine], kv2.at[h, mine], 5, 4, h, sib)
@@ -247,7 +250,7 @@
 
         @pl.when(h == HKV - 1)
         def _():
-            for part in range(3):
+            for part in range(4):
                 last(part).start()
 
     def pass_on2(h):
@@ -258,8 +261,9 @@
 
         @pl.when(h == HKV - 1)
         def _():
-            last(0).wait_recv()
-            last_relay().start()
+            for z in range(2):
+                last(z).wait_recv()
+                last_relay(z).start()
 
     @pl.loop(0, HKV // U0)
     def _(g):
@@ -282,6 +286,11 @@
     arrived(kv1.at[HKV - 1, link, 1:3], 2, HKV - 1)
     attend([HKV - 1], near(kv1, 1), 4, bias1, qt, oacc, ml, vt, sref, hook=lambda: pass_on2(jnp.int32(0)))
 
+    @pl.loop(0, HKV)
+    def _(h):
+        for sent in (swap, out_k, out_v, relay):
+            sent(h).wait_send()
+
     @pl.loop(0, (HKV - 1) // U2)
     def _(g):
         heads = [g * U2 + u for u in range(U2)]
@@ -292,23 +301,20 @@
 
         attend(heads, far(kv2), 2, bias2, qt, oacc, ml, vt, sref, arrive, out=lambda u: ob.at[heads[u]])
 
-    for part in (1, 2):
-        last(part).wait_recv()
-    last_relay().wait_recv()
-
-    @pl.loop(0, HKV)
-    def _(h):
-        for sent in (swap, out_k, out_v, relay):
-            sent(h).wait_send()
-
     @pl.loop(0, HKV - 1)
     def _(h):
         forward(h).wait_send()
         relay2(h).wait_send()
 
-    for part in range(3):
+    for z in range(2):
+        last_relay(z).wait_recv()
+    for part in (2, 3):
+        last(part).wait_recv()
+
+    for part in range(4):
         last(part).wait_send()
-    last_relay().wait_send()
+    for z in range(2):
+        last_relay(z).wait_send()
 
 
 def spread(ob, qt, kv2, bias2, oacc, ml, o_hbm, last, vt, sref, sem):
@@ -359,8 +365,8 @@
                 pltpu.SemaphoreType.DMA((HKV,)),
                 pltpu.SemaphoreType.DMA((6, HKV)),
                 pltpu.SemaphoreType.DMA((6, HKV)),
-                pltpu.SemaphoreType.DMA((3,)),
-                pltpu.SemaphoreType.DMA((3,)),
+                pltpu.SemaphoreType.DMA((6,)),
+                pltpu.SemaphoreType.DMA((6,)),
             ],
             compiler_params=pltpu.CompilerParams(
                 vmem_limit_bytes=36 << 20, collective_id=0, has_side_effects=True),

time: 42.9 us -> 42.9 us (level)
  no operation moved by 1% of the time
where the time goes in v16:
time: 42.9 us; the launch traced here: 42.8 us
  Pallas kernels  42.8 us (100%)
    pallas_call x1, Pallas kernels, local(): pl.pallas_call(kernel, out_shape=[pltpu.VMEM((HKV - 1, T, G, D), BF), plt...  40.7 us
    pallas_call x1, Pallas kernels, local(): pl.pallas_call(spread, out_shape=jax.ShapeDtypeStruct(q.shape, q.dtype),...  2.07 us

profile of v16, /device:TPU:0, one launch (start us, length us, event | category | flops | bytes accessed | tf_op | source)
XLA Modules:
  0.0 42.8 jit_solution(11182130281707643016)
XLA Ops:
  0.0 40.7 %shard_map.37 = (bf16[7,256,8,128]{3,2,1,0:T(8,128)(2,1)S(1)}, bf16[8,256,8,128]{3,2,1,0:T(8,128)(2,1)S(1)}, bf16[8,2,2,256,128]{4,3,2,1,0:T(8,128)(2,1)S(1)}, f...) custom-call(bf16[256,64,128]{2,1,0:T(8,128)(2,1)} %q_hbm.1, ...), custom_call_target="tpu_custom_call" | custom-call | tf_op jit(solution)/shard_map/pallas_call | solution.py:344
  40.7 2.1 %shard_map.38 = bf16[256,64,128]{2,1,0:T(8,128)(2,1)} custom-call(bf16[7,256,8,128]{3,2,1,0:T(8,128)(2,1)S(1)} %get-tuple-element.11.ob, bf16[8,256,8,128]{3,2,1,0:T(8,128)(2,1)S(1)} %get-tuple-element.12.qt, bf16[8,2,2,256,128]{4,3,2,1,0:T(8,128)(2,1)S(1)} %get-tuple-element.13.kv2, f32[64,256]{1,0:T(8,128)S(1)} %get-tuple-element.14.bias2, ...), custom_call_target="tpu_custom_call" | custom-call | tf_op jit(solution)/shard_map/pallas_call | solution.py:374

commit v17 on v16

--- a/solution.py
+++ b/solution.py
@@ -7,6 +7,7 @@
 
 T = 256
 CUT = 128
+SENDS = ((2, 2), (4, 2), (6, 1), (7, 1))
 HKV = 8
 G = 8
 D = 128
@@ -157,11 +158,9 @@
     def swap(h):
         return rdma(kv1.at[h, :, 0, cz], kv1.at[h, :, 0, cz], 0, 5, h, sib)
 
-    def out_k(h):
-        return rdma(kv1.at[h, 0, 0], kv1.at[h, 0, 1 + link], 1, link, h, over(1))
-
-    def out_v(h):
-        return rdma(kv1.at[h, 1, 0], kv1.at[h, 1, 1 + link], 2, link, h, over(0))
+    def out(h, i, n):
+        heads = pl.ds(h, n)
+        return rdma(kv1.at[heads, i, 0], kv1.at[heads, i, 1 + link], 1 + i, link, h, over(1 - i))
 
     def half(h, i, z):
         return rdma(kv1.at[h, i, 0, z], kv1.at[h, i, 1 + link, z], 1 + i, link, h, over(1 - i))
@@ -200,15 +199,20 @@
     def relaid(h, i):
         kv1[h, i, 0, cz] = wide[i, pl.ds(h, T, stride=HKV), :].astype(BF)
 
+    def relaid(h, i):
+        kv1[h, i, 0, cz] = wide[i, pl.ds(h, T, stride=HKV), :].astype(BF)
+
     for i in range(2):
         loads[i].wait()
         wide[i] = raw[i].astype(F32).reshape(T * HKV, D)
         relaid(0, i)
-        relaid(1, i)
         if i == 0:
             pl.semaphore_wait(barrier, 3)
+        else:
+            relaid(1, 0)
         half(0, i, cz).start()
     swap(0).start()
+    relaid(1, 1)
 
     for h in range(2, HKV):
         for i in range(2):
@@ -226,11 +230,11 @@
         for i in range(2):
             half(h, i, 1 - cz).start()
 
-    @pl.loop(2, HKV)
-    def _(h):
-        arrived(kv1.at[h, :, 0, cz], 5, h)
-        out_k(h).start()
-        out_v(h).start()
+    for h, n in SENDS:
+        for x in range(h, h + n):
+            arrived(kv1.at[x, :, 0, cz], 5, x)
+        for i in range(2):
+            out(h, i, n).start()
 
     @pl.loop(0, HKV)
     def _(h):
@@ -240,8 +244,18 @@
     mask(2, 3, bias2)
 
     def pass_on(h):
-        arrived(kv1.at[h, mine, 1], 0, h)
-        arrived(kv1.at[h, mine, 2], 1, h)
+        middle = (h >= 2) & (h < 6)
+
+        @pl.when(jnp.logical_not(middle))
+        def _():
+            arrived(kv1.at[h, mine, 1], 0, h)
+            arrived(kv1.at[h, mine, 2], 1, h)
+
+        @pl.when(middle & (h % 2 == 0))
+        def _():
+            arrived(kv1.at[0:2, mine, 1], 0, h)
+            arrived(kv1.at[0:2, mine, 2], 1, h)
+
         relay(h).start()
 
         @pl.when(h < HKV - 1)
@@ -286,10 +300,14 @@
     arrived(kv1.at[HKV - 1, link, 1:3], 2, HKV - 1)
     attend([HKV - 1], near(kv1, 1), 4, bias1, qt, oacc, ml, vt, sref, hook=lambda: pass_on2(jnp.int32(0)))
 
+    for h, n in ((0, 1), (1, 1)) + SENDS:
+        for i in range(2):
+            out(h, i, n).wait_send()
+
     @pl.loop(0, HKV)
     def _(h):
-        for sent in (swap, out_k, out_v, relay):
-            sent(h).wait_send()
+        swap(h).wait_send()
+        relay(h).wait_send()
 
     @pl.loop(0, (HKV - 1) // U2)
     def _(g):

time: 42.9 us -> 42.9 us (level)
  no operation moved by 1% of the time
where the time goes in v17:
time: 42.9 us; the launch traced here: 42.8 us
  Pallas kernels  42.7 us (100%)
    pallas_call x1, Pallas kernels, local(): pl.pallas_call(kernel, out_shape=[pltpu.VMEM((HKV - 1, T, G, D), BF), plt...  40.7 us
    pallas_call x1, Pallas kernels, local(): pl.pallas_call(spread, out_shape=jax.ShapeDtypeStruct(q.shape, q.dtype),...  2.07 us

profile of v17, /device:TPU:0, one launch (start us, length us, event | category | flops | bytes accessed | tf_op | source)
XLA Modules:
  0.0 42.8 jit_solution(16496886291380772537)
XLA Ops:
  0.0 40.7 %shard_map.37 = (bf16[7,256,8,128]{3,2,1,0:T(8,128)(2,1)S(1)}, bf16[8,256,8,128]{3,2,1,0:T(8,128)(2,1)S(1)}, bf16[8,2,2,256,128]{4,3,2,1,0:T(8,128)(2,1)S(1)}, f...) custom-call(bf16[256,64,128]{2,1,0:T(8,128)(2,1)} %q_hbm.1, ...), custom_call_target="tpu_custom_call" | custom-call | tf_op jit(solution)/shard_map/pallas_call | solution.py:362
  40.7 2.1 %shard_map.38 = bf16[256,64,128]{2,1,0:T(8,128)(2,1)} custom-call(bf16[7,256,8,128]{3,2,1,0:T(8,128)(2,1)S(1)} %get-tuple-element.11.ob, bf16[8,256,8,128]{3,2,1,0:T(8,128)(2,1)S(1)} %get-tuple-element.12.qt, bf16[8,2,2,256,128]{4,3,2,1,0:T(8,128)(2,1)S(1)} %get-tuple-element.13.kv2, f32[64,256]{1,0:T(8,128)S(1)} %get-tuple-element.14.bias2, ...), custom_call_target="tpu_custom_call" | custom-call | tf_op jit(solution)/shard_map/pallas_call | solution.py:392

commit v18 on v17

--- a/solution.py
+++ b/solution.py
@@ -140,14 +140,14 @@
 
     sib = {"cz": 1 - cz}
 
+    loads = [pltpu.make_async_copy(x, raw.at[i], lsem.at[i]) for i, x in enumerate((k_hbm, v_hbm))]
+    for x in loads:
+        x.start()
+
     barrier = pltpu.get_barrier_semaphore()
     for dev in ({"cy": 1 - cy, "cz": 1 - cx}, {"cx": 1 - cx, "cz": 1 - cx}, sib):
         pl.semaphore_signal(barrier, inc=1, device_id=dev, device_id_type=pl.DeviceIdType.MESH)
 
-    loads = [pltpu.make_async_copy(x, raw.at[i], lsem.at[i]) for i, x in enumerate((k_hbm, v_hbm))]
-    for x in loads:
-        x.start()
-
     def qload(h):
         return pltpu.make_async_copy(q_hbm.at[:, pl.ds(pl.multiple_of(h * G, G), G), :], qt.at[h], qsem.at[h])
 
@@ -168,8 +168,12 @@
     def relay(h):
         return rdma(kv1.at[h, mine, 1:3], kv1.at[h, mine, 1:3], 3, 2, h, sib)
 
-    def forward(h):
-        return rdma(kv1.at[h, mine, 2 - link], kv2.at[h, mine], 4, 3, h, over(link))
+    def forward(h, z=None):
+        src, dst = kv1.at[h, mine, 2 - link], kv2.at[h, mine]
+        if z is None:
+            return rdma(src, dst, 4, 3, h, over(link))
+        return pltpu.make_async_remote_copy(src.at[z], dst.at[z], lssem.at[6 + z], lrsem.at[6 + z], over(link),
+                                            pl.DeviceIdType.MESH)
 
     def last(part):
         z, rows = ((0, pl.ds(0, T)), (1, pl.ds(0, CUT)), (1, pl.ds(CUT, T - CUT)), (1, pl.ds(CUT, T - CUT)))[part]
@@ -258,9 +262,14 @@
 
         relay(h).start()
 
-        @pl.when(h < HKV - 1)
+        @pl.when(h < HKV - 2)
         def _():
             forward(h).start()
+
+        @pl.when(h == HKV - 2)
+        def _():
+            for z in range(2):
+                forward(h, z).start()
 
         @pl.when(h == HKV - 1)
         def _():
@@ -268,10 +277,16 @@
                 last(part).start()
 
     def pass_on2(h):
-        @pl.when(h < HKV - 1)
+        @pl.when(h < HKV - 2)
         def _():
             arrived(kv2.at[h, mine], 3, h)
             relay2(h).start()
+
+        @pl.when(h == HKV - 2)
+        def _():
+            for z in range(2):
+                forward(h, z).wait_recv()
+                rdma(kv2.at[h, mine, z], kv2.at[h, mine, z], 5, 4, h, sib).start()
 
         @pl.when(h == HKV - 1)
         def _():
@@ -309,21 +324,27 @@
         swap(h).wait_send()
         relay(h).wait_send()
 
-    @pl.loop(0, (HKV - 1) // U2)
-    def _(g):
-        heads = [g * U2 + u for u in range(U2)]
-
-        def arrive(u):
-            pass_on2(heads[u] + 1)
-            arrived(kv2.at[heads[u], link], 4, heads[u])
-
-        attend(heads, far(kv2), 2, bias2, qt, oacc, ml, vt, sref, arrive, out=lambda u: ob.at[heads[u]])
-
-    @pl.loop(0, HKV - 1)
-    def _(h):
-        forward(h).wait_send()
-        relay2(h).wait_send()
-
+    def diagonal(h, before=None):
+        pass_on2(h + 1)
+        if before:
+            before()
+        arrived(kv2.at[h, link], 4, h)
+        attend([h], far(kv2), 2, bias2, qt, oacc, ml, vt, sref, out=lambda u: ob.at[h])
+
+    @pl.loop(0, HKV - 2)
+    def _(h):
+        diagonal(h)
+
+    def old_sends():
+        @pl.loop(0, HKV - 2)
+        def _(h):
+            forward(h).wait_send()
+            relay2(h).wait_send()
+
+    diagonal(jnp.int32(HKV - 2), old_sends)
+    for z in range(2):
+        forward(HKV - 2, z).wait_send()
+    relay2(HKV - 2).wait_send()
     for z in range(2):
         last_relay(z).wait_recv()
     for part in (2, 3):
@@ -383,8 +404,8 @@
                 pltpu.SemaphoreType.DMA((HKV,)),
                 pltpu.SemaphoreType.DMA((6, HKV)),
                 pltpu.SemaphoreType.DMA((6, HKV)),
-                pltpu.SemaphoreType.DMA((6,)),
-                pltpu.SemaphoreType.DMA((6,)),
+                pltpu.SemaphoreType.DMA((8,)),
+                pltpu.SemaphoreType.DMA((8,)),
             ],
             compiler_params=pltpu.CompilerParams(
                 vmem_limit_bytes=36 << 20, collective_id=0, has_side_effects=True),

time: 42.9 us -> 42.9 us (level)
  no operation moved by 1% of the time
where the time goes in v18:
time: 42.9 us; the launch traced here: 42.8 us
  Pallas kernels  42.8 us (100%)
    pallas_call x1, Pallas kernels, local(): pl.pallas_call(kernel, out_shape=[pltpu.VMEM((HKV - 1, T, G, D), BF), plt...  40.7 us
    pallas_call x1, Pallas kernels, local(): pl.pallas_call(spread, out_shape=jax.ShapeDtypeStruct(q.shape, q.dtype),...  2.07 us

profile of v18, /device:TPU:0, one launch (start us, length us, event | category | flops | bytes accessed | tf_op | source)
XLA Modules:
  0.0 42.8 jit_solution(16181848466577881195)
XLA Ops:
  0.0 40.7 %shard_map.37 = (bf16[7,256,8,128]{3,2,1,0:T(8,128)(2,1)S(1)}, bf16[8,256,8,128]{3,2,1,0:T(8,128)(2,1)S(1)}, bf16[8,2,2,256,128]{4,3,2,1,0:T(8,128)(2,1)S(1)}, f...) custom-call(bf16[256,64,128]{2,1,0:T(8,128)(2,1)} %q_hbm.1, ...), custom_call_target="tpu_custom_call" | custom-call | tf_op jit(solution)/shard_map/pallas_call | solution.py:383
  40.7 2.1 %shard_map.38 = bf16[256,64,128]{2,1,0:T(8,128)(2,1)} custom-call(bf16[7,256,8,128]{3,2,1,0:T(8,128)(2,1)S(1)} %get-tuple-element.11.ob, bf16[8,256,8,128]{3,2,1,0:T(8,128)(2,1)S(1)} %get-tuple-element.12.qt, bf16[8,2,2,256,128]{4,3,2,1,0:T(8,128)(2,1)S(1)} %get-tuple-element.13.kv2, f32[64,256]{1,0:T(8,128)S(1)} %get-tuple-element.14.bias2, ...), custom_call_target="tpu_custom_call" | custom-call | tf_op jit(solution)/shard_map/pallas_call | solution.py:413

commit v19 on v18

--- a/solution.py
+++ b/solution.py
@@ -19,7 +19,6 @@
 C = (D ** -0.5) * 1.4426950408889634
 ORDER = (0, 2, 4, 6, 7, 5, 3, 1)
 AHEAD = 4
-HOOK = 4
 U0, U1, U2 = 1, 1, 1
 BF = jnp.bfloat16
 F32 = jnp.float32
@@ -92,8 +91,8 @@
         scores(*todo[at])
         at += 1
     for i, (u, j) in enumerate(items):
-        if hook and i == HOOK:
-            hook()
+        if hook and i == hook[0]:
+            hook[1]()
         top = jnp.max(tops[i], axis=0, keepdims=True)
         m, a = top, None
         if not first:
@@ -290,9 +289,8 @@
 
         @pl.when(h == HKV - 1)
         def _():
-            for z in range(2):
-                last(z).wait_recv()
-                last_relay(z).start()
+            last(0).wait_recv()
+            last_relay(0).start()
 
     @pl.loop(0, HKV // U0)
     def _(g):
@@ -306,14 +304,17 @@
 
     pass_on(jnp.int32(0))
 
-    @pl.loop(0, HKV - 1)
+    def neighbours(h, hook=None):
+        arrived(kv1.at[h, link, 1:3], 2, h)
+        attend([h], near(kv1, 1), 4, bias1, qt, oacc, ml, vt, sref, hook=hook)
+
+    @pl.loop(0, HKV - 2)
     def _(h):
         pass_on(h + 1)
-        arrived(kv1.at[h, link, 1:3], 2, h)
-        attend([h], near(kv1, 1), 4, bias1, qt, oacc, ml, vt, sref)
-
-    arrived(kv1.at[HKV - 1, link, 1:3], 2, HKV - 1)
-    attend([HKV - 1], near(kv1, 1), 4, bias1, qt, oacc, ml, vt, sref, hook=lambda: pass_on2(jnp.int32(0)))
+        neighbours(h)
+
+    neighbours(HKV - 2, (6, lambda: pass_on(jnp.int32(HKV - 1))))
+    neighbours(HKV - 1, (4, lambda: pass_on2(jnp.int32(0))))
 
     for h, n in ((0, 1), (1, 1)) + SENDS:
         for i in range(2):
@@ -324,12 +325,12 @@
         swap(h).wait_send()
         relay(h).wait_send()
 
-    def diagonal(h, before=None):
+    def diagonal(h, before=None, hook=None):
         pass_on2(h + 1)
         if before:
             before()
         arrived(kv2.at[h, link], 4, h)
-        attend([h], far(kv2), 2, bias2, qt, oacc, ml, vt, sref, out=lambda u: ob.at[h])
+        attend([h], far(kv2), 2, bias2, qt, oacc, ml, vt, sref, out=lambda u: ob.at[h], hook=hook)
 
     @pl.loop(0, HKV - 2)
     def _(h):
@@ -341,7 +342,11 @@
             forward(h).wait_send()
             relay2(h).wait_send()
 
-    diagonal(jnp.int32(HKV - 2), old_sends)
+    def late():
+        last(1).wait_recv()
+        last_relay(1).start()
+
+    diagonal(jnp.int32(HKV - 2), old_sends, (3, late))
     for z in range(2):
         forward(HKV - 2, z).wait_send()
     relay2(HKV - 2).wait_send()

time: 42.9 us -> 43.4 us (1.012)
  Pallas kernels: 42.8 us -> 43.3 us
    pallas_call x1, Pallas kernels: 40.7 us -> 41.2 us  [local(): pl.pallas_call(kernel, out_shape=[pltpu.VMEM((HKV - 1, T, G, D), BF), plt...]
where the time goes in v19:
time: 43.4 us; the launch traced here: 43.3 us
  Pallas kernels  43.3 us (100%)
    pallas_call x1, Pallas kernels, local(): pl.pallas_call(kernel, out_shape=[pltpu.VMEM((HKV - 1, T, G, D), BF), plt...  41.2 us
    pallas_call x1, Pallas kernels, local(): pl.pallas_call(spread, out_shape=jax.ShapeDtypeStruct(q.shape, q.dtype),...  2.07 us

profile of v19, /device:TPU:0, one launch (start us, length us, event | category | flops | bytes accessed | tf_op | source)
XLA Modules:
  0.0 43.3 jit_solution(2448384607354644102)
XLA Ops:
  0.0 41.2 %shard_map.37 = (bf16[7,256,8,128]{3,2,1,0:T(8,128)(2,1)S(1)}, bf16[8,256,8,128]{3,2,1,0:T(8,128)(2,1)S(1)}, bf16[8,2,2,256,128]{4,3,2,1,0:T(8,128)(2,1)S(1)}, f...) custom-call(bf16[256,64,128]{2,1,0:T(8,128)(2,1)} %q_hbm.1, ...), custom_call_target="tpu_custom_call" | custom-call | tf_op jit(solution)/shard_map/pallas_call | solution.py:388
  41.2 2.1 %shard_map.38 = bf16[256,64,128]{2,1,0:T(8,128)(2,1)} custom-call(bf16[7,256,8,128]{3,2,1,0:T(8,128)(2,1)S(1)} %get-tuple-element.11.ob, bf16[8,256,8,128]{3,2,1,0:T(8,128)(2,1)S(1)} %get-tuple-element.12.qt, bf16[8,2,2,256,128]{4,3,2,1,0:T(8,128)(2,1)S(1)} %get-tuple-element.13.kv2, f32[64,256]{1,0:T(8,128)S(1)} %get-tuple-element.14.bias2, ...), custom_call_target="tpu_custom_call" | custom-call | tf_op jit(solution)/shard_map/pallas_call | solution.py:418

commit v20 on v17

--- a/solution.py
+++ b/solution.py
@@ -19,7 +19,6 @@
 C = (D ** -0.5) * 1.4426950408889634
 ORDER = (0, 2, 4, 6, 7, 5, 3, 1)
 AHEAD = 4
-HOOK = 4
 U0, U1, U2 = 1, 1, 1
 BF = jnp.bfloat16
 F32 = jnp.float32
@@ -92,8 +91,8 @@
         scores(*todo[at])
         at += 1
     for i, (u, j) in enumerate(items):
-        if hook and i == HOOK:
-            hook()
+        if hook and i == hook[0]:
+            hook[1]()
         top = jnp.max(tops[i], axis=0, keepdims=True)
         m, a = top, None
         if not first:
@@ -291,14 +290,17 @@
 
     pass_on(jnp.int32(0))
 
-    @pl.loop(0, HKV - 1)
+    def neighbours(h, hook=None):
+        arrived(kv1.at[h, link, 1:3], 2, h)
+        attend([h], near(kv1, 1), 4, bias1, qt, oacc, ml, vt, sref, hook=hook)
+
+    @pl.loop(0, HKV - 2)
     def _(h):
         pass_on(h + 1)
-        arrived(kv1.at[h, link, 1:3], 2, h)
-        attend([h], near(kv1, 1), 4, bias1, qt, oacc, ml, vt, sref)
-
-    arrived(kv1.at[HKV - 1, link, 1:3], 2, HKV - 1)
-    attend([HKV - 1], near(kv1, 1), 4, bias1, qt, oacc, ml, vt, sref, hook=lambda: pass_on2(jnp.int32(0)))
+        neighbours(h)
+
+    neighbours(HKV - 2, (4, lambda: pass_on(jnp.int32(HKV - 1))))
+    neighbours(HKV - 1, (4, lambda: pass_on2(jnp.int32(0))))
 
     for h, n in ((0, 1), (1, 1)) + SENDS:
         for i in range(2):

time: 42.9 us -> 42.9 us (level)
  no operation moved by 1% of the time
where the time goes in v20:
time: 42.9 us; the launch traced here: 42.8 us
  Pallas kernels  42.7 us (100%)
    pallas_call x1, Pallas kernels, local(): pl.pallas_call(kernel, out_shape=[pltpu.VMEM((HKV - 1, T, G, D), BF), plt...  40.7 us
    pallas_call x1, Pallas kernels, local(): pl.pallas_call(spread, out_shape=jax.ShapeDtypeStruct(q.shape, q.dtype),...  2.07 us

profile of v20, /device:TPU:0, one launch (start us, length us, event | category | flops | bytes accessed | tf_op | source)
XLA Modules:
  0.0 42.8 jit_solution(8478478618615774202)
XLA Ops:
  0.0 40.7 %shard_map.37 = (bf16[7,256,8,128]{3,2,1,0:T(8,128)(2,1)S(1)}, bf16[8,256,8,128]{3,2,1,0:T(8,128)(2,1)S(1)}, bf16[8,2,2,256,128]{4,3,2,1,0:T(8,128)(2,1)S(1)}, f...) custom-call(bf16[256,64,128]{2,1,0:T(8,128)(2,1)} %q_hbm.1, ...), custom_call_target="tpu_custom_call" | custom-call | tf_op jit(solution)/shard_map/pallas_call | solution.py:364
  40.7 2.1 %shard_map.38 = bf16[256,64,128]{2,1,0:T(8,128)(2,1)} custom-call(bf16[7,256,8,128]{3,2,1,0:T(8,128)(2,1)S(1)} %get-tuple-element.11.ob, bf16[8,256,8,128]{3,2,1,0:T(8,128)(2,1)S(1)} %get-tuple-element.12.qt, bf16[8,2,2,256,128]{4,3,2,1,0:T(8,128)(2,1)S(1)} %get-tuple-element.13.kv2, f32[64,256]{1,0:T(8,128)S(1)} %get-tuple-element.14.bias2, ...), custom_call_target="tpu_custom_call" | custom-call | tf_op jit(solution)/shard_map/pallas_call | solution.py:394

commit v21 on v17

--- a/solution.py
+++ b/solution.py
@@ -140,13 +140,15 @@
 
     sib = {"cz": 1 - cz}
 
+    half_t = T // 2
+    loads = [pltpu.make_async_copy(x.at[pl.ds(r, half_t)], raw.at[i, pl.ds(r, half_t)], lsem.at[2 * i + r // half_t])
+             for i, x in enumerate((k_hbm, v_hbm)) for r in (0, half_t)]
+    for x in loads:
+        x.start()
+
     barrier = pltpu.get_barrier_semaphore()
     for dev in ({"cy": 1 - cy, "cz": 1 - cx}, {"cx": 1 - cx, "cz": 1 - cx}, sib):
         pl.semaphore_signal(barrier, inc=1, device_id=dev, device_id_type=pl.DeviceIdType.MESH)
-
-    loads = [pltpu.make_async_copy(x, raw.at[i], lsem.at[i]) for i, x in enumerate((k_hbm, v_hbm))]
-    for x in loads:
-        x.start()
 
     def qload(h):
         return pltpu.make_async_copy(q_hbm.at[:, pl.ds(pl.multiple_of(h * G, G), G), :], qt.at[h], qsem.at[h])
@@ -203,8 +205,10 @@
         kv1[h, i, 0, cz] = wide[i, pl.ds(h, T, stride=HKV), :].astype(BF)
 
     for i in range(2):
-        loads[i].wait()
-        wide[i] = raw[i].astype(F32).reshape(T * HKV, D)
+        for r in range(2):
+            loads[2 * i + r].wait()
+            rows = raw[i, r * half_t:(r + 1) * half_t]
+            wide[i, r * half_t * HKV:(r + 1) * half_t * HKV] = rows.astype(F32).reshape(half_t * HKV, D)
         relaid(0, i)
         if i == 0:
             pl.semaphore_wait(barrier, 3)
@@ -379,7 +383,7 @@
                 pltpu.VMEM((AHEAD + 1, 4 * T, QB), F32),
                 pltpu.VMEM((2 * SUB, QB), F32),
                 pltpu.VMEM((4 * SUB, QB), F32),
-                pltpu.SemaphoreType.DMA((2,)),
+                pltpu.SemaphoreType.DMA((4,)),
                 pltpu.SemaphoreType.DMA((HKV,)),
                 pltpu.SemaphoreType.DMA((6, HKV)),
                 pltpu.SemaphoreType.DMA((6, HKV)),

time: 42.9 us -> 42.8 us (level)
  no operation moved by 1% of the time
where the time goes in v21:
time: 42.8 us; the launch traced here: 42.7 us
  Pallas kernels  42.7 us (100%)
    pallas_call x1, Pallas kernels, local(): pl.pallas_call(kernel, out_shape=[pltpu.VMEM((HKV - 1, T, G, D), BF), plt...  40.6 us
    pallas_call x1, Pallas kernels, local(): pl.pallas_call(spread, out_shape=jax.ShapeDtypeStruct(q.shape, q.dtype),...  2.07 us

profile of v21, /device:TPU:0, one launch (start us, length us, event | category | flops | bytes accessed | tf_op | source)
XLA Modules:
  0.0 42.7 jit_solution(8441451229492963276)
XLA Ops:
  0.0 40.6 %shard_map.37 = (bf16[7,256,8,128]{3,2,1,0:T(8,128)(2,1)S(1)}, bf16[8,256,8,128]{3,2,1,0:T(8,128)(2,1)S(1)}, bf16[8,2,2,256,128]{4,3,2,1,0:T(8,128)(2,1)S(1)}, f...) custom-call(bf16[256,64,128]{2,1,0:T(8,128)(2,1)} %q_hbm.1, ...), custom_call_target="tpu_custom_call" | custom-call | tf_op jit(solution)/shard_map/pallas_call | solution.py:366
  40.6 2.1 %shard_map.38 = bf16[256,64,128]{2,1,0:T(8,128)(2,1)} custom-call(bf16[7,256,8,128]{3,2,1,0:T(8,128)(2,1)S(1)} %get-tuple-element.11.ob, bf16[8,256,8,128]{3,2,1,0:T(8,128)(2,1)S(1)} %get-tuple-element.12.qt, bf16[8,2,2,256,128]{4,3,2,1,0:T(8,128)(2,1)S(1)} %get-tuple-element.13.kv2, f32[64,256]{1,0:T(8,128)S(1)} %get-tuple-element.14.bias2, ...), custom_call_target="tpu_custom_call" | custom-call | tf_op jit(solution)/shard_map/pallas_call | solution.py:396

commit v22 on v21

--- a/solution.py
+++ b/solution.py
@@ -6,7 +6,7 @@
 from jax.sharding import PartitionSpec as P
 
 T = 256
-CUT = 128
+CUT = 192
 SENDS = ((2, 2), (4, 2), (6, 1), (7, 1))
 HKV = 8
 G = 8

time: 42.8 us -> 43 us (level)
  no operation moved by 1% of the time
where the time goes in v22:
time: 43 us; the launch traced here: 42.9 us
  Pallas kernels  42.9 us (100%)
    pallas_call x1, Pallas kernels, local(): pl.pallas_call(kernel, out_shape=[pltpu.VMEM((HKV - 1, T, G, D), BF), plt...  40.8 us
    pallas_call x1, Pallas kernels, local(): pl.pallas_call(spread, out_shape=jax.ShapeDtypeStruct(q.shape, q.dtype),...  2.07 us

profile of v22, /device:TPU:0, one launch (start us, length us, event | category | flops | bytes accessed | tf_op | source)
XLA Modules:
  0.0 42.9 jit_solution(7403225045327798337)
XLA Ops:
  0.0 40.8 %shard_map.37 = (bf16[7,256,8,128]{3,2,1,0:T(8,128)(2,1)S(1)}, bf16[8,256,8,128]{3,2,1,0:T(8,128)(2,1)S(1)}, bf16[8,2,2,256,128]{4,3,2,1,0:T(8,128)(2,1)S(1)}, f...) custom-call(bf16[256,64,128]{2,1,0:T(8,128)(2,1)} %q_hbm.1, ...), custom_call_target="tpu_custom_call" | custom-call | tf_op jit(solution)/shard_map/pallas_call | solution.py:366
  40.8 2.1 %shard_map.38 = bf16[256,64,128]{2,1,0:T(8,128)(2,1)} custom-call(bf16[7,256,8,128]{3,2,1,0:T(8,128)(2,1)S(1)} %get-tuple-element.11.ob, bf16[8,256,8,128]{3,2,1,0:T(8,128)(2,1)S(1)} %get-tuple-element.12.qt, bf16[8,2,2,256,128]{4,3,2,1,0:T(8,128)(2,1)S(1)} %get-tuple-element.13.kv2, f32[64,256]{1,0:T(8,128)S(1)} %get-tuple-element.14.bias2, ...), custom_call_target="tpu_custom_call" | custom-call | tf_op jit(solution)/shard_map/pallas_call | solution.py:396

commit v23 on v22

--- a/solution.py
+++ b/solution.py
@@ -6,7 +6,7 @@
 from jax.sharding import PartitionSpec as P
 
 T = 256
-CUT = 192
+CUT = 64
 SENDS = ((2, 2), (4, 2), (6, 1), (7, 1))
 HKV = 8
 G = 8

time: 43 us -> 42.8 us (level)
  no operation moved by 1% of the time
where the time goes in v23:
time: 42.8 us; the launch traced here: 42.7 us
  Pallas kernels  42.7 us (100%)
    pallas_call x1, Pallas kernels, local(): pl.pallas_call(kernel, out_shape=[pltpu.VMEM((HKV - 1, T, G, D), BF), plt...  40.6 us
    pallas_call x1, Pallas kernels, local(): pl.pallas_call(spread, out_shape=jax.ShapeDtypeStruct(q.shape, q.dtype),...  2.07 us

profile of v23, /device:TPU:0, one launch (start us, length us, event | category | flops | bytes accessed | tf_op | source)
XLA Modules:
  0.0 42.7 jit_solution(12609155918898278104)
XLA Ops:
  0.0 40.6 %shard_map.37 = (bf16[7,256,8,128]{3,2,1,0:T(8,128)(2,1)S(1)}, bf16[8,256,8,128]{3,2,1,0:T(8,128)(2,1)S(1)}, bf16[8,2,2,256,128]{4,3,2,1,0:T(8,128)(2,1)S(1)}, f...) custom-call(bf16[256,64,128]{2,1,0:T(8,128)(2,1)} %q_hbm.1, ...), custom_call_target="tpu_custom_call" | custom-call | tf_op jit(solution)/shard_map/pallas_call | solution.py:366
  40.6 2.1 %shard_map.38 = bf16[256,64,128]{2,1,0:T(8,128)(2,1)} custom-call(bf16[7,256,8,128]{3,2,1,0:T(8,128)(2,1)S(1)} %get-tuple-element.11.ob, bf16[8,256,8,128]{3,2,1,0:T(8,128)(2,1)S(1)} %get-tuple-element.12.qt, bf16[8,2,2,256,128]{4,3,2,1,0:T(8,128)(2,1)S(1)} %get-tuple-element.13.kv2, f32[64,256]{1,0:T(8,128)S(1)} %get-tuple-element.14.bias2, ...), custom_call_target="tpu_custom_call" | custom-call | tf_op jit(solution)/shard_map/pallas_call | solution.py:396

commit v24 on v23

--- a/solution.py
+++ b/solution.py
@@ -6,7 +6,7 @@
 from jax.sharding import PartitionSpec as P
 
 T = 256
-CUT = 64
+CUT = 96
 SENDS = ((2, 2), (4, 2), (6, 1), (7, 1))
 HKV = 8
 G = 8

time: 42.8 us -> 42.8 us (level)
  no operation moved by 1% of the time
where the time goes in v24:
time: 42.8 us; the launch traced here: 42.7 us
  Pallas kernels  42.7 us (100%)
    pallas_call x1, Pallas kernels, local(): pl.pallas_call(kernel, out_shape=[pltpu.VMEM((HKV - 1, T, G, D), BF), plt...  40.6 us
    pallas_call x1, Pallas kernels, local(): pl.pallas_call(spread, out_shape=jax.ShapeDtypeStruct(q.shape, q.dtype),...  2.07 us

profile of v24, /device:TPU:0, one launch (start us, length us, event | category | flops | bytes accessed | tf_op | source)
XLA Modules:
  0.0 42.7 jit_solution(124816725113312421)
XLA Ops:
  0.0 40.6 %shard_map.37 = (bf16[7,256,8,128]{3,2,1,0:T(8,128)(2,1)S(1)}, bf16[8,256,8,128]{3,2,1,0:T(8,128)(2,1)S(1)}, bf16[8,2,2,256,128]{4,3,2,1,0:T(8,128)(2,1)S(1)}, f...) custom-call(bf16[256,64,128]{2,1,0:T(8,128)(2,1)} %q_hbm.1, ...), custom_call_target="tpu_custom_call" | custom-call | tf_op jit(solution)/shard_map/pallas_call | solution.py:366
  40.6 2.1 %shard_map.38 = bf16[256,64,128]{2,1,0:T(8,128)(2,1)} custom-call(bf16[7,256,8,128]{3,2,1,0:T(8,128)(2,1)S(1)} %get-tuple-element.11.ob, bf16[8,256,8,128]{3,2,1,0:T(8,128)(2,1)S(1)} %get-tuple-element.12.qt, bf16[8,2,2,256,128]{4,3,2,1,0:T(8,128)(2,1)S(1)} %get-tuple-element.13.kv2, f32[64,256]{1,0:T(8,128)S(1)} %get-tuple-element.14.bias2, ...), custom_call_target="tpu_custom_call" | custom-call | tf_op jit(solution)/shard_map/pallas_call | solution.py:396
